TPU v7x, 256 devices: a whole 4x4x8 slice. The times are simulated.
256 devices in a mesh: owner: 16 (over y, x), rows: 16 (over z, core).
Axes of the slice: x: 4, y: 4, z: 8, core: 2. Of those that a mesh axis runs over, the one named last changes fastest.
Arguments:
- train_gate: float32 [64, 2048, 1024], P('owner', 'rows'), may hold values from -0.1875 to 0.1875
- train_up: float32 [64, 2048, 1024], P('owner', 'rows'), may hold values from -0.1875 to 0.1875
- train_down: float32 [64, 1024, 2048], P('owner', None, 'rows'), may hold values from -0.25 to 0.25
- router_weight: float32 [2048, 64], P('rows', 'owner'), may hold values from -0.125 to 0.125
- router_gain: float32 [2048], P('rows'), may hold values from 0.25 to 1.75
Outputs:
- ready_gate: bfloat16 [64, 2048, 1024], P('owner', None, 'rows')
- ready_up: bfloat16 [64, 2048, 1024], P('owner', None, 'rows')
- ready_down: bfloat16 [64, 1024, 2048], P('owner', 'rows')
- scale_gate: float32 [64, 1024], P('owner', 'rows')
- scale_up: float32 [64, 1024], P('owner', 'rows')
- scale_down: float32 [64, 1024], P('owner', 'rows')
- serve_router: bfloat16 [2048, 64], replicated
All inputs are finite; a program needn't handle non-finite values. Where the computation divides by a largest or mean magnitude, that divisor is 1e-20 or more.
Results may differ from a plain program's by a relative error of at most 0.0013.
Values may be sent and summed in bfloat16 or wider, within the bound.
No kernel may reach another device: no remote copies, remote signals or barrier semaphores. Data moves between devices by JAX's collectives and lax.ppermute only.
A program may use at most 64 MiB of HBM per device.

v0:
```python
import jax
import jax.numpy as jnp
from jax import lax
from jax.sharding import PartitionSpec as P

D_MODEL = 2048


def copy_for_each(shard, axis):
    size = lax.axis_size(axis)
    return lax.all_to_all(
        jnp.broadcast_to(shard[None], (size, *shard.shape)), axis, 0, 0, tiled=True
    )


def over_copies(shard, axis):
    everything = copy_for_each(shard, axis)
    return jnp.sum(everything, axis=0)


def together(arrays, axis):
    ends = [0]
    for a in arrays:
        ends.append(ends[-1] + a.size)
    total = over_copies(jnp.concatenate([a.ravel() for a in arrays]), axis)
    return tuple((total[b:e].reshape(a.shape) for a, b, e in zip(arrays, ends, ends[1:])))


def sent_together(arrays, axis, split_dim, concat_dim, along):
    ends, at = ([], 0)
    for a in arrays[:-1]:
        at += a.shape[along]
        ends.append(at)
    both = jnp.concatenate(arrays, axis=along)
    return tuple(
        jnp.split(
            lax.all_to_all(both, axis, split_axis=split_dim, concat_axis=concat_dim, tiled=True),
            ends,
            axis=along,
        )
    )


def laid_out(tiles, dim):
    tiles = jnp.moveaxis(tiles, 0, dim)
    dims = tiles.shape
    return tiles.reshape(*dims[:dim], dims[dim] * dims[dim + 1], *dims[dim + 2 :])


def gather_directly(shard, axis, dim):
    tiles = copy_for_each(shard, axis)
    return laid_out(tiles, dim)


def local(train_gate, train_up, train_down, router_weight, router_gain):
    total_gate, total_up, total_down = together(
        (
            jnp.sum(jnp.abs(train_gate), axis=1),
            jnp.sum(jnp.abs(train_up), axis=1),
            jnp.sum(jnp.abs(train_down), axis=2),
        ),
        "rows",
    )
    scale_gate = total_gate / D_MODEL
    scale_up = total_up / D_MODEL
    scale_down = total_down / D_MODEL
    narrow_gate, narrow_up, narrow_down = (
        (train_gate / jnp.expand_dims(scale_gate, 1)).astype(jnp.bfloat16),
        (train_up / jnp.expand_dims(scale_up, 1)).astype(jnp.bfloat16),
        (train_down / jnp.expand_dims(scale_down, 2)).astype(jnp.bfloat16),
    )
    ready_gate, ready_up = sent_together((narrow_gate, narrow_up), "rows", 2, 1, 0)
    ready_down = lax.all_to_all(narrow_down, "rows", split_axis=1, concat_axis=2, tiled=True)
    scale_gate = lax.dynamic_slice_in_dim(
        scale_gate, lax.axis_index("rows") * ready_gate.shape[2], ready_gate.shape[2], axis=1
    )
    scale_up = lax.dynamic_slice_in_dim(
        scale_up, lax.axis_index("rows") * ready_up.shape[2], ready_up.shape[2], axis=1
    )
    scale_down = lax.dynamic_slice_in_dim(
        scale_down, lax.axis_index("rows") * ready_down.shape[1], ready_down.shape[1], axis=1
    )
    part_router = (router_weight * router_gain[:, None]).astype(jnp.bfloat16)
    row_router = gather_directly(part_router, "rows", 0)
    serve_router = gather_directly(row_router, "owner", 1)
    return (ready_gate, ready_up, ready_down, scale_gate, scale_up, scale_down, serve_router)


def solution(mesh):
    return jax.shard_map(
        local,
        mesh=mesh,
        in_specs=(
            P("owner", "rows", None),
            P("owner", "rows", None),
            P("owner", None, "rows"),
            P("rows", "owner"),
            P("rows"),
        ),
        out_specs=(
            P("owner", None, "rows"),
            P("owner", None, "rows"),
            P("owner", "rows", None),
            P("owner", "rows"),
            P("owner", "rows"),
            P("owner", "rows"),
            P(),
        ),
        check_vma=False,
    )
```

profile of v0, /device:TPU:1, one launch (start us, length us, event | category | flops | bytes accessed | tf_op | source)
XLA Modules:
  0.0 150.2 jit_solution(6789340445049301006)
XLA Ops:
  0.6 0.8 multiply_convert_fusion
  2.1 10.0 %all-to-all-start.3 = ((bf16[16,128,4]{1,2,0:T(4,128)(2,1)}), bf16[16,128,4]{1,2,0:T(4,128)(2,1)S(1)}, u32[]{:S(2)}, u32[]{:S(2)}) async-start(bf16[16,128,4]{1,2,0:T(4,128)(2,1)} %broadcast_in_dim.9), calls=%async_computation.3 | async-start | bytes 32768 | tf_op jit(solution)/shard_map/all_to_all | solution.py:11
  12.1 2.0 %abs_reduce_fusion.1 = f32[4,1024]{1,0:T(4,128)S(1)} fusion(f32[4,128,1024]{2,1,0:T(8,128)} %param.6), kind=kLoop, calls=%fused_computation.3 | loop fusion | flops 1044480 | bytes 2113536 | tf_op jit(solution)/shard_map/reduce_sum | solution.py:59
  14.9 4.4 %all-to-all-done.3 = bf16[16,128,4]{1,2,0:T(4,128)(2,1)S(1)} async-done(((bf16[16,128,4]{1,2,0:T(4,128)(2,1)}), bf16[16,128,4]{1,2,0:T(4,128)(2,1)S(1)}, u32[]{:S(2)}, u32[]{:S(2)}) %all-to-all-start.3) | async-done | bytes 16416 | tf_op jit(solution)/shard_map/all_to_all | solution.py:11
  20.0 26.0 %all_to_all.49 = f32[16,1,12288]{2,1,0:T(1,128)S(1)} all-to-all(f32[16,1,12288]{2,1,0:T(1,128)S(1)} %broadcast_in_dim.8), channel_id=1, replica_groups=mesh['owner'=16,'rows'=16] {'rows'}, dimensions={0} | all-to-all | bytes 1572864 | tf_op jit(solution)/shard_map/all_to_all | solution.py:11
  46.0 0.8 broadcast_in_dim.11
  46.8 6.8 %all-to-all-start.4 = ((bf16[16,2048,4]{1,2,0:T(4,128)(2,1)}), bf16[16,2048,4]{1,2,0:T(4,128)(2,1)S(1)}, u32[]{:S(2)}, u32[]{:S(2)}) async-start(bf16[16,2048,4]{1,2,0:T(4,128)(2,1)} %broadcast_in_dim.11), calls=%async_computation.4 | async-start | bytes 524288 | tf_op jit(solution)/shard_map/all_to_all | solution.py:11
  54.3 7.2 %fusion = bf16[4,1024,128]{2,0,1:T(4,128)(2,1)} fusion(f32[4,1024,128]{2,1,0:T(8,128)S(1)} %copy-done, f32[4,1024]{0,1:T(8,128)S(1)} %copy.50), kind=kLoop, calls=%fused_computation.5 | loop fusion | flops 1048576 | bytes 3162112 | tf_op jit(solution)/shard_map/convert_element_type | solution.py:70
  61.5 1.2 all-to-all-done.4
  62.7 4.0 %all-to-all-start.2 = ((bf16[4,1024,128]{2,0,1:T(4,128)(2,1)}), bf16[4,1024,128]{2,0,1:T(4,128)(2,1)S(1)}, u32[]{:S(2)}, u32[]{:S(2)}) async-start(bf16[4,1024,128]{2,0,1:T(4,128)(2,1)} %fusion), calls=%async_computation.2 | async-start | bytes 2097152 | tf_op jit(solution)/shard_map/all_to_all | solution.py:73
  66.6 1.9 %copy.44 = f32[4,128,1024]{1,0,2:T(4,128)} copy(f32[4,128,1024]{2,1,0:T(8,128)S(1)} %copy-done.2) | data formatting | bytes 4194304 | tf_op args[0]
  68.5 2.0 %copy.46 = f32[4,128,1024]{1,0,2:T(4,128)S(1)} copy(f32[4,128,1024]{2,1,0:T(8,128)} %param.6) | data formatting | bytes 4194304 | tf_op args[1]
  70.5 1.0 copy.43
  71.6 1.0 copy.45
  72.6 3.6 %divide_convert_fusion.1 = bf16[4,128,1024]{1,0,2:T(4,128)(2,1)S(1)} fusion(f32[4,128,1024]{1,0,2:T(4,128)} %copy.44, f32[4,1024]{0,1:T(8,128)} %copy.43), kind=kLoop, calls=%fused_computation.7 | loop fusion | flops 1048576 | bytes 3162112 | tf_op jit(solution)/shard_map/convert_element_type | solution.py:68
  76.2 2.5 %divide_convert_fusion = bf16[4,128,1024]{1,0,2:T(4,128)(2,1)S(1)} fusion(f32[4,128,1024]{1,0,2:T(4,128)S(1)} %copy.46, f32[4,1024]{0,1:T(8,128)S(1)} %copy-done.3), kind=kLoop, calls=%fused_computation.6 | loop fusion | flops 1048576 | bytes 3162112 | tf_op jit(solution)/shard_map/convert_element_type | solution.py:69
  78.7 2.4 %pad_maximum_fusion = bf16[8,128,1024]{1,0,2:T(8,128)(2,1)} fusion(bf16[4,128,1024]{1,0,2:T(4,128)(2,1)S(1)} %divide_convert_fusion, bf16[4,128,1024]{1,0,2:T(4,128)(2,1)S(1)} %divide_convert_fusion.1), kind=kLoop, calls=%fused_computation | loop fusion | flops 4194304 | bytes 4194304 | tf_op jit(solution)/shard_map/concatenate | solution.py:34
  81.1 13.6 %all-to-all-done.2 = bf16[4,1024,128]{2,0,1:T(4,128)(2,1)S(1)} async-done(((bf16[4,1024,128]{2,0,1:T(4,128)(2,1)}), bf16[4,1024,128]{2,0,1:T(4,128)(2,1)S(1)}, u32[]{:S(2)}, u32[]{:S(2)}) %all-to-all-start.2) | async-done | bytes 1048608 | tf_op jit(solution)/shard_map/all_to_all | solution.py:73
  94.7 3.6 %all-to-all-start.1 = ((bf16[8,128,1024]{1,0,2:T(8,128)(2,1)}), bf16[8,128,1024]{1,0,2:T(8,128)(2,1)S(1)}, u32[]{:S(2)}, u32[]{:S(2)}) async-start(bf16[8,128,1024]{1,0,2:T(8,128)(2,1)} %pad_maximum_fusion), calls=%async_computation.1 | async-start | bytes 4194304 | tf_op jit(solution)/shard_map/all_to_all | solution.py:37
  101.0 1.6 %copy.52 = bf16[4,64,16,128]{3,2,1,0:T(8,128)(2,1)} copy(bf16[4,64,16,128]{3,0,1,2:T(4,128)(2,1)S(1)} %bitcast.33) | data formatting | bytes 2097152 | tf_op jit(solution)/shard_map/all_to_all | solution.py:73
  102.7 2.3 %all_to_all.41 = bf16[4,64,2048]{2,1,0:T(8,128)(2,1)} reshape(bf16[4,64,16,128]{3,2,1,0:T(8,128)(2,1)} %copy.52) | data formatting | bytes 2097152 | tf_op jit(solution)/shard_map/all_to_all | solution.py:73
  104.9 42.2 %all-to-all-done.1 = bf16[8,128,1024]{1,0,2:T(8,128)(2,1)S(1)} async-done(((bf16[8,128,1024]{1,0,2:T(8,128)(2,1)}), bf16[8,128,1024]{1,0,2:T(8,128)(2,1)S(1)}, u32[]{:S(2)}, u32[]{:S(2)}) %all-to-all-start.1) | async-done | bytes 2097184 | tf_op jit(solution)/shard_map/all_to_all | solution.py:37
  147.7 1.2 copy.70
  148.9 1.2 copy.71
  (27 shorter events, 6.1 us)
Async XLA Ops:
  0.6 13.4 %copy-start = (f32[4,1024,128]{2,1,0:T(8,128)S(1)}, f32[4,1024,128]{2,1,0:T(8,128)}, u32[]{:S(2)}) copy-start(f32[4,1024,128]{2,1,0:T(8,128)} %param.7) | copy-start | bytes 6291460
  2.1 17.3 %all-to-all-start.3 = ((bf16[16,128,4]{1,2,0:T(4,128)(2,1)}), bf16[16,128,4]{1,2,0:T(4,128)(2,1)S(1)}, u32[]{:S(2)}, u32[]{:S(2)}) async-start(bf16[16,128,4]{1,2,0:T(4,128)(2,1)} %broadcast_in_dim.9), calls=%async_computation.3 | async-start | bytes 32768 | tf_op jit(solution)/shard_map/all_to_all | solution.py:11
  12.1 2.6 %copy-start.1 = (f32[4,128,1024]{2,1,0:T(8,128)S(1)}, f32[4,128,1024]{2,1,0:T(8,128)}, u32[]{:S(2)}) copy-start(f32[4,128,1024]{2,1,0:T(8,128)} %param.5) | copy-start | bytes 6291460
  46.8 15.9 %all-to-all-start.4 = ((bf16[16,2048,4]{1,2,0:T(4,128)(2,1)}), bf16[16,2048,4]{1,2,0:T(4,128)(2,1)S(1)}, u32[]{:S(2)}, u32[]{:S(2)}) async-start(bf16[16,2048,4]{1,2,0:T(4,128)(2,1)} %broadcast_in_dim.11), calls=%async_computation.4 | async-start | bytes 524288 | tf_op jit(solution)/shard_map/all_to_all | solution.py:11
  61.5 5.1 %copy-start.2 = (f32[4,128,1024]{2,1,0:T(8,128)S(1)}, f32[4,128,1024]{2,1,0:T(8,128)}, u32[]{:S(2)}) copy-start(f32[4,128,1024]{2,1,0:T(8,128)} %param.5) | copy-start | bytes 6291460
  62.7 32.0 %all-to-all-start.2 = ((bf16[4,1024,128]{2,0,1:T(4,128)(2,1)}), bf16[4,1024,128]{2,0,1:T(4,128)(2,1)S(1)}, u32[]{:S(2)}, u32[]{:S(2)}) async-start(bf16[4,1024,128]{2,0,1:T(4,128)(2,1)} %fusion), calls=%async_computation.2 | async-start | bytes 2097152 | tf_op jit(solution)/shard_map/all_to_all | solution.py:73
  72.6 3.6 %copy-start.3 = (f32[4,1024]{0,1:T(8,128)S(1)}, f32[4,1024]{0,1:T(8,128)}, u32[]{:S(2)}) copy-start(f32[4,1024]{0,1:T(8,128)} %copy.45) | copy-start | bytes 49156
  94.7 52.5 %all-to-all-start.1 = ((bf16[8,128,1024]{1,0,2:T(8,128)(2,1)}), bf16[8,128,1024]{1,0,2:T(8,128)(2,1)S(1)}, u32[]{:S(2)}, u32[]{:S(2)}) async-start(bf16[8,128,1024]{1,0,2:T(8,128)(2,1)} %pad_maximum_fusion), calls=%async_computation.1 | async-start | bytes 4194304 | tf_op jit(solution)/shard_map/all_to_all | solution.py:37
where the time goes:
time: 151 us; the launch traced here: 150 us
  waiting for transfers between devices  61.4 us (41%)
  blocking collectives  26 us (17%)
  starting transfers between devices  24.3 us (16%)
  other arithmetic  19.8 us (13%)
  local copies, waits for them, and re-layouts  17.9 us (12%)
    all_to_all x1, waiting for transfers between devices, sent_together(): lax.all_to_all(both, axis, split_axis=split_dim, concat_axis=concat_dim,...  42.2 us
    all_to_all x1, blocking collectives, copy_for_each(): lax.all_to_all(jnp.broadcast_to(shard[None], (size, *shard.shape)), axis,...  26 us
    all_to_all x2, starting transfers between devices, copy_for_each(): lax.all_to_all(jnp.broadcast_to(shard[None], (size, *shard.shape)), axis,...  16.7 us
    all_to_all x1, waiting for transfers between devices, local(): lax.all_to_all(narrow_down, 'rows', split_axis=1, concat_axis=2, tiled=True)  13.6 us
    convert_element_type x1, other arithmetic, local(): (train_down / jnp.expand_dims(scale_down, 2)).astype(jnp.bfloat16)  7.16 us
    all_to_all x2, waiting for transfers between devices, copy_for_each(): lax.all_to_all(jnp.broadcast_to(shard[None], (size, *shard.shape)), axis,...  5.62 us
    unnamed x12, local copies, waits for them, and re-layouts  4.13 us
    all_to_all x1, starting transfers between devices, local(): lax.all_to_all(narrow_down, 'rows', split_axis=1, concat_axis=2, tiled=True)  3.96 us
  transfers between devices with their start and end apart: 4, of which 4 were waited for; matrix products, arithmetic and copies ran while one was open for 20% of the time, Pallas kernels for 0%

commit v1 on v0

v1 whole, which is shorter than its diff:
```python
import functools

import jax
import jax.numpy as jnp
from jax import lax
from jax.experimental import pallas as pl
from jax.experimental.pallas import tpu as pltpu
from jax.sharding import PartitionSpec as P


D_MODEL = 2048
E = 4
N = 3 * E
CHIPS = 8
POWER = 13
AMP = 700.0
FLOOR = 1e-25

FIRST = (3, -3)
REST = (1, -1, 2, -2, 4, 0)
ORDER = (
    (3, 0), (-3, 0), (3, 1), (-3, 1), (1, 0), (-1, 0), (2, 0), (-2, 0),
    (4, 0), (4, 1), (2, 1), (-2, 1), (1, 1), (-1, 1), (0, 1),
)


def place():
    r = lax.axis_index("rows")
    return r // 2, r % 2


def pairs_of(dz, dc):
    return [
        (2 * z + c, 2 * ((z + dz) % CHIPS) + (c ^ dc)) for z in range(CHIPS) for c in range(2)
    ]


def code(x, sums):
    v = x * (AMP / jnp.maximum(sums, FLOOR))
    v2 = v * v
    v4 = v2 * v2
    return (v4 * v4 * v4 * v).astype(jnp.bfloat16)


def fetches(dzs, z, ins, buf, sems):
    gate, up, down = ins
    out = []
    for i, dz in enumerate(dzs):
        at = pl.ds(pl.multiple_of(lax.rem(z + (dz % CHIPS), CHIPS) * 128, 128), 128)
        out.append(
            [
                pltpu.make_async_copy(gate.at[:, :, at], buf.at[i, 0], sems.at[i, 0]),
                pltpu.make_async_copy(up.at[:, :, at], buf.at[i, 1], sems.at[i, 1]),
                pltpu.make_async_copy(down.at[:, at, :], buf.at[i, 2], sems.at[i, 2]),
            ]
        )
    return out


def encode(dzs, place_ref, ins, outs, sums, buf, sems):
    z, c = place_ref[0], place_ref[1]
    copies = fetches(dzs, z, ins, buf, sems)
    for three in copies:
        for copy in three:
            copy.start()
    diagonal = lax.broadcasted_iota(jnp.int32, (128, 128), 0) == lax.broadcasted_iota(
        jnp.int32, (128, 128), 1
    )
    mine = c == 0
    for i, three in enumerate(copies):
        same, other = outs[2 * i], outs[2 * i + 1]
        for copy in three:
            copy.wait()

        def put(n, coded):
            low, high = coded[:64], coded[64:]
            same[n] = jnp.where(mine, low, high)
            other[n] = jnp.where(mine, high, low)

        def one(e, carry):
            for a in range(2):
                x = buf[i, a, e]
                total = jnp.sum(jnp.abs(x), axis=0, keepdims=True)
                sums[i, a * E + e] = total
                put(a * E + e, code(x, total).T)
            x = buf[i, 2, e]
            total = jnp.sum(jnp.abs(x), axis=1, keepdims=True)
            sums[i, 2 * E + e] = jnp.sum(jnp.where(diagonal, total, 0.0), axis=0, keepdims=True)
            put(2 * E + e, code(x, total))
            return carry

        lax.fori_loop(0, E, one, 0)


def first_kernel(place_ref, gate, up, down, *rest):
    outs, (sums, buf, sems) = rest[: 2 * len(FIRST)], rest[2 * len(FIRST) :]
    encode(FIRST, place_ref, (gate, up, down), outs, sums, buf, sems)


def rest_kernel(place_ref, gate, up, down, early, router, gain, *rest):
    outs, (table, sums, buf, sems) = rest[: 2 * len(REST)], rest[2 * len(REST) :]
    encode(REST, place_ref, (gate, up, down), outs, sums, buf, sems)
    z = place_ref[0]
    left = lax.broadcasted_iota(jnp.int32, (1, 128), 1) < 64
    served = (router[...] * gain[...]).astype(jnp.bfloat16).astype(jnp.float32)
    for dzs, ref in ((FIRST, early), (REST, sums)):
        for i, dz in enumerate(dzs):
            chip = lax.rem(z + (dz % CHIPS), CHIPS)
            for q in range(N // 2):
                a, b = ref[i, 2 * q], ref[i, 2 * q + 1]
                at = slice(q * 128, q * 128 + 128)
                table[2 * chip, :, at] = jnp.where(left, a, pltpu.roll(b, 64, 1))
                table[2 * chip + 1, :, at] = jnp.where(left, pltpu.roll(a, 64, 1), b)
            for core in range(2):
                for q in range(4):
                    at = slice((N // 2 + q) * 128, (N // 2 + q) * 128 + 128)
                    table[2 * chip + core, :, at] = served[q : q + 1]


def scale_kernel(table, gate, up, down, factors, rows):
    total = table[0]
    for s in range(1, 16):
        total = total + table[s]
    scale = total[:, : N // 2 * 128] / D_MODEL
    for n in range(N):
        out = (gate, up, down)[n // E]
        out[n % E : n % E + 1, :] = scale[:, n * 64 : n * 64 + 64]
    for s in range(16):
        f = jnp.maximum(table[s, :, : N // 2 * 128], FLOOR) / (AMP * scale)
        f = [f[:, q * 128 : q * 128 + 128] for q in range(N // 2)]
        factors[s] = jnp.concatenate(f + f[:2], axis=0).T
        for q in range(4):
            at = slice((N // 2 + q) * 128, (N // 2 + q) * 128 + 128)
            rows[q : q + 1, s * 128 : s * 128 + 128] = table[s, :, at].astype(jnp.bfloat16)


def decode_kernel(where, n_alias, place_ref, factors, *rest):
    n = len(where)
    pieces, rest = rest[:n], rest[n + n_alias :]
    outs, (buf, sems) = rest[:3], rest[3:]
    z, c = place_ref[0], place_ref[1]
    copies = []
    for i, (dz, dc) in enumerate(where):
        s = 2 * lax.rem(z + (-dz % CHIPS), CHIPS) + (c if dc == 0 else 1 - c)
        f = factors[s]
        for k in range(N):
            w = pieces[i][k].astype(jnp.float32)
            root = jnp.exp(jnp.log(jnp.abs(w)) * (1.0 / POWER))
            root = jnp.where(w < 0, -root, root)
            half = k % 2 * 64
            buf[i, k] = (root * f[half : half + 64, k // 2 : k // 2 + 1]).astype(jnp.bfloat16)
        at = pl.ds(pl.multiple_of(s * 128, 128), 128)
        for a in range(3):
            copy = pltpu.make_async_copy(
                buf.at[i, a * E : a * E + E], outs[a].at[:, :, at], sems.at[i, a]
            )
            copy.start()
            copies.append(copy)
    for copy in copies:
        copy.wait()


SMEM = pl.BlockSpec(memory_space=pltpu.SMEM)
VMEM = pl.BlockSpec(memory_space=pltpu.VMEM)
ANY = pl.BlockSpec(memory_space=pl.ANY)
PIECE = jax.ShapeDtypeStruct((N, 64, 128), jnp.bfloat16)


def decode(where, place_, factors, pieces, before):
    n = len(where)
    out = jax.ShapeDtypeStruct((E, 64, 16 * 128), jnp.bfloat16)
    return pl.pallas_call(
        functools.partial(decode_kernel, where, len(before)),
        out_shape=(out,) * 3,
        in_specs=[SMEM, VMEM] + [VMEM] * n + [ANY] * len(before),
        out_specs=(ANY,) * 3,
        scratch_shapes=[
            pltpu.VMEM((n, N, 64, 128), jnp.bfloat16),
            pltpu.SemaphoreType.DMA((n, 3)),
        ],
        input_output_aliases={2 + n + a: a for a in range(len(before))},
        cost_estimate=pl.CostEstimate(
            flops=n * 10_000_000, transcendentals=0, bytes_accessed=n * 400_000
        ),
    )(place_, factors, *pieces, *before)


GROUPS = (
    ((0, 0), (0, 1), (3, 0), (-3, 0), (3, 1), (-3, 1)),
    ((1, 0), (-1, 0), (2, 0), (-2, 0)),
    ((4, 0), (4, 1), (2, 1), (-2, 1), (1, 1), (-1, 1)),
)


def local(train_gate, train_up, train_down, router_weight, router_gain):
    z, c = place()
    place_ = jnp.stack([z, c]).astype(jnp.int32)
    ins = (train_gate, train_up, train_down)

    def scratch(n):
        return [
            pltpu.VMEM((n, 3, E, 128, 128), jnp.float32),
            pltpu.SemaphoreType.DMA((n, 3)),
        ]

    def rows_of(n):
        return jax.ShapeDtypeStruct((n, N, 1, 128), jnp.float32)

    nf, nr = len(FIRST), len(REST)
    *sent_first, early = pl.pallas_call(
        first_kernel,
        out_shape=(PIECE,) * (2 * nf) + (rows_of(nf),),
        in_specs=[SMEM, ANY, ANY, ANY],
        out_specs=(VMEM,) * (2 * nf + 1),
        scratch_shapes=scratch(nf),
        name="first",
    )(place_, *ins)
    *sent_rest, table = pl.pallas_call(
        rest_kernel,
        out_shape=(PIECE,) * (2 * nr) + (jax.ShapeDtypeStruct((16, 1, 1280), jnp.float32),),
        in_specs=[SMEM, ANY, ANY, ANY, VMEM, VMEM, VMEM],
        out_specs=(VMEM,) * (2 * nr + 1),
        scratch_shapes=[pltpu.VMEM((nr, N, 1, 128), jnp.float32)] + scratch(nr),
        name="rest",
    )(place_, *ins, early, router_weight.T, router_gain[None])
    sent = {}
    for dzs, pieces in ((FIRST, sent_first), (REST, sent_rest)):
        for i, dz in enumerate(dzs):
            sent[dz, 0], sent[dz, 1] = pieces[2 * i], pieces[2 * i + 1]
    got = {(0, 0): sent[0, 0]}
    for dz, dc in ORDER:
        got[dz, dc] = lax.ppermute(sent[dz, dc], "rows", pairs_of(dz, dc))
    table = lax.all_to_all(table, "rows", 0, 0, tiled=True)
    small = jax.ShapeDtypeStruct((E, 64), jnp.float32)
    scale_gate, scale_up, scale_down, factors, rows = pl.pallas_call(
        scale_kernel,
        out_shape=(small,) * 3
        + (
            jax.ShapeDtypeStruct((16, 128, 8), jnp.float32),
            jax.ShapeDtypeStruct((4, D_MODEL), jnp.bfloat16),
        ),
        in_specs=[VMEM],
        out_specs=(VMEM,) * 5,
        name="scales",
    )(table)
    wide = lax.all_to_all(jnp.broadcast_to(rows[None], (16, 4, D_MODEL)), "owner", 0, 0, tiled=True)
    serve_router = wide.reshape(64, D_MODEL).T
    outs = ()
    for where in GROUPS:
        outs = decode(where, place_, factors, [got[k] for k in where], outs)
    ready_gate, ready_up, ready_down = outs
    return (
        ready_gate.transpose(0, 2, 1),
        ready_up.transpose(0, 2, 1),
        ready_down,
        scale_gate,
        scale_up,
        scale_down,
        serve_router,
    )


def solution(mesh):
    return jax.shard_map(
        local,
        mesh=mesh,
        in_specs=(
            P("owner", "rows", None),
            P("owner", "rows", None),
            P("owner", None, "rows"),
            P("rows", "owner"),
            P("rows"),
        ),
        out_specs=(
            P("owner", None, "rows"),
            P("owner", None, "rows"),
            P("owner", "rows", None),
            P("owner", "rows"),
            P("owner", "rows"),
            P("owner", "rows"),
            P(),
        ),
        check_vma=False,
    )
```

time: 151 us -> 96.1 us (0.64)
  waiting for transfers between devices: 61.4 us -> 13.2 us
  starting transfers between devices: 24.3 us -> 54.5 us
  blocking collectives: 26 us -> 0 us
  Pallas kernels: 0 us -> 22.7 us
  other arithmetic: 19.8 us -> 0.67 us
  local copies, waits for them, and re-layouts: 17.9 us -> 3.65 us
    all_to_all x4 -> x2, waiting for transfers between devices: 61.4 us -> 0.01 us  [the longest x1 0.01 us: local(): table = lax.all_to_all(table, 'rows', 0, 0, tiled=True)]
    ppermute x0 -> x15, starting transfers between devices: none -> 42.4 us  [local(): got[dz, dc] = lax.ppermute(sent[dz, dc], 'rows', pairs_of(dz, dc))]
    all_to_all x1 -> x0, blocking collectives: 26 us -> none  [copy_for_each(): lax.all_to_all(jnp.broadcast_to(shard[None], (size, *shard.shape)), axis,...]
    pallas_call x0 -> x6, Pallas kernels: none -> 22.7 us  [the longest x3 10.2 us: decode(): pl.pallas_call(functools.partial(decode_kernel, where, len(before)), out_...]
    convert_element_type x4 -> x0, other arithmetic: 14 us -> none  [the longest x1 7.16 us: local(): (train_down / jnp.expand_dims(scale_down, 2)).astype(jnp.bfloat16)]
    ppermute x0 -> x15, waiting for transfers between devices: none -> 13.2 us  [local(): got[dz, dc] = lax.ppermute(sent[dz, dc], 'rows', pairs_of(dz, dc))]
    all_to_all x4 -> x2, starting transfers between devices: 24.3 us -> 12.1 us  [the longest x1 6.76 us: local(): lax.all_to_all(jnp.broadcast_to(rows[None], (16, 4, D_MODEL)), 'owner', 0...]
    all_to_all x3 -> x0, local copies, waits for them, and re-layouts: 4.21 us -> none  [the longest x2 3.94 us: local(): lax.all_to_all(narrow_down, 'rows', split_axis=1, concat_axis=2, tiled=True)]
  transfers between devices with their start and end apart: 4 -> 17, of which waited for: 4 -> 5; matrix products, arithmetic and copies ran while one was open for 20% -> 2% of each run, Pallas kernels for 0% -> 13%
where the time goes in v1:
time: 96.1 us; the launch traced here: 95.6 us
  starting transfers between devices  54.5 us (57%)
  Pallas kernels  22.7 us (24%)
  waiting for transfers between devices  13.2 us (14%)
  local copies, waits for them, and re-layouts  3.65 us (4%)
    ppermute x15, starting transfers between devices, local(): got[dz, dc] = lax.ppermute(sent[dz, dc], 'rows', pairs_of(dz, dc))  42.4 us
    ppermute x15, waiting for transfers between devices, local(): got[dz, dc] = lax.ppermute(sent[dz, dc], 'rows', pairs_of(dz, dc))  13.2 us
    pallas_call x3, Pallas kernels, decode(): pl.pallas_call(functools.partial(decode_kernel, where, len(before)), out_...  10.2 us
    all_to_all x1, starting transfers between devices, local(): lax.all_to_all(jnp.broadcast_to(rows[None], (16, 4, D_MODEL)), 'owner', 0...  6.76 us
    pallas_call x1, Pallas kernels, local(): pl.pallas_call(rest_kernel, out_shape=(PIECE,) * (2 * nr) + (jax.ShapeDty...  6.62 us
    all_to_all x1, starting transfers between devices, local(): table = lax.all_to_all(table, 'rows', 0, 0, tiled=True)  5.37 us
    pallas_call x1, Pallas kernels, local(): pl.pallas_call(first_kernel, out_shape=(PIECE,) * (2 * nf) + (rows_of(nf)...  3.6 us
    pallas_call x1, Pallas kernels, local(): pl.pallas_call(scale_kernel, out_shape=(small,) * 3 + (jax.ShapeDtypeStru...  2.27 us
  transfers between devices with their start and end apart: 17, of which 5 were waited for; matrix products, arithmetic and copies ran while one was open for 2% of the time, Pallas kernels for 13%

profile of v1, /device:TPU:1, one launch (start us, length us, event | category | flops | bytes accessed | tf_op | source)
XLA Modules:
  0.0 95.6 jit_solution(7324288140611145614)
XLA Ops:
  1.3 3.6 %first.1 = (bf16[12,64,128]{2,1,0:T(8,128)(2,1)}, bf16[12,64,128]{2,1,0:T(8,128)(2,1)}, bf16[12,64,128]{2,1,0:T(8,128)(2,1)}, bf16[12,64,128]{2,1,0:T(8,128)(2,1)}, f32[2,12,1,128]{3,2,1,0:T(1,128)}) custom-call(s32[2]{0:T(128)} %pad_add_fusion.place_ref, f32[4,128,1024]{2,1,0:T(8,128)} %gate.3, f32[4,128,1024]{2,1,0:T(8,128)} %up.3, f32[4,1024,128]{2,1,0:T(8,128)} %down.3), custom_call_target="tpu_custom_call" | custom-call | tf_op jit(solution)/shard_map/first/pallas_call | solution.py:210
  5.0 6.6 %rest.1 = (bf16[12,64,128]{2,1,0:T(8,128)(2,1)}, bf16[12,64,128]{2,1,0:T(8,128)(2,1)}, bf16[12,64,128]{2,1,0:T(8,128)(2,1)}, bf16[12,64,128]{2,1,0:T(8,128)(2,1)...) custom-call(s32[2]{0:T(128)} %pad_add_fusion.place_ref, ...), custom_call_target="tpu_custom_call" | custom-call | tf_op jit(solution)/shard_map/rest/pallas_call | solution.py:218
  11.6 7.8 %collective-permute-start = (bf16[12,64,128]{2,1,0:T(8,128)(2,1)}, bf16[12,64,128]{2,1,0:T(8,128)(2,1)S(1)}, u32[]{:S(2)}, u32[]{:S(2)}) collective-permute-start(bf16[12,64,128]{2,1,0:T(8,128)(2,1)} %get-tuple-element.42), channel_id=1, source_target_pairs={{0,8},{1,9},{2,10},{3,11},{4,12},{5,13},{6,14},{7,15},{8,0},{9,1},... | collective-permute-start | bytes 589832 | tf_op jit(solution)/shard_map/ppermute | solution.py:232
  20.2 1.9 %collective-permute-start.7 = (bf16[12,64,128]{2,1,0:T(8,128)(2,1)}, bf16[12,64,128]{2,1,0:T(8,128)(2,1)S(1)}, u32[]{:S(2)}, u32[]{:S(2)}) collective-permute-start(bf16[12,64,128]{2,1,0:T(8,128)(2,1)} %get-tuple-element.49), channel_id=1, source_target_pairs={{0,14},{1,15},{2,0},{3,1},{4,2},{5,3},{6,4},{7,5},{8,6},{9,7},{10,... | collective-permute-start | bytes 589832 | tf_op jit(solution)/shard_map/ppermute | solution.py:232
  22.1 3.6 %collective-permute-start.9 = (bf16[12,64,128]{2,1,0:T(8,128)(2,1)}, bf16[12,64,128]{2,1,0:T(8,128)(2,1)S(1)}, u32[]{:S(2)}, u32[]{:S(2)}) collective-permute-start(bf16[12,64,128]{2,1,0:T(8,128)(2,1)} %get-tuple-element.51), channel_id=1, source_target_pairs={{0,12},{1,13},{2,14},{3,15},{4,0},{5,1},{6,2},{7,3},{8,4},{9,5},{1... | collective-permute-start | bytes 589832 | tf_op jit(solution)/shard_map/ppermute | solution.py:232
  25.7 5.4 %all-to-all-start = ((f32[16,1,1280]{2,1,0:T(1,128)}), f32[16,1,1280]{2,1,0:T(1,128)S(1)}, u32[]{:S(2)}, u32[]{:S(2)}) async-start(f32[16,1,1280]{2,1,0:T(1,128)} %get-tuple-element.40), calls=%async_computation | async-start | bytes 163840 | tf_op jit(solution)/shard_map/all_to_all | solution.py:233
  31.4 2.0 %collective-permute-done.6.rest_0_ = bf16[12,64,128]{2,1,0:T(8,128)(2,1)S(1)} collective-permute-done((bf16[12,64,128]{2,1,0:T(8,128)(2,1)}, bf16[12,64,128]{2,1,0:T(8,128)(2,1)S(1)}, u32[]{:S(2)}, u32[]{:S(2)}) %collective-permute-start.6) | collective-permute-done | bytes 196640 | tf_op jit(solution)/shard_map/ppermute | solution.py:232
  33.4 1.6 %collective-permute-start.11 = (bf16[12,64,128]{2,1,0:T(8,128)(2,1)S(1)}, bf16[12,64,128]{2,1,0:T(8,128)(2,1)S(1)}, u32[]{:S(2)}, u32[]{:S(2)}) collective-permute-start(bf16[12,64,128]{2,1,0:T(8,128)(2,1)S(1)} %copy-done.19), channel_id=1, source_target_pairs={{0,6},{1,7},{2,8},{3,9},{4,10},{5,11},{6,12},{7,13},{8,14},{9,15},... | collective-permute-start | bytes 589832 | tf_op jit(solution)/shard_map/ppermute | solution.py:232
  35.0 3.0 %collective-permute-start.12 = (bf16[12,64,128]{2,1,0:T(8,128)(2,1)S(1)}, bf16[12,64,128]{2,1,0:T(8,128)(2,1)S(1)}, u32[]{:S(2)}, u32[]{:S(2)}) collective-permute-start(bf16[12,64,128]{2,1,0:T(8,128)(2,1)S(1)} %copy-done.18), channel_id=1, source_target_pairs={{0,10},{1,11},{2,12},{3,13},{4,14},{5,15},{6,0},{7,1},{8,2},{9,3},... | collective-permute-start | bytes 589832 | tf_op jit(solution)/shard_map/ppermute | solution.py:232
  37.9 7.1 %collective-permute-start.13 = (bf16[12,64,128]{2,1,0:T(8,128)(2,1)S(1)}, bf16[12,64,128]{2,1,0:T(8,128)(2,1)S(1)}, u32[]{:S(2)}, u32[]{:S(2)}) collective-permute-start(bf16[12,64,128]{2,1,0:T(8,128)(2,1)S(1)} %copy-done.17), channel_id=1, source_target_pairs={{0,7},{1,6},{2,9},{3,8},{4,11},{5,10},{6,13},{7,12},{8,15},{9,14},... | collective-permute-start | bytes 589832 | tf_op jit(solution)/shard_map/ppermute | solution.py:232
  45.1 1.7 %collective-permute-start.14 = (bf16[12,64,128]{2,1,0:T(8,128)(2,1)S(1)}, bf16[12,64,128]{2,1,0:T(8,128)(2,1)S(1)}, u32[]{:S(2)}, u32[]{:S(2)}) collective-permute-start(bf16[12,64,128]{2,1,0:T(8,128)(2,1)S(1)} %copy-done.16), channel_id=1, source_target_pairs={{0,11},{1,10},{2,13},{3,12},{4,15},{5,14},{6,1},{7,0},{8,3},{9,2},... | collective-permute-start | bytes 589832 | tf_op jit(solution)/shard_map/ppermute | solution.py:232
  47.4 2.3 %scales.1 = (f32[4,64]{1,0:T(4,128)}, f32[4,64]{1,0:T(4,128)}, f32[4,64]{1,0:T(4,128)}, f32[16,128,8]{2,1,0:T(8,128)}, bf16[4,2048]{1,0:T(4,128)(2,1)}) custom-call(f32[16,1,1280]{2,1,0:T(1,128)} %copy-done), custom_call_target="tpu_custom_call" | custom-call | tf_op jit(solution)/shard_map/scales/pallas_call | solution.py:235
  49.7 1.5 %broadcast_in_dim.10 = bf16[16,4,2048]{2,1,0:T(4,128)(2,1)} broadcast(bf16[4,2048]{1,0:T(4,128)(2,1)} %get-tuple-element.70), dimensions={1,2} | broadcast | bytes 278528 | tf_op jit(solution)/shard_map/broadcast_in_dim | solution.py:246
  51.2 6.8 %all-to-all-start.1 = ((bf16[16,4,2048]{2,1,0:T(4,128)(2,1)}), bf16[16,4,2048]{2,1,0:T(4,128)(2,1)S(1)}, u32[]{:S(2)}, u32[]{:S(2)}) async-start(bf16[16,4,2048]{2,1,0:T(4,128)(2,1)} %broadcast_in_dim.10), calls=%async_computation.1 | async-start | bytes 524288 | tf_op jit(solution)/shard_map/all_to_all | solution.py:246
  58.0 7.8 %collective-permute-start.1 = (bf16[12,64,128]{2,1,0:T(8,128)(2,1)}, bf16[12,64,128]{2,1,0:T(8,128)(2,1)S(1)}, u32[]{:S(2)}, u32[]{:S(2)}) collective-permute-start(bf16[12,64,128]{2,1,0:T(8,128)(2,1)} %get-tuple-element.43), channel_id=1, source_target_pairs={{0,9},{1,8},{2,11},{3,10},{4,13},{5,12},{6,15},{7,14},{8,1},{9,0},... | collective-permute-start | bytes 589832 | tf_op jit(solution)/shard_map/ppermute | solution.py:232
  65.8 1.4 %collective-permute-start.2 = (bf16[12,64,128]{2,1,0:T(8,128)(2,1)}, bf16[12,64,128]{2,1,0:T(8,128)(2,1)S(1)}, u32[]{:S(2)}, u32[]{:S(2)}) collective-permute-start(bf16[12,64,128]{2,1,0:T(8,128)(2,1)} %get-tuple-element.44), channel_id=1, source_target_pairs={{0,5},{1,4},{2,7},{3,6},{4,9},{5,8},{6,11},{7,10},{8,13},{9,12},{1... | collective-permute-start | bytes 589832 | tf_op jit(solution)/shard_map/ppermute | solution.py:232
  67.3 2.4 %collective-permute-start.3 = (bf16[12,64,128]{2,1,0:T(8,128)(2,1)}, bf16[12,64,128]{2,1,0:T(8,128)(2,1)S(1)}, u32[]{:S(2)}, u32[]{:S(2)}) collective-permute-start(bf16[12,64,128]{2,1,0:T(8,128)(2,1)} %get-tuple-element.45), channel_id=1, source_target_pairs={{0,13},{1,12},{2,15},{3,14},{4,1},{5,0},{6,3},{7,2},{8,5},{9,4},{1... | collective-permute-start | bytes 589832 | tf_op jit(solution)/shard_map/ppermute | solution.py:232
  70.8 1.9 %collective-permute-start.5 = (bf16[12,64,128]{2,1,0:T(8,128)(2,1)}, bf16[12,64,128]{2,1,0:T(8,128)(2,1)S(1)}, u32[]{:S(2)}, u32[]{:S(2)}) collective-permute-start(bf16[12,64,128]{2,1,0:T(8,128)(2,1)} %get-tuple-element.47), channel_id=1, source_target_pairs={{0,15},{1,14},{2,1},{3,0},{4,3},{5,2},{6,5},{7,4},{8,7},{9,6},{10,... | collective-permute-start | bytes 589832 | tf_op jit(solution)/shard_map/ppermute | solution.py:232
  72.7 3.6 %shard_map.108 = (bf16[4,64,2048]{2,1,0:T(8,128)(2,1)}, bf16[4,64,2048]{2,1,0:T(8,128)(2,1)}, bf16[4,64,2048]{2,1,0:T(8,128)(2,1)}) custom-call(s32[2]{0:T(128)} %pad_add_fusion.place_ref, f32[16,128,8]{2,1,0:T(8,128)} %get-tuple-element.41.factors, bf16[12,64,128]{2,1,0:T(8,128)(2,1)} %get-tuple-element.52.rest_0_, bf16[12,64,128]{2,1,0:T(8,128)(2,1)} %copy-done.11, ...), custom_call_target="tpu_custom_call" | custom-call | flops 60000000 | bytes 2400000 | tf_op jit(solution)/shard_map/pallas_call | solution.py:172
  76.4 3.0 %shard_map.109 = (bf16[4,64,2048]{2,1,0:T(8,128)(2,1)}, bf16[4,64,2048]{2,1,0:T(8,128)(2,1)}, bf16[4,64,2048]{2,1,0:T(8,128)(2,1)}) custom-call(s32[2]{0:T(128)} %pad_add_fusion.place_ref, f32[16,128,8]{2,1,0:T(8,128)} %get-tuple-element.41.factors, bf16[12,64,128]{2,1,0:T(8,128)(2,1)} %copy-done.2, ...), custom_call_target="tpu_custom_call", output_to_operand_aliasing={{0}: (6, {}), {1}: (7, {}), {2}: (8, {})} | custom-call | flops 40000000 | bytes 1600000 | tf_op jit(solution)/shard_map/pallas_call | solution.py:172
  79.4 4.1 %collective-permute-done.2.rest_2_ = bf16[12,64,128]{2,1,0:T(8,128)(2,1)S(1)} collective-permute-done((bf16[12,64,128]{2,1,0:T(8,128)(2,1)}, bf16[12,64,128]{2,1,0:T(8,128)(2,1)S(1)}, u32[]{:S(2)}, u32[]{:S(2)}) %collective-permute-start.2) | collective-permute-done | bytes 196640 | tf_op jit(solution)/shard_map/ppermute | solution.py:232
  83.5 3.0 %collective-permute-done.3.rest_3_ = bf16[12,64,128]{2,1,0:T(8,128)(2,1)S(1)} collective-permute-done((bf16[12,64,128]{2,1,0:T(8,128)(2,1)}, bf16[12,64,128]{2,1,0:T(8,128)(2,1)S(1)}, u32[]{:S(2)}, u32[]{:S(2)}) %collective-permute-start.3) | collective-permute-done | bytes 196640 | tf_op jit(solution)/shard_map/ppermute | solution.py:232
  86.5 2.9 %collective-permute-done.4.rest_4_ = bf16[12,64,128]{2,1,0:T(8,128)(2,1)S(1)} collective-permute-done((bf16[12,64,128]{2,1,0:T(8,128)(2,1)}, bf16[12,64,128]{2,1,0:T(8,128)(2,1)S(1)}, u32[]{:S(2)}, u32[]{:S(2)}) %collective-permute-start.4) | collective-permute-done | bytes 196640 | tf_op jit(solution)/shard_map/ppermute | solution.py:232
  91.2 3.6 %shard_map.110 = (bf16[4,64,2048]{2,1,0:T(8,128)(2,1)}, bf16[4,64,2048]{2,1,0:T(8,128)(2,1)}, bf16[4,64,2048]{2,1,0:T(8,128)(2,1)}) custom-call(s32[2]{0:T(128)} %pad_add_fusion.place_ref, f32[16,128,8]{2,1,0:T(8,128)} %get-tuple-element.41.factors, bf16[12,64,128]{2,1,0:T(8,128)(2,1)} %copy-done.1, ...), custom_call_target="tpu_custom_call", output_to_operand_aliasing={{0}: (8, {}), {1}: (9, {}), {2}: (10, {})} | custom-call | flops 60000000 | bytes 2400000 | tf_op jit(solution)/shard_map/pallas_call | solution.py:172
  (59 shorter events, 6.1 us)
Async XLA Ops:
  4.9 33.0 %copy-start.17 = (bf16[12,64,128]{2,1,0:T(8,128)(2,1)S(1)}, bf16[12,64,128]{2,1,0:T(8,128)(2,1)}, u32[]{:S(2)}) copy-start(bf16[12,64,128]{2,1,0:T(8,128)(2,1)} %get-tuple-element.56) | copy-start | bytes 589828
  5.0 40.1 %copy-start.16 = (bf16[12,64,128]{2,1,0:T(8,128)(2,1)S(1)}, bf16[12,64,128]{2,1,0:T(8,128)(2,1)}, u32[]{:S(2)}) copy-start(bf16[12,64,128]{2,1,0:T(8,128)(2,1)} %get-tuple-element.57) | copy-start | bytes 589828
  11.6 19.4 %collective-permute-start = (bf16[12,64,128]{2,1,0:T(8,128)(2,1)}, bf16[12,64,128]{2,1,0:T(8,128)(2,1)S(1)}, u32[]{:S(2)}, u32[]{:S(2)}) collective-permute-start(bf16[12,64,128]{2,1,0:T(8,128)(2,1)} %get-tuple-element.42), channel_id=1, source_target_pairs={{0,8},{1,9},{2,10},{3,11},{4,12},{5,13},{6,14},{7,15},{8,0},{9,1},... | collective-permute-start | bytes 589832 | tf_op jit(solution)/shard_map/ppermute | solution.py:232
  19.4 14.0 %collective-permute-start.6 = (bf16[12,64,128]{2,1,0:T(8,128)(2,1)}, bf16[12,64,128]{2,1,0:T(8,128)(2,1)S(1)}, u32[]{:S(2)}, u32[]{:S(2)}) collective-permute-start(bf16[12,64,128]{2,1,0:T(8,128)(2,1)} %get-tuple-element.48), channel_id=1, source_target_pairs={{0,2},{1,3},{2,4},{3,5},{4,6},{5,7},{6,8},{7,9},{8,10},{9,11},{10,... | collective-permute-start | bytes 589832 | tf_op jit(solution)/shard_map/ppermute | solution.py:232
  20.2 14.8 %collective-permute-start.7 = (bf16[12,64,128]{2,1,0:T(8,128)(2,1)}, bf16[12,64,128]{2,1,0:T(8,128)(2,1)S(1)}, u32[]{:S(2)}, u32[]{:S(2)}) collective-permute-start(bf16[12,64,128]{2,1,0:T(8,128)(2,1)} %get-tuple-element.49), channel_id=1, source_target_pairs={{0,14},{1,15},{2,0},{3,1},{4,2},{5,3},{6,4},{7,5},{8,6},{9,7},{10,... | collective-permute-start | bytes 589832 | tf_op jit(solution)/shard_map/ppermute | solution.py:232
  22.1 15.8 %collective-permute-start.8 = (bf16[12,64,128]{2,1,0:T(8,128)(2,1)}, bf16[12,64,128]{2,1,0:T(8,128)(2,1)S(1)}, u32[]{:S(2)}, u32[]{:S(2)}) collective-permute-start(bf16[12,64,128]{2,1,0:T(8,128)(2,1)} %get-tuple-element.50), channel_id=1, source_target_pairs={{0,4},{1,5},{2,6},{3,7},{4,8},{5,9},{6,10},{7,11},{8,12},{9,13},{1... | collective-permute-start | bytes 589832 | tf_op jit(solution)/shard_map/ppermute | solution.py:232
  22.1 23.0 %collective-permute-start.9 = (bf16[12,64,128]{2,1,0:T(8,128)(2,1)}, bf16[12,64,128]{2,1,0:T(8,128)(2,1)S(1)}, u32[]{:S(2)}, u32[]{:S(2)}) collective-permute-start(bf16[12,64,128]{2,1,0:T(8,128)(2,1)} %get-tuple-element.51), channel_id=1, source_target_pairs={{0,12},{1,13},{2,14},{3,15},{4,0},{5,1},{6,2},{7,3},{8,4},{9,5},{1... | collective-permute-start | bytes 589832 | tf_op jit(solution)/shard_map/ppermute | solution.py:232
  25.7 21.1 %all-to-all-start = ((f32[16,1,1280]{2,1,0:T(1,128)}), f32[16,1,1280]{2,1,0:T(1,128)S(1)}, u32[]{:S(2)}, u32[]{:S(2)}) async-start(f32[16,1,1280]{2,1,0:T(1,128)} %get-tuple-element.40), calls=%async_computation | async-start | bytes 163840 | tf_op jit(solution)/shard_map/all_to_all | solution.py:233
  31.0 59.5 %copy-start.1 = (bf16[12,64,128]{2,1,0:T(8,128)(2,1)}, bf16[12,64,128]{2,1,0:T(8,128)(2,1)S(1)}, u32[]{:S(2)}) copy-start(bf16[12,64,128]{2,1,0:T(8,128)(2,1)S(1)} %collective-permute-done.rest_0_) | copy-start | bytes 589828
  31.1 27.0 %collective-permute-start.10 = (bf16[12,64,128]{2,1,0:T(8,128)(2,1)}, bf16[12,64,128]{2,1,0:T(8,128)(2,1)S(1)}, u32[]{:S(2)}, u32[]{:S(2)}) collective-permute-start(bf16[12,64,128]{2,1,0:T(8,128)(2,1)} %get-tuple-element.53), channel_id=1, source_target_pairs={{0,1},{1,0},{2,3},{3,2},{4,5},{5,4},{6,7},{7,6},{8,9},{9,8},{10,11... | collective-permute-start | bytes 589832 | tf_op jit(solution)/shard_map/ppermute | solution.py:232
  33.4 42.9 %copy-start.2 = (bf16[12,64,128]{2,1,0:T(8,128)(2,1)}, bf16[12,64,128]{2,1,0:T(8,128)(2,1)S(1)}, u32[]{:S(2)}) copy-start(bf16[12,64,128]{2,1,0:T(8,128)(2,1)S(1)} %collective-permute-done.6.rest_0_) | copy-start | bytes 589828
  33.4 32.5 %collective-permute-start.11 = (bf16[12,64,128]{2,1,0:T(8,128)(2,1)S(1)}, bf16[12,64,128]{2,1,0:T(8,128)(2,1)S(1)}, u32[]{:S(2)}, u32[]{:S(2)}) collective-permute-start(bf16[12,64,128]{2,1,0:T(8,128)(2,1)S(1)} %copy-done.19), channel_id=1, source_target_pairs={{0,6},{1,7},{2,8},{3,9},{4,10},{5,11},{6,12},{7,13},{8,14},{9,15},... | collective-permute-start | bytes 589832 | tf_op jit(solution)/shard_map/ppermute | solution.py:232
  35.0 41.4 %copy-start.3 = (bf16[12,64,128]{2,1,0:T(8,128)(2,1)}, bf16[12,64,128]{2,1,0:T(8,128)(2,1)S(1)}, u32[]{:S(2)}) copy-start(bf16[12,64,128]{2,1,0:T(8,128)(2,1)S(1)} %collective-permute-done.7.rest_1_) | copy-start | bytes 589828
  35.0 32.3 %collective-permute-start.12 = (bf16[12,64,128]{2,1,0:T(8,128)(2,1)S(1)}, bf16[12,64,128]{2,1,0:T(8,128)(2,1)S(1)}, u32[]{:S(2)}, u32[]{:S(2)}) collective-permute-start(bf16[12,64,128]{2,1,0:T(8,128)(2,1)S(1)} %copy-done.18), channel_id=1, source_target_pairs={{0,10},{1,11},{2,12},{3,13},{4,14},{5,15},{6,0},{7,1},{8,2},{9,3},... | collective-permute-start | bytes 589832 | tf_op jit(solution)/shard_map/ppermute | solution.py:232
  37.9 38.4 %copy-start.4 = (bf16[12,64,128]{2,1,0:T(8,128)(2,1)}, bf16[12,64,128]{2,1,0:T(8,128)(2,1)S(1)}, u32[]{:S(2)}) copy-start(bf16[12,64,128]{2,1,0:T(8,128)(2,1)S(1)} %collective-permute-done.8.rest_2_) | copy-start | bytes 589828
  37.9 31.8 %collective-permute-start.13 = (bf16[12,64,128]{2,1,0:T(8,128)(2,1)S(1)}, bf16[12,64,128]{2,1,0:T(8,128)(2,1)S(1)}, u32[]{:S(2)}, u32[]{:S(2)}) collective-permute-start(bf16[12,64,128]{2,1,0:T(8,128)(2,1)S(1)} %copy-done.17), channel_id=1, source_target_pairs={{0,7},{1,6},{2,9},{3,8},{4,11},{5,10},{6,13},{7,12},{8,15},{9,14},... | collective-permute-start | bytes 589832 | tf_op jit(solution)/shard_map/ppermute | solution.py:232
  45.1 31.3 %copy-start.5 = (bf16[12,64,128]{2,1,0:T(8,128)(2,1)}, bf16[12,64,128]{2,1,0:T(8,128)(2,1)S(1)}, u32[]{:S(2)}) copy-start(bf16[12,64,128]{2,1,0:T(8,128)(2,1)S(1)} %collective-permute-done.9.rest_3_) | copy-start | bytes 589828
  45.1 25.7 %collective-permute-start.14 = (bf16[12,64,128]{2,1,0:T(8,128)(2,1)S(1)}, bf16[12,64,128]{2,1,0:T(8,128)(2,1)S(1)}, u32[]{:S(2)}, u32[]{:S(2)}) collective-permute-start(bf16[12,64,128]{2,1,0:T(8,128)(2,1)S(1)} %copy-done.16), channel_id=1, source_target_pairs={{0,11},{1,10},{2,13},{3,12},{4,15},{5,14},{6,1},{7,0},{8,3},{9,2},... | collective-permute-start | bytes 589832 | tf_op jit(solution)/shard_map/ppermute | solution.py:232
  51.2 43.6 %all-to-all-start.1 = ((bf16[16,4,2048]{2,1,0:T(4,128)(2,1)}), bf16[16,4,2048]{2,1,0:T(4,128)(2,1)S(1)}, u32[]{:S(2)}, u32[]{:S(2)}) async-start(bf16[16,4,2048]{2,1,0:T(4,128)(2,1)} %broadcast_in_dim.10), calls=%async_computation.1 | async-start | bytes 524288 | tf_op jit(solution)/shard_map/all_to_all | solution.py:246
  58.0 21.4 %collective-permute-start.1 = (bf16[12,64,128]{2,1,0:T(8,128)(2,1)}, bf16[12,64,128]{2,1,0:T(8,128)(2,1)S(1)}, u32[]{:S(2)}, u32[]{:S(2)}) collective-permute-start(bf16[12,64,128]{2,1,0:T(8,128)(2,1)} %get-tuple-element.43), channel_id=1, source_target_pairs={{0,9},{1,8},{2,11},{3,10},{4,13},{5,12},{6,15},{7,14},{8,1},{9,0},... | collective-permute-start | bytes 589832 | tf_op jit(solution)/shard_map/ppermute | solution.py:232
  65.8 17.7 %collective-permute-start.2 = (bf16[12,64,128]{2,1,0:T(8,128)(2,1)}, bf16[12,64,128]{2,1,0:T(8,128)(2,1)S(1)}, u32[]{:S(2)}, u32[]{:S(2)}) collective-permute-start(bf16[12,64,128]{2,1,0:T(8,128)(2,1)} %get-tuple-element.44), channel_id=1, source_target_pairs={{0,5},{1,4},{2,7},{3,6},{4,9},{5,8},{6,11},{7,10},{8,13},{9,12},{1... | collective-permute-start | bytes 589832 | tf_op jit(solution)/shard_map/ppermute | solution.py:232
  67.3 19.2 %collective-permute-start.3 = (bf16[12,64,128]{2,1,0:T(8,128)(2,1)}, bf16[12,64,128]{2,1,0:T(8,128)(2,1)S(1)}, u32[]{:S(2)}, u32[]{:S(2)}) collective-permute-start(bf16[12,64,128]{2,1,0:T(8,128)(2,1)} %get-tuple-element.45), channel_id=1, source_target_pairs={{0,13},{1,12},{2,15},{3,14},{4,1},{5,0},{6,3},{7,2},{8,5},{9,4},{1... | collective-permute-start | bytes 589832 | tf_op jit(solution)/shard_map/ppermute | solution.py:232
  69.7 19.7 %collective-permute-start.4 = (bf16[12,64,128]{2,1,0:T(8,128)(2,1)}, bf16[12,64,128]{2,1,0:T(8,128)(2,1)S(1)}, u32[]{:S(2)}, u32[]{:S(2)}) collective-permute-start(bf16[12,64,128]{2,1,0:T(8,128)(2,1)} %get-tuple-element.46), channel_id=1, source_target_pairs={{0,3},{1,2},{2,5},{3,4},{4,7},{5,6},{6,9},{7,8},{8,11},{9,10},{10,... | collective-permute-start | bytes 589832 | tf_op jit(solution)/shard_map/ppermute | solution.py:232
  70.8 19.8 %collective-permute-start.5 = (bf16[12,64,128]{2,1,0:T(8,128)(2,1)}, bf16[12,64,128]{2,1,0:T(8,128)(2,1)S(1)}, u32[]{:S(2)}, u32[]{:S(2)}) collective-permute-start(bf16[12,64,128]{2,1,0:T(8,128)(2,1)} %get-tuple-element.47), channel_id=1, source_target_pairs={{0,15},{1,14},{2,1},{3,0},{4,3},{5,2},{6,5},{7,4},{8,7},{9,6},{10,... | collective-permute-start | bytes 589832 | tf_op jit(solution)/shard_map/ppermute | solution.py:232
  (13 other events, 115.2 us)

commit v2 on v1

--- a/solution.py
+++ b/solution.py
@@ -19,8 +19,8 @@
 FIRST = (3, -3)
 REST = (1, -1, 2, -2, 4, 0)
 ORDER = (
-    (3, 0), (-3, 0), (3, 1), (-3, 1), (1, 0), (-1, 0), (2, 0), (-2, 0),
-    (4, 0), (4, 1), (2, 1), (-2, 1), (1, 1), (-1, 1), (0, 1),
+    (3, 0), (-3, 0), (3, 1), (-3, 1), (0, 1), (4, 0), (4, 1), (2, 0), (-2, 0),
+    (2, 1), (-2, 1), (1, 0), (-1, 0), (1, 1), (-1, 1),
 )
 
 
@@ -117,7 +117,7 @@
                     table[2 * chip + core, :, at] = served[q : q + 1]
 
 
-def scale_kernel(table, gate, up, down, factors, rows):
+def scale_kernel(table, gate, up, down, factors, rows, line):
     total = table[0]
     for s in range(1, 16):
         total = total + table[s]
@@ -131,7 +131,9 @@
         factors[s] = jnp.concatenate(f + f[:2], axis=0).T
         for q in range(4):
             at = slice((N // 2 + q) * 128, (N // 2 + q) * 128 + 128)
-            rows[q : q + 1, s * 128 : s * 128 + 128] = table[s, :, at].astype(jnp.bfloat16)
+            line[q : q + 1, s * 128 : s * 128 + 128] = table[s, :, at].astype(jnp.bfloat16)
+    for d in range(16):
+        rows[d] = line[...]
 
 
 def decode_kernel(where, n_alias, place_ref, factors, *rest):
@@ -163,7 +165,11 @@
 SMEM = pl.BlockSpec(memory_space=pltpu.SMEM)
 VMEM = pl.BlockSpec(memory_space=pltpu.VMEM)
 ANY = pl.BlockSpec(memory_space=pl.ANY)
-PIECE = jax.ShapeDtypeStruct((N, 64, 128), jnp.bfloat16)
+PIECE = pltpu.VMEM((N, 64, 128), jnp.bfloat16)
+
+
+def kept(x):
+    return pltpu.with_memory_space_constraint(x, pltpu.VMEM)
 
 
 def decode(where, place_, factors, pieces, before):
@@ -182,13 +188,14 @@
         cost_estimate=pl.CostEstimate(
             flops=n * 10_000_000, transcendentals=0, bytes_accessed=n * 400_000
         ),
-    )(place_, factors, *pieces, *before)
+    )(place_, kept(factors), *map(kept, pieces), *before)
 
 
 GROUPS = (
     ((0, 0), (0, 1), (3, 0), (-3, 0), (3, 1), (-3, 1)),
-    ((1, 0), (-1, 0), (2, 0), (-2, 0)),
-    ((4, 0), (4, 1), (2, 1), (-2, 1), (1, 1), (-1, 1)),
+    ((4, 0), (4, 1), (2, 0), (-2, 0)),
+    ((2, 1), (-2, 1), (1, 0), (-1, 0)),
+    ((1, 1), (-1, 1)),
 )
 
 
@@ -236,14 +243,15 @@
         scale_kernel,
         out_shape=(small,) * 3
         + (
-            jax.ShapeDtypeStruct((16, 128, 8), jnp.float32),
-            jax.ShapeDtypeStruct((4, D_MODEL), jnp.bfloat16),
+            pltpu.VMEM((16, 128, 8), jnp.float32),
+            pltpu.VMEM((16, 4, D_MODEL), jnp.bfloat16),
         ),
         in_specs=[VMEM],
         out_specs=(VMEM,) * 5,
+        scratch_shapes=[pltpu.VMEM((4, D_MODEL), jnp.bfloat16)],
         name="scales",
     )(table)
-    wide = lax.all_to_all(jnp.broadcast_to(rows[None], (16, 4, D_MODEL)), "owner", 0, 0, tiled=True)
+    wide = lax.all_to_all(rows, "owner", 0, 0, tiled=True)
     serve_router = wide.reshape(64, D_MODEL).T
     outs = ()
     for where in GROUPS:

time: 96.1 us -> 96.3 us (level)
  local copies, waits for them, and re-layouts: 3.65 us -> 14.7 us
  waiting for transfers between devices: 13.2 us -> 7.36 us
  starting transfers between devices: 54.5 us -> 51.3 us
  Pallas kernels: 22.7 us -> 21 us
    unnamed x40 -> x34, local copies, waits for them, and re-layouts: 1.36 us -> 12.9 us
    ppermute x15, waiting for transfers between devices: 13.2 us -> 3.77 us  [local(): got[dz, dc] = lax.ppermute(sent[dz, dc], 'rows', pairs_of(dz, dc))]
    ppermute x15, starting transfers between devices: 42.4 us -> 37.7 us  [local(): got[dz, dc] = lax.ppermute(sent[dz, dc], 'rows', pairs_of(dz, dc))]
    all_to_all x1, waiting for transfers between devices: 0.01 us -> 3.59 us  [local(): table = lax.all_to_all(table, 'rows', 0, 0, tiled=True)]
    broadcast_in_dim x1 -> x0, local copies, waits for them, and re-layouts: 1.52 us -> none  [local(): jnp.broadcast_to(rows[None], (16, 4, D_MODEL))]
    all_to_all x1, starting transfers between devices: 5.37 us -> 6.79 us  [local(): table = lax.all_to_all(table, 'rows', 0, 0, tiled=True)]
    pallas_call x3 -> x4, Pallas kernels: 10.2 us -> 9.46 us  [decode(): pl.pallas_call(functools.partial(decode_kernel, where, len(before)), out_...]
  transfers between devices with their start and end apart: 17 -> 17, of which waited for: 5 -> 3; matrix products, arithmetic and copies ran while one was open for 2% -> 0% of each run, Pallas kernels for 13% -> 18%
where the time goes in v2:
time: 96.3 us; the launch traced here: 95.7 us
  starting transfers between devices  51.3 us (53%)
  Pallas kernels  21 us (22%)
  local copies, waits for them, and re-layouts  14.7 us (15%)
  waiting for transfers between devices  7.36 us (8%)
    ppermute x15, starting transfers between devices, local(): got[dz, dc] = lax.ppermute(sent[dz, dc], 'rows', pairs_of(dz, dc))  37.7 us
    unnamed x34, local copies, waits for them, and re-layouts  12.9 us
    pallas_call x4, Pallas kernels, decode(): pl.pallas_call(functools.partial(decode_kernel, where, len(before)), out_...  9.46 us
    all_to_all x1, starting transfers between devices, local(): wide = lax.all_to_all(rows, 'owner', 0, 0, tiled=True)  6.81 us
    all_to_all x1, starting transfers between devices, local(): table = lax.all_to_all(table, 'rows', 0, 0, tiled=True)  6.79 us
    pallas_call x1, Pallas kernels, local(): pl.pallas_call(rest_kernel, out_shape=(PIECE,) * (2 * nr) + (jax.ShapeDty...  6.02 us
    ppermute x15, waiting for transfers between devices, local(): got[dz, dc] = lax.ppermute(sent[dz, dc], 'rows', pairs_of(dz, dc))  3.77 us
    all_to_all x1, waiting for transfers between devices, local(): table = lax.all_to_all(table, 'rows', 0, 0, tiled=True)  3.59 us
  transfers between devices with their start and end apart: 17, of which 3 were waited for; matrix products, arithmetic and copies ran while one was open for 0% of the time, Pallas kernels for 18%

profile of v2, /device:TPU:1, one launch (start us, length us, event | category | flops | bytes accessed | tf_op | source)
XLA Modules:
  0.0 95.7 jit_solution(5100422639799148648)
XLA Ops:
  1.2 3.5 %first.1 = (bf16[12,64,128]{2,1,0:T(8,128)(2,1)}, bf16[12,64,128]{2,1,0:T(8,128)(2,1)S(1)}, bf16[12,64,128]{2,1,0:T(8,128)(2,1)}, bf16[12,64,128]{2,1,0:T(8,128)(2,1)S(1)}, f32[2,12,1,128]{3,2,1,0:T(1,128)}) custom-call(s32[2]{0:T(128)} %pad_add_fusion.place_ref, f32[4,128,1024]{2,1,0:T(8,128)} %gate.3, f32[4,128,1024]{2,1,0:T(8,128)} %up.3, ...), custom_call_target="tpu_custom_call" | custom-call | tf_op jit(solution)/shard_map/first/pallas_call | solution.py:217
  4.8 5.2 %collective-permute-start.11 = (bf16[12,64,128]{2,1,0:T(8,128)(2,1)}, bf16[12,64,128]{2,1,0:T(8,128)(2,1)S(1)}, u32[]{:S(2)}, u32[]{:S(2)}) collective-permute-start(bf16[12,64,128]{2,1,0:T(8,128)(2,1)} %get-tuple-element.57), channel_id=1, source_target_pairs={{0,6},{1,7},{2,8},{3,9},{4,10},{5,11},{6,12},{7,13},{8,14},{9,15},... | collective-permute-start | bytes 589832 | tf_op jit(solution)/shard_map/ppermute | solution.py:239
  10.0 2.2 %collective-permute-start.12 = (bf16[12,64,128]{2,1,0:T(8,128)(2,1)}, bf16[12,64,128]{2,1,0:T(8,128)(2,1)S(1)}, u32[]{:S(2)}, u32[]{:S(2)}) collective-permute-start(bf16[12,64,128]{2,1,0:T(8,128)(2,1)} %get-tuple-element.58), channel_id=1, source_target_pairs={{0,10},{1,11},{2,12},{3,13},{4,14},{5,15},{6,0},{7,1},{8,2},{9,3},... | collective-permute-start | bytes 589832 | tf_op jit(solution)/shard_map/ppermute | solution.py:239
  12.2 2.4 %collective-permute-start.13 = (bf16[12,64,128]{2,1,0:T(8,128)(2,1)S(1)}, bf16[12,64,128]{2,1,0:T(8,128)(2,1)S(1)}, u32[]{:S(2)}, u32[]{:S(2)}) collective-permute-start(bf16[12,64,128]{2,1,0:T(8,128)(2,1)S(1)} %get-tuple-element.59), channel_id=1, source_target_pairs={{0,7},{1,6},{2,9},{3,8},{4,11},{5,10},{6,13},{7,12},{8,15},{9,14},... | collective-permute-start | bytes 589832 | tf_op jit(solution)/shard_map/ppermute | solution.py:239
  14.6 3.1 %collective-permute-start.14 = (bf16[12,64,128]{2,1,0:T(8,128)(2,1)S(1)}, bf16[12,64,128]{2,1,0:T(8,128)(2,1)S(1)}, u32[]{:S(2)}, u32[]{:S(2)}) collective-permute-start(bf16[12,64,128]{2,1,0:T(8,128)(2,1)S(1)} %get-tuple-element.60), channel_id=1, source_target_pairs={{0,11},{1,10},{2,13},{3,12},{4,15},{5,14},{6,1},{7,0},{8,3},{9,2},... | collective-permute-start | bytes 589832 | tf_op jit(solution)/shard_map/ppermute | solution.py:239
  17.7 6.0 %rest.1 = (bf16[12,64,128]{2,1,0:T(8,128)(2,1)S(1)}, bf16[12,64,128]{2,1,0:T(8,128)(2,1)S(1)}, bf16[12,64,128]{2,1,0:T(8,128)(2,1)S(1)}, bf16[12,64,128]{2,1,0:T...) custom-call(s32[2]{0:T(128)} %pad_add_fusion.place_ref, ...), custom_call_target="tpu_custom_call" | custom-call | tf_op jit(solution)/shard_map/rest/pallas_call | solution.py:225
  27.1 1.3 %collective-permute-start.2 = (bf16[12,64,128]{2,1,0:T(8,128)(2,1)S(1)}, bf16[12,64,128]{2,1,0:T(8,128)(2,1)S(1)}, u32[]{:S(2)}, u32[]{:S(2)}) collective-permute-start(bf16[12,64,128]{2,1,0:T(8,128)(2,1)S(1)} %get-tuple-element.47), channel_id=1, source_target_pairs={{0,5},{1,4},{2,7},{3,6},{4,9},{5,8},{6,11},{7,10},{8,13},{9,12},{1... | collective-permute-start | bytes 589832 | tf_op jit(solution)/shard_map/ppermute | solution.py:239
  28.4 6.8 %all-to-all-start = ((f32[16,1,1280]{2,1,0:T(1,128)}), f32[16,1,1280]{2,1,0:T(1,128)S(1)}, u32[]{:S(2)}, u32[]{:S(2)}) async-start(f32[16,1,1280]{2,1,0:T(1,128)} %get-tuple-element.43), calls=%async_computation | async-start | bytes 163840 | tf_op jit(solution)/shard_map/all_to_all | solution.py:240
  35.9 5.3 %collective-permute-start.6 = (bf16[12,64,128]{2,1,0:T(8,128)(2,1)S(1)}, bf16[12,64,128]{2,1,0:T(8,128)(2,1)S(1)}, u32[]{:S(2)}, u32[]{:S(2)}) collective-permute-start(bf16[12,64,128]{2,1,0:T(8,128)(2,1)S(1)} %get-tuple-element.51), channel_id=1, source_target_pairs={{0,8},{1,9},{2,10},{3,11},{4,12},{5,13},{6,14},{7,15},{8,0},{9,1},... | collective-permute-start | bytes 589832 | tf_op jit(solution)/shard_map/ppermute | solution.py:239
  42.9 2.5 %collective-permute-start.8 = (bf16[12,64,128]{2,1,0:T(8,128)(2,1)}, bf16[12,64,128]{2,1,0:T(8,128)(2,1)S(1)}, u32[]{:S(2)}, u32[]{:S(2)}) collective-permute-start(bf16[12,64,128]{2,1,0:T(8,128)(2,1)} %get-tuple-element.53), channel_id=1, source_target_pairs={{0,4},{1,5},{2,6},{3,7},{4,8},{5,9},{6,10},{7,11},{8,12},{9,13},{1... | collective-permute-start | bytes 589832 | tf_op jit(solution)/shard_map/ppermute | solution.py:239
  46.1 1.2 %collective-permute-start.9 = (bf16[12,64,128]{2,1,0:T(8,128)(2,1)}, bf16[12,64,128]{2,1,0:T(8,128)(2,1)S(1)}, u32[]{:S(2)}, u32[]{:S(2)}) collective-permute-start(bf16[12,64,128]{2,1,0:T(8,128)(2,1)} %get-tuple-element.54), channel_id=1, source_target_pairs={{0,12},{1,13},{2,14},{3,15},{4,0},{5,1},{6,2},{7,3},{8,4},{9,5},{1... | collective-permute-start | bytes 589832 | tf_op jit(solution)/shard_map/ppermute | solution.py:239
  48.0 3.6 %all-to-all-done.table = f32[16,1,1280]{2,1,0:T(1,128)S(1)} async-done(((f32[16,1,1280]{2,1,0:T(1,128)}), f32[16,1,1280]{2,1,0:T(1,128)S(1)}, u32[]{:S(2)}, u32[]{:S(2)}) %all-to-all-start) | async-done | bytes 81952 | tf_op jit(solution)/shard_map/all_to_all | solution.py:240
  52.2 2.0 %scales.1 = (f32[4,64]{1,0:T(4,128)}, f32[4,64]{1,0:T(4,128)}, f32[4,64]{1,0:T(4,128)}, f32[16,128,8]{2,1,0:T(8,128)S(1)}, bf16[16,4,2048]{2,1,0:T(4,128)(2,1)}) custom-call(f32[16,1,1280]{2,1,0:T(1,128)} %copy-done.16), custom_call_target="tpu_custom_call" | custom-call | tf_op jit(solution)/shard_map/scales/pallas_call | solution.py:242
  54.2 6.8 %all-to-all-start.1 = ((bf16[16,4,2048]{2,1,0:T(4,128)(2,1)}), bf16[16,4,2048]{2,1,0:T(4,128)(2,1)}, u32[]{:S(2)}, u32[]{:S(2)}) async-start(bf16[16,4,2048]{2,1,0:T(4,128)(2,1)} %get-tuple-element.76), calls=%async_computation.1 | async-start | bytes 524288 | tf_op jit(solution)/shard_map/all_to_all | solution.py:254
  61.0 9.0 %collective-permute-start.3 = (bf16[12,64,128]{2,1,0:T(8,128)(2,1)}, bf16[12,64,128]{2,1,0:T(8,128)(2,1)S(1)}, u32[]{:S(2)}, u32[]{:S(2)}) collective-permute-start(bf16[12,64,128]{2,1,0:T(8,128)(2,1)} %get-tuple-element.48), channel_id=1, source_target_pairs={{0,13},{1,12},{2,15},{3,14},{4,1},{5,0},{6,3},{7,2},{8,5},{9,4},{1... | collective-permute-start | bytes 589832 | tf_op jit(solution)/shard_map/ppermute | solution.py:239
  70.0 3.5 %collective-permute-done.8.rest_2_ = bf16[12,64,128]{2,1,0:T(8,128)(2,1)S(1)} collective-permute-done((bf16[12,64,128]{2,1,0:T(8,128)(2,1)}, bf16[12,64,128]{2,1,0:T(8,128)(2,1)S(1)}, u32[]{:S(2)}, u32[]{:S(2)}) %collective-permute-start.8) | collective-permute-done | bytes 196640 | tf_op jit(solution)/shard_map/ppermute | solution.py:239
  73.5 2.6 %collective-permute-start = (bf16[12,64,128]{2,1,0:T(8,128)(2,1)}, bf16[12,64,128]{2,1,0:T(8,128)(2,1)}, u32[]{:S(2)}, u32[]{:S(2)}) collective-permute-start(bf16[12,64,128]{2,1,0:T(8,128)(2,1)} %copy-done.13), channel_id=1, source_target_pairs={{0,3},{1,2},{2,5},{3,4},{4,7},{5,6},{6,9},{7,8},{8,11},{9,10},{10,... | collective-permute-start | bytes 589832 | tf_op jit(solution)/shard_map/ppermute | solution.py:239
  76.8 2.1 %collective-permute-start.1 = (bf16[12,64,128]{2,1,0:T(8,128)(2,1)}, bf16[12,64,128]{2,1,0:T(8,128)(2,1)}, u32[]{:S(2)}, u32[]{:S(2)}) collective-permute-start(bf16[12,64,128]{2,1,0:T(8,128)(2,1)} %copy-done.12), channel_id=1, source_target_pairs={{0,15},{1,14},{2,1},{3,0},{4,3},{5,2},{6,5},{7,4},{8,7},{9,6},{10,... | collective-permute-start | bytes 589832 | tf_op jit(solution)/shard_map/ppermute | solution.py:239
  78.8 0.9 copy-done.1
  84.4 2.6 %shard_map.108 = (bf16[4,64,2048]{2,1,0:T(8,128)(2,1)}, bf16[4,64,2048]{2,1,0:T(8,128)(2,1)}, bf16[4,64,2048]{2,1,0:T(8,128)(2,1)}) custom-call(s32[2]{0:T(128)} %pad_add_fusion.place_ref, f32[16,128,8]{2,1,0:T(8,128)S(1)} %get-tuple-element.44.factors, bf16[12,64,128]{2,1,0:T(8,128)(2,1)S(1)} %copy-done.9, bf16[12,64,128]{2,1,0:T(8,128)(2,1)S(1)} %copy-done.11, ...), custom_call_target="tpu_custom_call" | custom-call | flops 60000000 | bytes 2400000 | tf_op jit(solution)/shard_map/pallas_call | solution.py:178
  87.0 2.2 %shard_map.109 = (bf16[4,64,2048]{2,1,0:T(8,128)(2,1)}, bf16[4,64,2048]{2,1,0:T(8,128)(2,1)}, bf16[4,64,2048]{2,1,0:T(8,128)(2,1)}) custom-call(s32[2]{0:T(128)} %pad_add_fusion.place_ref, f32[16,128,8]{2,1,0:T(8,128)S(1)} %get-tuple-element.44.factors, ...), custom_call_target="tpu_custom_call", output_to_operand_aliasing={{0}: (6, {}), {1}: (7, {}), {2}: (8, {})} | custom-call | flops 40000000 | bytes 1600000 | tf_op jit(solution)/shard_map/pallas_call | solution.py:178
  89.2 2.6 %shard_map.110 = (bf16[4,64,2048]{2,1,0:T(8,128)(2,1)}, bf16[4,64,2048]{2,1,0:T(8,128)(2,1)}, bf16[4,64,2048]{2,1,0:T(8,128)(2,1)}) custom-call(s32[2]{0:T(128)} %pad_add_fusion.place_ref, f32[16,128,8]{2,1,0:T(8,128)S(1)} %get-tuple-element.44.factors, ...), custom_call_target="tpu_custom_call", output_to_operand_aliasing={{0}: (6, {}), {1}: (7, {}), {2}: (8, {})} | custom-call | flops 40000000 | bytes 1600000 | tf_op jit(solution)/shard_map/pallas_call | solution.py:178
  91.8 2.1 %shard_map.111 = (bf16[4,64,2048]{2,1,0:T(8,128)(2,1)}, bf16[4,64,2048]{2,1,0:T(8,128)(2,1)}, bf16[4,64,2048]{2,1,0:T(8,128)(2,1)}) custom-call(s32[2]{0:T(128)} %pad_add_fusion.place_ref, f32[16,128,8]{2,1,0:T(8,128)S(1)} %get-tuple-element.44.factors, ...), custom_call_target="tpu_custom_call", output_to_operand_aliasing={{0}: (4, {}), {1}: (5, {}), {2}: (6, {})} | custom-call | flops 20000000 | bytes 800000 | tf_op jit(solution)/shard_map/pallas_call | solution.py:178
  94.0 1.7 %reshape.17 = bf16[64,2048]{1,0:T(8,128)(2,1)} reshape(bf16[16,4,2048]{2,1,0:T(4,128)(2,1)} %all-to-all-done.1) | data formatting | bytes 524288 | tf_op jit(solution)/shard_map/reshape | solution.py:255
  (53 shorter events, 13.7 us)
Async XLA Ops:
  4.8 30.4 %collective-permute-start.11 = (bf16[12,64,128]{2,1,0:T(8,128)(2,1)}, bf16[12,64,128]{2,1,0:T(8,128)(2,1)S(1)}, u32[]{:S(2)}, u32[]{:S(2)}) collective-permute-start(bf16[12,64,128]{2,1,0:T(8,128)(2,1)} %get-tuple-element.57), channel_id=1, source_target_pairs={{0,6},{1,7},{2,8},{3,9},{4,10},{5,11},{6,12},{7,13},{8,14},{9,15},... | collective-permute-start | bytes 589832 | tf_op jit(solution)/shard_map/ppermute | solution.py:239
  10.0 31.1 %collective-permute-start.12 = (bf16[12,64,128]{2,1,0:T(8,128)(2,1)}, bf16[12,64,128]{2,1,0:T(8,128)(2,1)S(1)}, u32[]{:S(2)}, u32[]{:S(2)}) collective-permute-start(bf16[12,64,128]{2,1,0:T(8,128)(2,1)} %get-tuple-element.58), channel_id=1, source_target_pairs={{0,10},{1,11},{2,12},{3,13},{4,14},{5,15},{6,0},{7,1},{8,2},{9,3},... | collective-permute-start | bytes 589832 | tf_op jit(solution)/shard_map/ppermute | solution.py:239
  12.2 30.0 %collective-permute-start.13 = (bf16[12,64,128]{2,1,0:T(8,128)(2,1)S(1)}, bf16[12,64,128]{2,1,0:T(8,128)(2,1)S(1)}, u32[]{:S(2)}, u32[]{:S(2)}) collective-permute-start(bf16[12,64,128]{2,1,0:T(8,128)(2,1)S(1)} %get-tuple-element.59), channel_id=1, source_target_pairs={{0,7},{1,6},{2,9},{3,8},{4,11},{5,10},{6,13},{7,12},{8,15},{9,14},... | collective-permute-start | bytes 589832 | tf_op jit(solution)/shard_map/ppermute | solution.py:239
  14.6 30.8 %collective-permute-start.14 = (bf16[12,64,128]{2,1,0:T(8,128)(2,1)S(1)}, bf16[12,64,128]{2,1,0:T(8,128)(2,1)S(1)}, u32[]{:S(2)}, u32[]{:S(2)}) collective-permute-start(bf16[12,64,128]{2,1,0:T(8,128)(2,1)S(1)} %get-tuple-element.60), channel_id=1, source_target_pairs={{0,11},{1,10},{2,13},{3,12},{4,15},{5,14},{6,1},{7,0},{8,3},{9,2},... | collective-permute-start | bytes 589832 | tf_op jit(solution)/shard_map/ppermute | solution.py:239
  27.1 20.5 %collective-permute-start.2 = (bf16[12,64,128]{2,1,0:T(8,128)(2,1)S(1)}, bf16[12,64,128]{2,1,0:T(8,128)(2,1)S(1)}, u32[]{:S(2)}, u32[]{:S(2)}) collective-permute-start(bf16[12,64,128]{2,1,0:T(8,128)(2,1)S(1)} %get-tuple-element.47), channel_id=1, source_target_pairs={{0,5},{1,4},{2,7},{3,6},{4,9},{5,8},{6,11},{7,10},{8,13},{9,12},{1... | collective-permute-start | bytes 589832 | tf_op jit(solution)/shard_map/ppermute | solution.py:239
  28.4 23.2 %all-to-all-start = ((f32[16,1,1280]{2,1,0:T(1,128)}), f32[16,1,1280]{2,1,0:T(1,128)S(1)}, u32[]{:S(2)}, u32[]{:S(2)}) async-start(f32[16,1,1280]{2,1,0:T(1,128)} %get-tuple-element.43), calls=%async_computation | async-start | bytes 163840 | tf_op jit(solution)/shard_map/all_to_all | solution.py:240
  35.2 0.7 copy-start
  35.9 25.1 %collective-permute-start.6 = (bf16[12,64,128]{2,1,0:T(8,128)(2,1)S(1)}, bf16[12,64,128]{2,1,0:T(8,128)(2,1)S(1)}, u32[]{:S(2)}, u32[]{:S(2)}) collective-permute-start(bf16[12,64,128]{2,1,0:T(8,128)(2,1)S(1)} %get-tuple-element.51), channel_id=1, source_target_pairs={{0,8},{1,9},{2,10},{3,11},{4,12},{5,13},{6,14},{7,15},{8,0},{9,1},... | collective-permute-start | bytes 589832 | tf_op jit(solution)/shard_map/ppermute | solution.py:239
  41.8 28.2 %collective-permute-start.7 = (bf16[12,64,128]{2,1,0:T(8,128)(2,1)S(1)}, bf16[12,64,128]{2,1,0:T(8,128)(2,1)S(1)}, u32[]{:S(2)}, u32[]{:S(2)}) collective-permute-start(bf16[12,64,128]{2,1,0:T(8,128)(2,1)S(1)} %get-tuple-element.52), channel_id=1, source_target_pairs={{0,9},{1,8},{2,11},{3,10},{4,13},{5,12},{6,15},{7,14},{8,1},{9,0},... | collective-permute-start | bytes 589832 | tf_op jit(solution)/shard_map/ppermute | solution.py:239
  42.9 30.6 %collective-permute-start.8 = (bf16[12,64,128]{2,1,0:T(8,128)(2,1)}, bf16[12,64,128]{2,1,0:T(8,128)(2,1)S(1)}, u32[]{:S(2)}, u32[]{:S(2)}) collective-permute-start(bf16[12,64,128]{2,1,0:T(8,128)(2,1)} %get-tuple-element.53), channel_id=1, source_target_pairs={{0,4},{1,5},{2,6},{3,7},{4,8},{5,9},{6,10},{7,11},{8,12},{9,13},{1... | collective-permute-start | bytes 589832 | tf_op jit(solution)/shard_map/ppermute | solution.py:239
  46.1 27.4 %collective-permute-start.9 = (bf16[12,64,128]{2,1,0:T(8,128)(2,1)}, bf16[12,64,128]{2,1,0:T(8,128)(2,1)S(1)}, u32[]{:S(2)}, u32[]{:S(2)}) collective-permute-start(bf16[12,64,128]{2,1,0:T(8,128)(2,1)} %get-tuple-element.54), channel_id=1, source_target_pairs={{0,12},{1,13},{2,14},{3,15},{4,0},{5,1},{6,2},{7,3},{8,4},{9,5},{1... | collective-permute-start | bytes 589832 | tf_op jit(solution)/shard_map/ppermute | solution.py:239
  47.6 28.5 %collective-permute-start.10 = (bf16[12,64,128]{2,1,0:T(8,128)(2,1)}, bf16[12,64,128]{2,1,0:T(8,128)(2,1)S(1)}, u32[]{:S(2)}, u32[]{:S(2)}) collective-permute-start(bf16[12,64,128]{2,1,0:T(8,128)(2,1)} %get-tuple-element.56), channel_id=1, source_target_pairs={{0,1},{1,0},{2,3},{3,2},{4,5},{5,4},{6,7},{7,6},{8,9},{9,8},{10,11... | collective-permute-start | bytes 589832 | tf_op jit(solution)/shard_map/ppermute | solution.py:239
  54.2 39.7 %all-to-all-start.1 = ((bf16[16,4,2048]{2,1,0:T(4,128)(2,1)}), bf16[16,4,2048]{2,1,0:T(4,128)(2,1)}, u32[]{:S(2)}, u32[]{:S(2)}) async-start(bf16[16,4,2048]{2,1,0:T(4,128)(2,1)} %get-tuple-element.76), calls=%async_computation.1 | async-start | bytes 524288 | tf_op jit(solution)/shard_map/all_to_all | solution.py:254
  61.0 28.2 %collective-permute-start.3 = (bf16[12,64,128]{2,1,0:T(8,128)(2,1)}, bf16[12,64,128]{2,1,0:T(8,128)(2,1)S(1)}, u32[]{:S(2)}, u32[]{:S(2)}) collective-permute-start(bf16[12,64,128]{2,1,0:T(8,128)(2,1)} %get-tuple-element.48), channel_id=1, source_target_pairs={{0,13},{1,12},{2,15},{3,14},{4,1},{5,0},{6,3},{7,2},{8,5},{9,4},{1... | collective-permute-start | bytes 589832 | tf_op jit(solution)/shard_map/ppermute | solution.py:239
  70.0 19.2 %collective-permute-start.4 = (bf16[12,64,128]{2,1,0:T(8,128)(2,1)}, bf16[12,64,128]{2,1,0:T(8,128)(2,1)}, u32[]{:S(2)}, u32[]{:S(2)}) collective-permute-start(bf16[12,64,128]{2,1,0:T(8,128)(2,1)} %copy-done.15), channel_id=1, source_target_pairs={{0,2},{1,3},{2,4},{3,5},{4,6},{5,7},{6,8},{7,9},{8,10},{9,11},{10,... | collective-permute-start | bytes 589832 | tf_op jit(solution)/shard_map/ppermute | solution.py:239
  73.5 15.7 %collective-permute-start.5 = (bf16[12,64,128]{2,1,0:T(8,128)(2,1)}, bf16[12,64,128]{2,1,0:T(8,128)(2,1)}, u32[]{:S(2)}, u32[]{:S(2)}) collective-permute-start(bf16[12,64,128]{2,1,0:T(8,128)(2,1)} %copy-done.14), channel_id=1, source_target_pairs={{0,14},{1,15},{2,0},{3,1},{4,2},{5,3},{6,4},{7,5},{8,6},{9,7},{10,... | collective-permute-start | bytes 589832 | tf_op jit(solution)/shard_map/ppermute | solution.py:239
  73.5 18.3 %collective-permute-start = (bf16[12,64,128]{2,1,0:T(8,128)(2,1)}, bf16[12,64,128]{2,1,0:T(8,128)(2,1)}, u32[]{:S(2)}, u32[]{:S(2)}) collective-permute-start(bf16[12,64,128]{2,1,0:T(8,128)(2,1)} %copy-done.13), channel_id=1, source_target_pairs={{0,3},{1,2},{2,5},{3,4},{4,7},{5,6},{6,9},{7,8},{8,11},{9,10},{10,... | collective-permute-start | bytes 589832 | tf_op jit(solution)/shard_map/ppermute | solution.py:239
  76.8 15.1 %collective-permute-start.1 = (bf16[12,64,128]{2,1,0:T(8,128)(2,1)}, bf16[12,64,128]{2,1,0:T(8,128)(2,1)}, u32[]{:S(2)}, u32[]{:S(2)}) collective-permute-start(bf16[12,64,128]{2,1,0:T(8,128)(2,1)} %copy-done.12), channel_id=1, source_target_pairs={{0,15},{1,14},{2,1},{3,0},{4,3},{5,2},{6,5},{7,4},{8,7},{9,6},{10,... | collective-permute-start | bytes 589832 | tf_op jit(solution)/shard_map/ppermute | solution.py:239
  78.8 0.9 copy-start.1
  79.8 0.9 copy-start.3
  80.7 0.9 copy-start.5
  81.6 0.9 copy-start.7
  82.6 0.9 copy-start.9
  83.5 0.9 copy-start.11
  (10 other events, 6.7 us)

commit v3 on v2

v3 whole, which is shorter than its diff:
```python
import functools

import jax
import jax.numpy as jnp
from jax import lax
from jax.experimental import pallas as pl
from jax.experimental.pallas import tpu as pltpu
from jax.sharding import PartitionSpec as P


D_MODEL = 2048
E = 4
N = 3 * E
CHIPS = 8
POWER = 13
AMP = 700.0
FLOOR = 1e-25

UNROLL = 2
MiB = 1 << 20
FIRST = (3, -3)
REST = (1, -1, 2, -2, 4, 0)
ORDER = (
    (3, 0), (-3, 0), (3, 1), (-3, 1), (0, 1), (4, 0), (4, 1), (2, 0), (-2, 0),
    (2, 1), (-2, 1), (1, 0), (-1, 0), (1, 1), (-1, 1),
)


def place():
    r = lax.axis_index("rows")
    return lax.shift_right_logical(r, 1), lax.bitwise_and(r, 1)


def pairs_of(dz, dc):
    return [
        (2 * z + c, 2 * ((z + dz) % CHIPS) + (c ^ dc)) for z in range(CHIPS) for c in range(2)
    ]


def code(x, sums):
    v = x * (AMP / jnp.maximum(sums, FLOOR))
    v2 = v * v
    v4 = v2 * v2
    return (v4 * v4 * v4 * v).astype(jnp.bfloat16)


def fetches(dzs, z, ins, buf, sems):
    gate, up, down = ins
    out = []
    for i, dz in enumerate(dzs):
        at = pl.ds(pl.multiple_of(lax.rem(z + (dz % CHIPS), CHIPS) * 128, 128), 128)
        out.append(
            [
                pltpu.make_async_copy(gate.at[:, :, at], buf.at[i, 0], sems.at[i, 0]),
                pltpu.make_async_copy(up.at[:, :, at], buf.at[i, 1], sems.at[i, 1]),
                pltpu.make_async_copy(down.at[:, at, :], buf.at[i, 2], sems.at[i, 2]),
            ]
        )
    return out


def encode(dzs, ins, outs, buf, sems):
    z, c = place()
    copies = fetches(dzs, z, ins, buf, sems)
    for three in copies:
        for copy in three:
            copy.start()
    mine = c == 0
    for i, three in enumerate(copies):
        same, other = outs[2 * i], outs[2 * i + 1]
        for copy in three:
            copy.wait()

        def put(n, coded):
            low, high = coded[:64], coded[64:]
            same[n] = jnp.where(mine, low, high)
            other[n] = jnp.where(mine, high, low)

        def one(e, carry):
            for a in range(2):
                x = buf[i, a, e]
                put(a * E + e, code(x, jnp.sum(jnp.abs(x), axis=0, keepdims=True)).T)
            x = buf[i, 2, e]
            put(2 * E + e, code(x, jnp.sum(jnp.abs(x), axis=1, keepdims=True)))
            return carry

        lax.fori_loop(0, E, one, 0, unroll=UNROLL)


def code_kernel(dzs, gate, up, down, *rest):
    outs, (buf, sems) = rest[: 2 * len(dzs)], rest[2 * len(dzs) :]
    encode(dzs, (gate, up, down), outs, buf, sems)


def sums_kernel(gate, up, down, router, gain, table, buf, tall, line, sems):
    copies = []
    for a, ref in enumerate((gate, up)):
        copies += [pltpu.make_async_copy(ref.at[e], buf.at[a * E + e], sems.at[a * E + e]) for e in range(E)]
    copies += [pltpu.make_async_copy(down.at[e], tall.at[e], sems.at[2 * E + e]) for e in range(E)]
    for copy in copies:
        copy.start()
    diagonal = lax.broadcasted_iota(jnp.int32, (128, 128), 0) == lax.broadcasted_iota(
        jnp.int32, (128, 128), 1
    )
    left = lax.broadcasted_iota(jnp.int32, (8, 128), 1) < 64
    served = (router[...] * gain[...]).astype(jnp.bfloat16).astype(jnp.float32)
    for d in range(16):
        for q in range(4):
            at = slice((N // 2 + q) * 128, (N // 2 + q) * 128 + 128)
            table[d, :, at] = served[q : q + 1]
    for n in range(N):
        q, half = n // 2, n % 2
        copies[n].wait()
        if n < 2 * E:
            line[half, q : q + 1, :] = jnp.sum(jnp.abs(buf[n]), axis=0, keepdims=True)
            continue
        for chip in range(CHIPS):
            at = slice(chip * 128, chip * 128 + 128)
            total = jnp.sum(jnp.abs(tall[n - 2 * E, at]), axis=1, keepdims=True)
            total = jnp.sum(jnp.where(diagonal, total, 0.0), axis=0, keepdims=True)
            line[half, q : q + 1, at] = total
    for chip in range(CHIPS):
        at = slice(chip * 128, chip * 128 + 128)
        a, b = line[0, :, at], line[1, :, at]
        for core, both in enumerate(
            (jnp.where(left, a, pltpu.roll(b, 64, 1)), jnp.where(left, pltpu.roll(a, 64, 1), b))
        ):
            for q in range(N // 2):
                table[2 * chip + core, :, q * 128 : q * 128 + 128] = both[q : q + 1]


def scale_kernel(table, gate, up, down, factors, rows, line):
    total = table[0]
    for s in range(1, 16):
        total = total + table[s]
    scale = total[:, : N // 2 * 128] / D_MODEL
    for n in range(N):
        out = (gate, up, down)[n // E]
        out[n % E : n % E + 1, :] = scale[:, n * 64 : n * 64 + 64]
    for s in range(16):
        f = jnp.maximum(table[s, :, : N // 2 * 128], FLOOR) / (AMP * scale)
        f = [f[:, q * 128 : q * 128 + 128] for q in range(N // 2)]
        factors[s] = jnp.concatenate(f + f[:2], axis=0).T
        for q in range(4):
            at = slice((N // 2 + q) * 128, (N // 2 + q) * 128 + 128)
            line[q : q + 1, s * 128 : s * 128 + 128] = table[s, :, at].astype(jnp.bfloat16)
    for d in range(16):
        rows[d] = line[...]


def decode_kernel(where, n_alias, with_router, factors, *rest):
    n = len(where)
    pieces, rest = rest[:n], rest[n:]
    if with_router:
        wide, rest = rest[0], rest[1:]
    outs, rest = rest[n_alias : n_alias + 3], rest[n_alias + 3 :]
    if with_router:
        served, rest = rest[0], rest[1:]
        for p in range(16):
            served[4 * p : 4 * p + 4, :] = wide[p]
    buf, sems = rest
    z, c = place()
    copies = []
    for i, (dz, dc) in enumerate(where):
        s = 2 * lax.rem(z + (-dz % CHIPS), CHIPS) + (c if dc == 0 else 1 - c)
        f = factors[s]
        for k in range(N):
            w = pieces[i][k].astype(jnp.float32)
            root = jnp.exp(jnp.log(jnp.abs(w)) * (1.0 / POWER))
            root = jnp.where(w < 0, -root, root)
            half = k % 2 * 64
            buf[i, k] = (root * f[half : half + 64, k // 2 : k // 2 + 1]).astype(jnp.bfloat16)
        at = pl.ds(pl.multiple_of(s * 128, 128), 128)
        for a in range(3):
            copy = pltpu.make_async_copy(
                buf.at[i, a * E : a * E + E], outs[a].at[:, :, at], sems.at[i, a]
            )
            copy.start()
            copies.append(copy)
    for copy in copies:
        copy.wait()


VMEM = pl.BlockSpec(memory_space=pltpu.VMEM)
ANY = pl.BlockSpec(memory_space=pl.ANY)
HBM = pl.BlockSpec(memory_space=pltpu.HBM)
PIECE = pltpu.HBM((N, 64, 128), jnp.bfloat16)


def kept(x, where=pltpu.VMEM):
    return pltpu.with_memory_space_constraint(x, where)


def decode(where, factors, pieces, before, wide=None):
    n = len(where)
    out = jax.ShapeDtypeStruct((E, 64, 16 * 128), jnp.bfloat16)
    extra = [] if wide is None else [kept(wide)]
    return pl.pallas_call(
        functools.partial(decode_kernel, where, len(before), wide is not None),
        out_shape=(out,) * 3 + (jax.ShapeDtypeStruct((64, D_MODEL), jnp.bfloat16),) * len(extra),
        in_specs=[VMEM] * (1 + n + len(extra)) + [ANY] * len(before),
        out_specs=(ANY,) * 3 + (VMEM,) * len(extra),
        scratch_shapes=[
            pltpu.VMEM((n, N, 64, 128), jnp.bfloat16),
            pltpu.SemaphoreType.DMA((n, 3)),
        ],
        input_output_aliases={1 + n + len(extra) + a: a for a in range(len(before))},
        cost_estimate=pl.CostEstimate(
            flops=n * 10_000_000, transcendentals=0, bytes_accessed=n * 400_000
        ),
        compiler_params=pltpu.CompilerParams(vmem_limit_bytes=8 * MiB),
    )(kept(factors), *pieces, *extra, *before)


GROUPS = (
    ((0, 0), (0, 1), (3, 0), (-3, 0), (3, 1), (-3, 1)),
    ((4, 0), (4, 1), (2, 0), (-2, 0)),
    ((2, 1), (-2, 1), (1, 0), (-1, 0)),
    ((1, 1), (-1, 1)),
)


def local(train_gate, train_up, train_down, router_weight, router_gain):
    ins = (train_gate, train_up, train_down)
    sent = {}

    def coded(dzs, limit):
        pieces = pl.pallas_call(
            functools.partial(code_kernel, dzs),
            out_shape=(PIECE,) * (2 * len(dzs)),
            in_specs=[HBM, HBM, HBM],
            out_specs=(VMEM,) * (2 * len(dzs)),
            scratch_shapes=[
                pltpu.VMEM((len(dzs), 3, E, 128, 128), jnp.float32),
                pltpu.SemaphoreType.DMA((len(dzs), 3)),
            ],
            compiler_params=pltpu.CompilerParams(vmem_limit_bytes=limit),
        )(*(pltpu.with_memory_space_constraint(x, pltpu.HBM) for x in ins))
        for i, dz in enumerate(dzs):
            sent[dz, 0], sent[dz, 1] = pieces[2 * i], pieces[2 * i + 1]

    coded(FIRST, 6 * MiB)
    table = pl.pallas_call(
        sums_kernel,
        out_shape=pltpu.VMEM((16, 1, 1280), jnp.float32),
        in_specs=[HBM, HBM, HBM, VMEM, VMEM],
        out_specs=VMEM,
        scratch_shapes=[
            pltpu.VMEM((2 * E, 128, 1024), jnp.float32),
            pltpu.VMEM((E, 1024, 128), jnp.float32),
            pltpu.VMEM((2, 8, 1024), jnp.float32),
            pltpu.SemaphoreType.DMA((N,)),
        ],
        compiler_params=pltpu.CompilerParams(vmem_limit_bytes=12 * MiB),
        name="totals",
    )(*ins, router_weight.T, router_gain[None])
    coded(REST, 12 * MiB)
    got = {(0, 0): sent[0, 0]}
    for dz, dc in ORDER:
        got[dz, dc] = lax.ppermute(sent[dz, dc], "rows", pairs_of(dz, dc))
    table = lax.all_to_all(table, "rows", 0, 0, tiled=True)
    small = jax.ShapeDtypeStruct((E, 64), jnp.float32)
    scale_gate, scale_up, scale_down, factors, rows = pl.pallas_call(
        scale_kernel,
        out_shape=(small,) * 3
        + (
            pltpu.VMEM((16, 128, 8), jnp.float32),
            pltpu.VMEM((16, 4, D_MODEL), jnp.bfloat16),
        ),
        in_specs=[VMEM],
        out_specs=(VMEM,) * 5,
        scratch_shapes=[pltpu.VMEM((4, D_MODEL), jnp.bfloat16)],
        compiler_params=pltpu.CompilerParams(vmem_limit_bytes=4 * MiB),
        name="scales",
    )(kept(table))
    wide = lax.all_to_all(rows, "owner", 0, 0, tiled=True)
    outs = ()
    for i, where in enumerate(GROUPS):
        pieces = [kept(got[k], pltpu.HBM if k == (0, 0) else pltpu.VMEM) for k in where]
        outs = decode(where, factors, pieces, outs, wide if i == 2 else None)
        if i == 2:
            *outs, served = outs
    serve_router = served.T
    ready_gate, ready_up, ready_down = outs
    return (
        ready_gate.transpose(0, 2, 1),
        ready_up.transpose(0, 2, 1),
        ready_down,
        scale_gate,
        scale_up,
        scale_down,
        serve_router,
    )


def solution(mesh):
    return jax.shard_map(
        local,
        mesh=mesh,
        in_specs=(
            P("owner", "rows", None),
            P("owner", "rows", None),
            P("owner", None, "rows"),
            P("rows", "owner"),
            P("rows"),
        ),
        out_specs=(
            P("owner", None, "rows"),
            P("owner", None, "rows"),
            P("owner", "rows", None),
            P("owner", "rows"),
            P("owner", "rows"),
            P("owner", "rows"),
            P(),
        ),
        check_vma=False,
    )
```

time: 96.3 us -> 89.5 us (0.929)
  local copies, waits for them, and re-layouts: 14.7 us -> 6.46 us
  waiting for transfers between devices: 7.36 us -> 9.56 us
  Pallas kernels: 21 us -> 18.8 us
  starting transfers between devices: 51.3 us -> 53.2 us
    unnamed x34 -> x32, local copies, waits for them, and re-layouts: 12.9 us -> 6.46 us
    ppermute x15, starting transfers between devices: 37.7 us -> 40.2 us  [local(): got[dz, dc] = lax.ppermute(sent[dz, dc], 'rows', pairs_of(dz, dc))]
    ppermute x15, waiting for transfers between devices: 3.77 us -> 5.57 us  [local(): got[dz, dc] = lax.ppermute(sent[dz, dc], 'rows', pairs_of(dz, dc))]
    reshape x1 -> x0, local copies, waits for them, and re-layouts: 1.72 us -> none  [local(): serve_router = wide.reshape(64, D_MODEL).T]
    pallas_call x6 -> x7, Pallas kernels: 19 us -> 17.7 us  [the longest x4 7.73 us: decode(): pl.pallas_call(functools.partial(decode_kernel, where, len(before), wide...]
  transfers between devices with their start and end apart: 17 -> 17, of which waited for: 3 -> 3; matrix products, arithmetic and copies ran while one was open for 0% -> 0% of each run, Pallas kernels for 18% -> 17%
where the time goes in v3:
time: 89.5 us; the launch traced here: 89.1 us
  starting transfers between devices  53.2 us (59%)
  Pallas kernels  18.8 us (21%)
  waiting for transfers between devices  9.56 us (11%)
  local copies, waits for them, and re-layouts  6.46 us (7%)
  between operations  0.98 us (1%)
    ppermute x15, starting transfers between devices, local(): got[dz, dc] = lax.ppermute(sent[dz, dc], 'rows', pairs_of(dz, dc))  40.2 us
    pallas_call x4, Pallas kernels, decode(): pl.pallas_call(functools.partial(decode_kernel, where, len(before), wide...  7.73 us
    pallas_call x2, Pallas kernels, coded(): pl.pallas_call(functools.partial(code_kernel, dzs), out_shape=(PIECE,) *...  7.4 us
    all_to_all x1, starting transfers between devices, local(): wide = lax.all_to_all(rows, 'owner', 0, 0, tiled=True)  6.75 us
    unnamed x32, local copies, waits for them, and re-layouts  6.46 us
    all_to_all x1, starting transfers between devices, local(): table = lax.all_to_all(table, 'rows', 0, 0, tiled=True)  6.31 us
    ppermute x15, waiting for transfers between devices, local(): got[dz, dc] = lax.ppermute(sent[dz, dc], 'rows', pairs_of(dz, dc))  5.57 us
    all_to_all x1, waiting for transfers between devices, local(): table = lax.all_to_all(table, 'rows', 0, 0, tiled=True)  3.99 us
  transfers between devices with their start and end apart: 17, of which 3 were waited for; matrix products, arithmetic and copies ran while one was open for 0% of the time, Pallas kernels for 17%

profile of v3, /device:TPU:1, one launch (start us, length us, event | category | flops | bytes accessed | tf_op | source)
XLA Modules:
  0.0 89.1 jit_solution(2798731002735346986)
XLA Ops:
  0.6 2.7 %shard_map.109 = (bf16[12,64,128]{2,1,0:T(8,128)(2,1)}, bf16[12,64,128]{2,1,0:T(8,128)(2,1)}, bf16[12,64,128]{2,1,0:T(8,128)(2,1)}, bf16[12,64,128]{2,1,0:T(8,128)(2,1)}) custom-call(f32[4,128,1024]{2,1,0:T(8,128)} %gate.5, f32[4,128,1024]{2,1,0:T(8,128)} %up.5, f32[4,1024,128]{2,1,0:T(8,128)} %down.5), custom_call_target="tpu_custom_call" | custom-call | tf_op jit(solution)/shard_map/pallas_call | solution.py:228
  3.3 5.2 %collective-permute-start.11 = (bf16[12,64,128]{2,1,0:T(8,128)(2,1)}, bf16[12,64,128]{2,1,0:T(8,128)(2,1)S(1)}, u32[]{:S(2)}, u32[]{:S(2)}) collective-permute-start(bf16[12,64,128]{2,1,0:T(8,128)(2,1)} %get-tuple-element.55), channel_id=1, source_target_pairs={{0,6},{1,7},{2,8},{3,9},{4,10},{5,11},{6,12},{7,13},{8,14},{9,15},... | collective-permute-start | bytes 589832 | tf_op jit(solution)/shard_map/ppermute | solution.py:260
  8.5 2.2 %collective-permute-start.12 = (bf16[12,64,128]{2,1,0:T(8,128)(2,1)}, bf16[12,64,128]{2,1,0:T(8,128)(2,1)S(1)}, u32[]{:S(2)}, u32[]{:S(2)}) collective-permute-start(bf16[12,64,128]{2,1,0:T(8,128)(2,1)} %get-tuple-element.56), channel_id=1, source_target_pairs={{0,10},{1,11},{2,12},{3,13},{4,14},{5,15},{6,0},{7,1},{8,2},{9,3},... | collective-permute-start | bytes 589832 | tf_op jit(solution)/shard_map/ppermute | solution.py:260
  10.8 2.4 %collective-permute-start.13 = (bf16[12,64,128]{2,1,0:T(8,128)(2,1)}, bf16[12,64,128]{2,1,0:T(8,128)(2,1)S(1)}, u32[]{:S(2)}, u32[]{:S(2)}) collective-permute-start(bf16[12,64,128]{2,1,0:T(8,128)(2,1)} %get-tuple-element.57), channel_id=1, source_target_pairs={{0,7},{1,6},{2,9},{3,8},{4,11},{5,10},{6,13},{7,12},{8,15},{9,14},... | collective-permute-start | bytes 589832 | tf_op jit(solution)/shard_map/ppermute | solution.py:260
  13.2 3.2 %collective-permute-start.14 = (bf16[12,64,128]{2,1,0:T(8,128)(2,1)}, bf16[12,64,128]{2,1,0:T(8,128)(2,1)S(1)}, u32[]{:S(2)}, u32[]{:S(2)}) collective-permute-start(bf16[12,64,128]{2,1,0:T(8,128)(2,1)} %get-tuple-element.58), channel_id=1, source_target_pairs={{0,11},{1,10},{2,13},{3,12},{4,15},{5,14},{6,1},{7,0},{8,3},{9,2},... | collective-permute-start | bytes 589832 | tf_op jit(solution)/shard_map/ppermute | solution.py:260
  16.4 4.7 %shard_map.108 = (bf16[12,64,128]{2,1,0:T(8,128)(2,1)}, bf16[12,64,128]{2,1,0:T(8,128)(2,1)}, bf16[12,64,128]{2,1,0:T(8,128)(2,1)}, bf16[12,64,128]{2,1,0:T(8,12...) custom-call(f32[4,128,1024]{2,1,0:T(8,128)} %gate.5, ...), custom_call_target="tpu_custom_call" | custom-call | tf_op jit(solution)/shard_map/pallas_call | solution.py:228
  21.1 1.8 %collective-permute-start.2 = (bf16[12,64,128]{2,1,0:T(8,128)(2,1)}, bf16[12,64,128]{2,1,0:T(8,128)(2,1)S(1)}, u32[]{:S(2)}, u32[]{:S(2)}) collective-permute-start(bf16[12,64,128]{2,1,0:T(8,128)(2,1)} %get-tuple-element.44), channel_id=1, source_target_pairs={{0,5},{1,4},{2,7},{3,6},{4,9},{5,8},{6,11},{7,10},{8,13},{9,12},{1... | collective-permute-start | bytes 589832 | tf_op jit(solution)/shard_map/ppermute | solution.py:260
  23.0 2.6 %totals.1 = f32[16,1,1280]{2,1,0:T(1,128)} custom-call(f32[4,128,1024]{2,1,0:T(8,128)S(1)} %copy-done, f32[4,128,1024]{2,1,0:T(8,128)S(1)} %copy-done.1, f32[4,1024,128]{2,1,0:T(8,128)S(1)} %copy-done.2, f32[4,128]{1,0:T(4,128)S(1)} %bitcast.5, f32[1,128]{1,0:T(1,128)S(1)} %bitcast.6), custom_call_target="tpu_custom_call" | custom-call | tf_op jit(solution)/shard_map/totals/pallas_call | solution.py:243
  25.6 6.3 %all-to-all-start = ((f32[16,1,1280]{2,1,0:T(1,128)}), f32[16,1,1280]{2,1,0:T(1,128)S(1)}, u32[]{:S(2)}, u32[]{:S(2)}) async-start(f32[16,1,1280]{2,1,0:T(1,128)} %totals.1), calls=%async_computation | async-start | bytes 163840 | tf_op jit(solution)/shard_map/all_to_all | solution.py:261
  32.0 5.3 %collective-permute-start.6 = (bf16[12,64,128]{2,1,0:T(8,128)(2,1)}, bf16[12,64,128]{2,1,0:T(8,128)(2,1)S(1)}, u32[]{:S(2)}, u32[]{:S(2)}) collective-permute-start(bf16[12,64,128]{2,1,0:T(8,128)(2,1)} %get-tuple-element.49), channel_id=1, source_target_pairs={{0,8},{1,9},{2,10},{3,11},{4,12},{5,13},{6,14},{7,15},{8,0},{9,1},... | collective-permute-start | bytes 589832 | tf_op jit(solution)/shard_map/ppermute | solution.py:260
  39.1 2.5 %collective-permute-start.8 = (bf16[12,64,128]{2,1,0:T(8,128)(2,1)S(1)}, bf16[12,64,128]{2,1,0:T(8,128)(2,1)S(1)}, u32[]{:S(2)}, u32[]{:S(2)}) collective-permute-start(bf16[12,64,128]{2,1,0:T(8,128)(2,1)S(1)} %copy-done.14), channel_id=1, source_target_pairs={{0,4},{1,5},{2,6},{3,7},{4,8},{5,9},{6,10},{7,11},{8,12},{9,13},{1... | collective-permute-start | bytes 589832 | tf_op jit(solution)/shard_map/ppermute | solution.py:260
  42.3 1.8 %collective-permute-start.9 = (bf16[12,64,128]{2,1,0:T(8,128)(2,1)S(1)}, bf16[12,64,128]{2,1,0:T(8,128)(2,1)S(1)}, u32[]{:S(2)}, u32[]{:S(2)}) collective-permute-start(bf16[12,64,128]{2,1,0:T(8,128)(2,1)S(1)} %copy-done.13), channel_id=1, source_target_pairs={{0,12},{1,13},{2,14},{3,15},{4,0},{5,1},{6,2},{7,3},{8,4},{9,5},{1... | collective-permute-start | bytes 589832 | tf_op jit(solution)/shard_map/ppermute | solution.py:260
  44.1 2.1 %collective-permute-done.2.rest_0_ = bf16[12,64,128]{2,1,0:T(8,128)(2,1)S(1)} collective-permute-done((bf16[12,64,128]{2,1,0:T(8,128)(2,1)}, bf16[12,64,128]{2,1,0:T(8,128)(2,1)S(1)}, u32[]{:S(2)}, u32[]{:S(2)}) %collective-permute-start.2) | collective-permute-done | bytes 196640 | tf_op jit(solution)/shard_map/ppermute | solution.py:260
  46.2 4.0 %all-to-all-done.table = f32[16,1,1280]{2,1,0:T(1,128)S(1)} async-done(((f32[16,1,1280]{2,1,0:T(1,128)}), f32[16,1,1280]{2,1,0:T(1,128)S(1)}, u32[]{:S(2)}, u32[]{:S(2)}) %all-to-all-start) | async-done | bytes 81952 | tf_op jit(solution)/shard_map/all_to_all | solution.py:261
  50.2 1.1 %scales.1 = (f32[4,64]{1,0:T(4,128)}, f32[4,64]{1,0:T(4,128)}, f32[4,64]{1,0:T(4,128)}, f32[16,128,8]{2,1,0:T(8,128)S(1)}, bf16[16,4,2048]{2,1,0:T(4,128)(2,1)}) custom-call(f32[16,1,1280]{2,1,0:T(1,128)S(1)} %all-to-all-done.table), custom_call_target="tpu_custom_call" | custom-call | tf_op jit(solution)/shard_map/scales/pallas_call | solution.py:263
  51.2 6.8 %all-to-all-start.1 = ((bf16[16,4,2048]{2,1,0:T(4,128)(2,1)}), bf16[16,4,2048]{2,1,0:T(4,128)(2,1)S(1)}, u32[]{:S(2)}, u32[]{:S(2)}) async-start(bf16[16,4,2048]{2,1,0:T(4,128)(2,1)} %get-tuple-element.48), calls=%async_computation.1 | async-start | bytes 524288 | tf_op jit(solution)/shard_map/all_to_all | solution.py:276
  58.0 10.5 %collective-permute-start.3 = (bf16[12,64,128]{2,1,0:T(8,128)(2,1)}, bf16[12,64,128]{2,1,0:T(8,128)(2,1)S(1)}, u32[]{:S(2)}, u32[]{:S(2)}) collective-permute-start(bf16[12,64,128]{2,1,0:T(8,128)(2,1)} %get-tuple-element.45), channel_id=1, source_target_pairs={{0,13},{1,12},{2,15},{3,14},{4,1},{5,0},{6,3},{7,2},{8,5},{9,4},{1... | collective-permute-start | bytes 589832 | tf_op jit(solution)/shard_map/ppermute | solution.py:260
  68.6 3.5 %collective-permute-done.8.rest_2_ = bf16[12,64,128]{2,1,0:T(8,128)(2,1)S(1)} collective-permute-done((bf16[12,64,128]{2,1,0:T(8,128)(2,1)S(1)}, bf16[12,64,128]{2,1,0:T(8,128)(2,1)S(1)}, u32[]{:S(2)}, u32[]{:S(2)}) %collective-permute-start.8) | collective-permute-done | bytes 196640 | tf_op jit(solution)/shard_map/ppermute | solution.py:260
  72.0 2.6 %collective-permute-start = (bf16[12,64,128]{2,1,0:T(8,128)(2,1)}, bf16[12,64,128]{2,1,0:T(8,128)(2,1)S(1)}, u32[]{:S(2)}, u32[]{:S(2)}) collective-permute-start(bf16[12,64,128]{2,1,0:T(8,128)(2,1)} %get-tuple-element.42), channel_id=1, source_target_pairs={{0,3},{1,2},{2,5},{3,4},{4,7},{5,6},{6,9},{7,8},{8,11},{9,10},{10,... | collective-permute-start | bytes 589832 | tf_op jit(solution)/shard_map/ppermute | solution.py:260
  75.3 2.1 %collective-permute-start.1 = (bf16[12,64,128]{2,1,0:T(8,128)(2,1)}, bf16[12,64,128]{2,1,0:T(8,128)(2,1)S(1)}, u32[]{:S(2)}, u32[]{:S(2)}) collective-permute-start(bf16[12,64,128]{2,1,0:T(8,128)(2,1)} %get-tuple-element.43), channel_id=1, source_target_pairs={{0,15},{1,14},{2,1},{3,0},{4,3},{5,2},{6,5},{7,4},{8,7},{9,6},{10,... | collective-permute-start | bytes 589832 | tf_op jit(solution)/shard_map/ppermute | solution.py:260
  81.1 2.9 %shard_map.110 = (bf16[4,64,2048]{2,1,0:T(8,128)(2,1)}, bf16[4,64,2048]{2,1,0:T(8,128)(2,1)}, bf16[4,64,2048]{2,1,0:T(8,128)(2,1)}) custom-call(f32[16,128,8]{2,1,0:T(8,128)S(1)} %get-tuple-element.41.factors, bf16[12,64,128]{2,1,0:T(8,128)(2,1)} %get-tuple-element.53.rest_0_, bf16[12,64,128]{2,1,0:T(8,128)(2,1)S(1)} %copy-done.10, ...), custom_call_target="tpu_custom_call" | custom-call | flops 60000000 | bytes 2400000 | tf_op jit(solution)/shard_map/pallas_call | solution.py:198
  84.0 1.5 %shard_map.111 = (bf16[4,64,2048]{2,1,0:T(8,128)(2,1)}, bf16[4,64,2048]{2,1,0:T(8,128)(2,1)}, bf16[4,64,2048]{2,1,0:T(8,128)(2,1)}) custom-call(f32[16,128,8]{2,1,0:T(8,128)S(1)} %get-tuple-element.41.factors, bf16[12,64,128]{2,1,0:T(8,128)(2,1)S(1)} %collective-permute-done.6.rest_0_, ...), custom_call_target="tpu_custom_call", output_to_operand_aliasing={{0}: (5, {}), {1}: (6, {}), {2}: (7, {})} | custom-call | flops 40000000 | bytes 1600000 | tf_op jit(solution)/shard_map/pallas_call | solution.py:198
  85.5 2.3 %shard_map.112 = (bf16[4,64,2048]{2,1,0:T(8,128)(2,1)}, bf16[4,64,2048]{2,1,0:T(8,128)(2,1)}, bf16[4,64,2048]{2,1,0:T(8,128)(2,1)}, bf16[64,2048]{1,0:T(8,128)(2,1)}) custom-call(f32[16,128,8]{2,1,0:T(8,128)S(1)} %get-tuple-element.41.factors, ...), custom_call_target="tpu_custom_call", output_to_operand_aliasing={{0}: (6, {}), {1}: (7, {}), {2}: (8, {})} | custom-call | flops 40000000 | bytes 1600000 | tf_op jit(solution)/shard_map/pallas_call | solution.py:198
  87.8 1.1 %shard_map.113 = (bf16[4,64,2048]{2,1,0:T(8,128)(2,1)}, bf16[4,64,2048]{2,1,0:T(8,128)(2,1)}, bf16[4,64,2048]{2,1,0:T(8,128)(2,1)}) custom-call(f32[16,128,8]{2,1,0:T(8,128)S(1)} %get-tuple-element.41.factors, bf16[12,64,128]{2,1,0:T(8,128)(2,1)S(1)} %collective-permute-done.rest_0_, ...), custom_call_target="tpu_custom_call", output_to_operand_aliasing={{0}: (3, {}), {1}: (4, {}), {2}: (5, {})} | custom-call | flops 20000000 | bytes 800000 | tf_op jit(solution)/shard_map/pallas_call | solution.py:198
  (50 shorter events, 6.9 us)
Async XLA Ops:
  3.3 28.6 %collective-permute-start.11 = (bf16[12,64,128]{2,1,0:T(8,128)(2,1)}, bf16[12,64,128]{2,1,0:T(8,128)(2,1)S(1)}, u32[]{:S(2)}, u32[]{:S(2)}) collective-permute-start(bf16[12,64,128]{2,1,0:T(8,128)(2,1)} %get-tuple-element.55), channel_id=1, source_target_pairs={{0,6},{1,7},{2,8},{3,9},{4,10},{5,11},{6,12},{7,13},{8,14},{9,15},... | collective-permute-start | bytes 589832 | tf_op jit(solution)/shard_map/ppermute | solution.py:260
  8.5 28.8 %collective-permute-start.12 = (bf16[12,64,128]{2,1,0:T(8,128)(2,1)}, bf16[12,64,128]{2,1,0:T(8,128)(2,1)S(1)}, u32[]{:S(2)}, u32[]{:S(2)}) collective-permute-start(bf16[12,64,128]{2,1,0:T(8,128)(2,1)} %get-tuple-element.56), channel_id=1, source_target_pairs={{0,10},{1,11},{2,12},{3,13},{4,14},{5,15},{6,0},{7,1},{8,2},{9,3},... | collective-permute-start | bytes 589832 | tf_op jit(solution)/shard_map/ppermute | solution.py:260
  10.8 27.6 %collective-permute-start.13 = (bf16[12,64,128]{2,1,0:T(8,128)(2,1)}, bf16[12,64,128]{2,1,0:T(8,128)(2,1)S(1)}, u32[]{:S(2)}, u32[]{:S(2)}) collective-permute-start(bf16[12,64,128]{2,1,0:T(8,128)(2,1)} %get-tuple-element.57), channel_id=1, source_target_pairs={{0,7},{1,6},{2,9},{3,8},{4,11},{5,10},{6,13},{7,12},{8,15},{9,14},... | collective-permute-start | bytes 589832 | tf_op jit(solution)/shard_map/ppermute | solution.py:260
  13.2 9.8 %copy-start.1 = (f32[4,128,1024]{2,1,0:T(8,128)S(1)}, f32[4,128,1024]{2,1,0:T(8,128)}, u32[]{:S(2)}) copy-start(f32[4,128,1024]{2,1,0:T(8,128)} %up.5) | copy-start | bytes 6291460
  13.2 9.8 %copy-start.2 = (f32[4,1024,128]{2,1,0:T(8,128)S(1)}, f32[4,1024,128]{2,1,0:T(8,128)}, u32[]{:S(2)}) copy-start(f32[4,1024,128]{2,1,0:T(8,128)} %down.5) | copy-start | bytes 6291460
  13.2 9.8 %copy-start.11 = (f32[128,4]{0,1:T(4,128)S(1)}, f32[128,4]{0,1:T(4,128)}, u32[]{:S(2)}) copy-start(f32[128,4]{0,1:T(4,128)} %param.8) | copy-start | bytes 6148
  13.2 9.8 %copy-start.12 = (f32[128]{0:T(128)S(1)}, f32[128]{0:T(128)}, u32[]{:S(2)}) copy-start(f32[128]{0:T(128)} %param.9) | copy-start | bytes 1540
  13.2 28.4 %collective-permute-start.14 = (bf16[12,64,128]{2,1,0:T(8,128)(2,1)}, bf16[12,64,128]{2,1,0:T(8,128)(2,1)S(1)}, u32[]{:S(2)}, u32[]{:S(2)}) collective-permute-start(bf16[12,64,128]{2,1,0:T(8,128)(2,1)} %get-tuple-element.58), channel_id=1, source_target_pairs={{0,11},{1,10},{2,13},{3,12},{4,15},{5,14},{6,1},{7,0},{8,3},{9,2},... | collective-permute-start | bytes 589832 | tf_op jit(solution)/shard_map/ppermute | solution.py:260
  21.1 25.0 %collective-permute-start.2 = (bf16[12,64,128]{2,1,0:T(8,128)(2,1)}, bf16[12,64,128]{2,1,0:T(8,128)(2,1)S(1)}, u32[]{:S(2)}, u32[]{:S(2)}) collective-permute-start(bf16[12,64,128]{2,1,0:T(8,128)(2,1)} %get-tuple-element.44), channel_id=1, source_target_pairs={{0,5},{1,4},{2,7},{3,6},{4,9},{5,8},{6,11},{7,10},{8,13},{9,12},{1... | collective-permute-start | bytes 589832 | tf_op jit(solution)/shard_map/ppermute | solution.py:260
  23.0 15.0 %copy-start.15 = (bf16[12,64,128]{2,1,0:T(8,128)(2,1)S(1)}, bf16[12,64,128]{2,1,0:T(8,128)(2,1)}, u32[]{:S(2)}) copy-start(bf16[12,64,128]{2,1,0:T(8,128)(2,1)} %get-tuple-element.50) | copy-start | bytes 589828
  23.0 16.1 %copy-start.14 = (bf16[12,64,128]{2,1,0:T(8,128)(2,1)S(1)}, bf16[12,64,128]{2,1,0:T(8,128)(2,1)}, u32[]{:S(2)}) copy-start(bf16[12,64,128]{2,1,0:T(8,128)(2,1)} %get-tuple-element.51) | copy-start | bytes 589828
  23.0 19.3 %copy-start.13 = (bf16[12,64,128]{2,1,0:T(8,128)(2,1)S(1)}, bf16[12,64,128]{2,1,0:T(8,128)(2,1)}, u32[]{:S(2)}) copy-start(bf16[12,64,128]{2,1,0:T(8,128)(2,1)} %get-tuple-element.52) | copy-start | bytes 589828
  25.6 24.5 %all-to-all-start = ((f32[16,1,1280]{2,1,0:T(1,128)}), f32[16,1,1280]{2,1,0:T(1,128)S(1)}, u32[]{:S(2)}, u32[]{:S(2)}) async-start(f32[16,1,1280]{2,1,0:T(1,128)} %totals.1), calls=%async_computation | async-start | bytes 163840 | tf_op jit(solution)/shard_map/all_to_all | solution.py:261
  32.0 26.1 %collective-permute-start.6 = (bf16[12,64,128]{2,1,0:T(8,128)(2,1)}, bf16[12,64,128]{2,1,0:T(8,128)(2,1)S(1)}, u32[]{:S(2)}, u32[]{:S(2)}) collective-permute-start(bf16[12,64,128]{2,1,0:T(8,128)(2,1)} %get-tuple-element.49), channel_id=1, source_target_pairs={{0,8},{1,9},{2,10},{3,11},{4,12},{5,13},{6,14},{7,15},{8,0},{9,1},... | collective-permute-start | bytes 589832 | tf_op jit(solution)/shard_map/ppermute | solution.py:260
  38.0 30.6 %collective-permute-start.7 = (bf16[12,64,128]{2,1,0:T(8,128)(2,1)S(1)}, bf16[12,64,128]{2,1,0:T(8,128)(2,1)S(1)}, u32[]{:S(2)}, u32[]{:S(2)}) collective-permute-start(bf16[12,64,128]{2,1,0:T(8,128)(2,1)S(1)} %copy-done.15), channel_id=1, source_target_pairs={{0,9},{1,8},{2,11},{3,10},{4,13},{5,12},{6,15},{7,14},{8,1},{9,0},... | collective-permute-start | bytes 589832 | tf_op jit(solution)/shard_map/ppermute | solution.py:260
  39.1 33.0 %collective-permute-start.8 = (bf16[12,64,128]{2,1,0:T(8,128)(2,1)S(1)}, bf16[12,64,128]{2,1,0:T(8,128)(2,1)S(1)}, u32[]{:S(2)}, u32[]{:S(2)}) collective-permute-start(bf16[12,64,128]{2,1,0:T(8,128)(2,1)S(1)} %copy-done.14), channel_id=1, source_target_pairs={{0,4},{1,5},{2,6},{3,7},{4,8},{5,9},{6,10},{7,11},{8,12},{9,13},{1... | collective-permute-start | bytes 589832 | tf_op jit(solution)/shard_map/ppermute | solution.py:260
  42.3 29.8 %collective-permute-start.9 = (bf16[12,64,128]{2,1,0:T(8,128)(2,1)S(1)}, bf16[12,64,128]{2,1,0:T(8,128)(2,1)S(1)}, u32[]{:S(2)}, u32[]{:S(2)}) collective-permute-start(bf16[12,64,128]{2,1,0:T(8,128)(2,1)S(1)} %copy-done.13), channel_id=1, source_target_pairs={{0,12},{1,13},{2,14},{3,15},{4,0},{5,1},{6,2},{7,3},{8,4},{9,5},{1... | collective-permute-start | bytes 589832 | tf_op jit(solution)/shard_map/ppermute | solution.py:260
  46.2 28.5 %collective-permute-start.10 = (bf16[12,64,128]{2,1,0:T(8,128)(2,1)}, bf16[12,64,128]{2,1,0:T(8,128)(2,1)S(1)}, u32[]{:S(2)}, u32[]{:S(2)}) collective-permute-start(bf16[12,64,128]{2,1,0:T(8,128)(2,1)} %get-tuple-element.54), channel_id=1, source_target_pairs={{0,1},{1,0},{2,3},{3,2},{4,5},{5,4},{6,7},{7,6},{8,9},{9,8},{10,11... | collective-permute-start | bytes 589832 | tf_op jit(solution)/shard_map/ppermute | solution.py:260
  51.2 34.3 %all-to-all-start.1 = ((bf16[16,4,2048]{2,1,0:T(4,128)(2,1)}), bf16[16,4,2048]{2,1,0:T(4,128)(2,1)S(1)}, u32[]{:S(2)}, u32[]{:S(2)}) async-start(bf16[16,4,2048]{2,1,0:T(4,128)(2,1)} %get-tuple-element.48), calls=%async_computation.1 | async-start | bytes 524288 | tf_op jit(solution)/shard_map/all_to_all | solution.py:276
  58.0 27.5 %collective-permute-start.3 = (bf16[12,64,128]{2,1,0:T(8,128)(2,1)}, bf16[12,64,128]{2,1,0:T(8,128)(2,1)S(1)}, u32[]{:S(2)}, u32[]{:S(2)}) collective-permute-start(bf16[12,64,128]{2,1,0:T(8,128)(2,1)} %get-tuple-element.45), channel_id=1, source_target_pairs={{0,13},{1,12},{2,15},{3,14},{4,1},{5,0},{6,3},{7,2},{8,5},{9,4},{1... | collective-permute-start | bytes 589832 | tf_op jit(solution)/shard_map/ppermute | solution.py:260
  68.6 17.0 %collective-permute-start.4 = (bf16[12,64,128]{2,1,0:T(8,128)(2,1)}, bf16[12,64,128]{2,1,0:T(8,128)(2,1)S(1)}, u32[]{:S(2)}, u32[]{:S(2)}) collective-permute-start(bf16[12,64,128]{2,1,0:T(8,128)(2,1)} %get-tuple-element.46), channel_id=1, source_target_pairs={{0,2},{1,3},{2,4},{3,5},{4,6},{5,7},{6,8},{7,9},{8,10},{9,11},{10,... | collective-permute-start | bytes 589832 | tf_op jit(solution)/shard_map/ppermute | solution.py:260
  72.0 13.5 %collective-permute-start.5 = (bf16[12,64,128]{2,1,0:T(8,128)(2,1)}, bf16[12,64,128]{2,1,0:T(8,128)(2,1)S(1)}, u32[]{:S(2)}, u32[]{:S(2)}) collective-permute-start(bf16[12,64,128]{2,1,0:T(8,128)(2,1)} %get-tuple-element.47), channel_id=1, source_target_pairs={{0,14},{1,15},{2,0},{3,1},{4,2},{5,3},{6,4},{7,5},{8,6},{9,7},{10,... | collective-permute-start | bytes 589832 | tf_op jit(solution)/shard_map/ppermute | solution.py:260
  72.0 15.8 %collective-permute-start = (bf16[12,64,128]{2,1,0:T(8,128)(2,1)}, bf16[12,64,128]{2,1,0:T(8,128)(2,1)S(1)}, u32[]{:S(2)}, u32[]{:S(2)}) collective-permute-start(bf16[12,64,128]{2,1,0:T(8,128)(2,1)} %get-tuple-element.42), channel_id=1, source_target_pairs={{0,3},{1,2},{2,5},{3,4},{4,7},{5,6},{6,9},{7,8},{8,11},{9,10},{10,... | collective-permute-start | bytes 589832 | tf_op jit(solution)/shard_map/ppermute | solution.py:260
  75.3 12.5 %collective-permute-start.1 = (bf16[12,64,128]{2,1,0:T(8,128)(2,1)}, bf16[12,64,128]{2,1,0:T(8,128)(2,1)S(1)}, u32[]{:S(2)}, u32[]{:S(2)}) collective-permute-start(bf16[12,64,128]{2,1,0:T(8,128)(2,1)} %get-tuple-element.43), channel_id=1, source_target_pairs={{0,15},{1,14},{2,1},{3,0},{4,3},{5,2},{6,5},{7,4},{8,7},{9,6},{10,... | collective-permute-start | bytes 589832 | tf_op jit(solution)/shard_map/ppermute | solution.py:260
  (9 other events, 16.2 us)

commit v4 on v3

--- a/solution.py
+++ b/solution.py
@@ -21,8 +21,7 @@
 FIRST = (3, -3)
 REST = (1, -1, 2, -2, 4, 0)
 ORDER = (
-    (3, 0), (-3, 0), (3, 1), (-3, 1), (0, 1), (4, 0), (4, 1), (2, 0), (-2, 0),
-    (2, 1), (-2, 1), (1, 0), (-1, 0), (1, 1), (-1, 1),
+    (3, 0), (-3, 0), (3, 1), (-3, 1), (2, 0), (-2, 0), (0, 1), (4, 0), (4, 1), (2, 1), (-2, 1), (1, 0), (-1, 0), (1, 1), (-1, 1),
 )
 
 
@@ -59,15 +58,16 @@
     return out
 
 
-def encode(dzs, ins, outs, buf, sems):
+def encode(dzs, ins, outs, buf, coded, sems, out_sems):
     z, c = place()
     copies = fetches(dzs, z, ins, buf, sems)
     for three in copies:
         for copy in three:
             copy.start()
     mine = c == 0
+    sending = []
     for i, three in enumerate(copies):
-        same, other = outs[2 * i], outs[2 * i + 1]
+        same, other = coded.at[2 * i], coded.at[2 * i + 1]
         for copy in three:
             copy.wait()
 
@@ -85,11 +85,16 @@
             return carry
 
         lax.fori_loop(0, E, one, 0, unroll=UNROLL)
+        for k in (2 * i, 2 * i + 1):
+            copy = pltpu.make_async_copy(coded.at[k], outs[k], out_sems.at[k])
+            copy.start()
+            sending.append(copy)
+    for copy in sending:
+        copy.wait()
 
 
 def code_kernel(dzs, gate, up, down, *rest):
-    outs, (buf, sems) = rest[: 2 * len(dzs)], rest[2 * len(dzs) :]
-    encode(dzs, (gate, up, down), outs, buf, sems)
+    encode(dzs, (gate, up, down), rest[: 2 * len(dzs)], *rest[2 * len(dzs) :])
 
 
 def sums_kernel(gate, up, down, router, gain, table, buf, tall, line, sems):
@@ -103,11 +108,9 @@
         jnp.int32, (128, 128), 1
     )
     left = lax.broadcasted_iota(jnp.int32, (8, 128), 1) < 64
+    row = lax.broadcasted_iota(jnp.int32, (8, 128), 0)
     served = (router[...] * gain[...]).astype(jnp.bfloat16).astype(jnp.float32)
-    for d in range(16):
-        for q in range(4):
-            at = slice((N // 2 + q) * 128, (N // 2 + q) * 128 + 128)
-            table[d, :, at] = served[q : q + 1]
+    ends = [jnp.where(row == 6, served[k : k + 1], served[k + 1 : k + 2]) for k in (0, 2)]
     for n in range(N):
         q, half = n // 2, n % 2
         copies[n].wait()
@@ -125,25 +128,30 @@
         for core, both in enumerate(
             (jnp.where(left, a, pltpu.roll(b, 64, 1)), jnp.where(left, pltpu.roll(a, 64, 1), b))
         ):
-            for q in range(N // 2):
-                table[2 * chip + core, :, q * 128 : q * 128 + 128] = both[q : q + 1]
+            high = both.astype(jnp.bfloat16).astype(jnp.float32)
+            parts = (high, both - high)
+            parts = [jnp.where(row < N // 2, p, end) for p, end in zip(parts, ends)]
+            table[2 * chip + core] = jnp.concatenate(parts, axis=0).astype(jnp.bfloat16)
 
 
 def scale_kernel(table, gate, up, down, factors, rows, line):
-    total = table[0]
+    def sums_of(s):
+        parts = table[s].astype(jnp.float32)
+        return parts[:8] + parts[8:]
+
+    total = sums_of(0)
     for s in range(1, 16):
-        total = total + table[s]
-    scale = total[:, : N // 2 * 128] / D_MODEL
+        total = total + sums_of(s)
+    scale = total / D_MODEL
     for n in range(N):
         out = (gate, up, down)[n // E]
-        out[n % E : n % E + 1, :] = scale[:, n * 64 : n * 64 + 64]
+        half = n % 2 * 64
+        out[n % E : n % E + 1, :] = scale[n // 2 : n // 2 + 1, half : half + 64]
     for s in range(16):
-        f = jnp.maximum(table[s, :, : N // 2 * 128], FLOOR) / (AMP * scale)
-        f = [f[:, q * 128 : q * 128 + 128] for q in range(N // 2)]
-        factors[s] = jnp.concatenate(f + f[:2], axis=0).T
-        for q in range(4):
-            at = slice((N // 2 + q) * 128, (N // 2 + q) * 128 + 128)
-            line[q : q + 1, s * 128 : s * 128 + 128] = table[s, :, at].astype(jnp.bfloat16)
+        factors[s] = (jnp.maximum(sums_of(s), FLOOR) / (AMP * scale)).T
+        at = slice(s * 128, s * 128 + 128)
+        line[0:2, at] = table[s, 6:8]
+        line[2:4, at] = table[s, 14:16]
     for d in range(16):
         rows[d] = line[...]
 
@@ -214,14 +222,15 @@
 
 GROUPS = (
     ((0, 0), (0, 1), (3, 0), (-3, 0), (3, 1), (-3, 1)),
-    ((4, 0), (4, 1), (2, 0), (-2, 0)),
+    ((2, 0), (-2, 0), (4, 0), (4, 1)),
     ((2, 1), (-2, 1), (1, 0), (-1, 0)),
-    ((1, 1), (-1, 1)),
+    ((1, 1),),
+    ((-1, 1),),
 )
 
 
 def local(train_gate, train_up, train_down, router_weight, router_gain):
-    ins = (train_gate, train_up, train_down)
+    in_hbm = [kept(x, pltpu.HBM) for x in (train_gate, train_up, train_down)]
     sent = {}
 
     def coded(dzs, limit):
@@ -229,20 +238,22 @@
             functools.partial(code_kernel, dzs),
             out_shape=(PIECE,) * (2 * len(dzs)),
             in_specs=[HBM, HBM, HBM],
-            out_specs=(VMEM,) * (2 * len(dzs)),
+            out_specs=(HBM,) * (2 * len(dzs)),
             scratch_shapes=[
                 pltpu.VMEM((len(dzs), 3, E, 128, 128), jnp.float32),
+                pltpu.VMEM((2 * len(dzs), N, 64, 128), jnp.bfloat16),
                 pltpu.SemaphoreType.DMA((len(dzs), 3)),
+                pltpu.SemaphoreType.DMA((2 * len(dzs),)),
             ],
             compiler_params=pltpu.CompilerParams(vmem_limit_bytes=limit),
-        )(*(pltpu.with_memory_space_constraint(x, pltpu.HBM) for x in ins))
+        )(*in_hbm)
         for i, dz in enumerate(dzs):
             sent[dz, 0], sent[dz, 1] = pieces[2 * i], pieces[2 * i + 1]
 
     coded(FIRST, 6 * MiB)
     table = pl.pallas_call(
         sums_kernel,
-        out_shape=pltpu.VMEM((16, 1, 1280), jnp.float32),
+        out_shape=pltpu.VMEM((16, 16, 128), jnp.bfloat16),
         in_specs=[HBM, HBM, HBM, VMEM, VMEM],
         out_specs=VMEM,
         scratch_shapes=[
@@ -253,7 +264,7 @@
         ],
         compiler_params=pltpu.CompilerParams(vmem_limit_bytes=12 * MiB),
         name="totals",
-    )(*ins, router_weight.T, router_gain[None])
+    )(train_gate, train_up, train_down, router_weight.T, router_gain[None])
     coded(REST, 12 * MiB)
     got = {(0, 0): sent[0, 0]}
     for dz, dc in ORDER:

time: 89.5 us -> 104 us (1.16)
  blocking collectives: 0 us -> 24.8 us
  starting transfers between devices: 53.2 us -> 45.2 us
  waiting for transfers between devices: 9.56 us -> 7.6 us
    all_to_all x0 -> x1, blocking collectives: none -> 24.8 us  [local(): table = lax.all_to_all(table, 'rows', 0, 0, tiled=True)]
    all_to_all x1 -> x0, starting transfers between devices: 6.31 us -> none  [local(): table = lax.all_to_all(table, 'rows', 0, 0, tiled=True)]
    all_to_all x1 -> x0, waiting for transfers between devices: 3.99 us -> none  [local(): table = lax.all_to_all(table, 'rows', 0, 0, tiled=True)]
    ppermute x15, waiting for transfers between devices: 5.57 us -> 7.6 us  [local(): got[dz, dc] = lax.ppermute(sent[dz, dc], 'rows', pairs_of(dz, dc))]
    ppermute x15, starting transfers between devices: 40.2 us -> 38.5 us  [local(): got[dz, dc] = lax.ppermute(sent[dz, dc], 'rows', pairs_of(dz, dc))]
    pallas_call x4 -> x5, Pallas kernels: 7.73 us -> 8.44 us  [decode(): pl.pallas_call(functools.partial(decode_kernel, where, len(before), wide...]
    unnamed x32 -> x26, local copies, waits for them, and re-layouts: 6.46 us -> 6.42 us
  transfers between devices with their start and end apart: 17 -> 16, of which waited for: 3 -> 2; matrix products, arithmetic and copies ran while one was open for 0% -> 0% of each run, Pallas kernels for 17% -> 14%
where the time goes in v4:
time: 104 us
  starting transfers between devices  45.2 us (43%)
  blocking collectives  24.8 us (24%)
  Pallas kernels  18.5 us (18%)
  waiting for transfers between devices  7.6 us (7%)
  local copies, waits for them, and re-layouts  6.42 us (6%)
    ppermute x15, starting transfers between devices, local(): got[dz, dc] = lax.ppermute(sent[dz, dc], 'rows', pairs_of(dz, dc))  38.5 us
    all_to_all x1, blocking collectives, local(): table = lax.all_to_all(table, 'rows', 0, 0, tiled=True)  24.8 us
    pallas_call x5, Pallas kernels, decode(): pl.pallas_call(functools.partial(decode_kernel, where, len(before), wide...  8.44 us
    ppermute x15, waiting for transfers between devices, local(): got[dz, dc] = lax.ppermute(sent[dz, dc], 'rows', pairs_of(dz, dc))  7.6 us
    pallas_call x2, Pallas kernels, coded(): pl.pallas_call(functools.partial(code_kernel, dzs), out_shape=(PIECE,) *...  7.05 us
    all_to_all x1, starting transfers between devices, local(): wide = lax.all_to_all(rows, 'owner', 0, 0, tiled=True)  6.75 us
    unnamed x26, local copies, waits for them, and re-layouts  6.42 us
  transfers between devices with their start and end apart: 16, of which 2 were waited for; matrix products, arithmetic and copies ran while one was open for 0% of the time, Pallas kernels for 14%

profile of v4, /device:TPU:1, one launch (start us, length us, event | category | flops | bytes accessed | tf_op | source)
XLA Modules:
  0.0 103.6 jit_solution(16524990702996438416)
XLA Ops:
  0.6 2.7 %shard_map.109 = (bf16[12,64,128]{2,1,0:T(8,128)(2,1)}, bf16[12,64,128]{2,1,0:T(8,128)(2,1)}, bf16[12,64,128]{2,1,0:T(8,128)(2,1)}, bf16[12,64,128]{2,1,0:T(8,128)(2,1)}) custom-call(f32[4,128,1024]{2,1,0:T(8,128)} %gate.5, f32[4,128,1024]{2,1,0:T(8,128)} %up.5, f32[4,1024,128]{2,1,0:T(8,128)} %down.5), custom_call_target="tpu_custom_call" | custom-call | tf_op jit(solution)/shard_map/pallas_call | solution.py:237
  3.3 5.2 %collective-permute-start.11 = (bf16[12,64,128]{2,1,0:T(8,128)(2,1)}, bf16[12,64,128]{2,1,0:T(8,128)(2,1)S(1)}, u32[]{:S(2)}, u32[]{:S(2)}) collective-permute-start(bf16[12,64,128]{2,1,0:T(8,128)(2,1)} %get-tuple-element.58), channel_id=1, source_target_pairs={{0,6},{1,7},{2,8},{3,9},{4,10},{5,11},{6,12},{7,13},{8,14},{9,15},... | collective-permute-start | bytes 589832 | tf_op jit(solution)/shard_map/ppermute | solution.py:271
  8.6 2.2 %collective-permute-start.12 = (bf16[12,64,128]{2,1,0:T(8,128)(2,1)}, bf16[12,64,128]{2,1,0:T(8,128)(2,1)S(1)}, u32[]{:S(2)}, u32[]{:S(2)}) collective-permute-start(bf16[12,64,128]{2,1,0:T(8,128)(2,1)} %get-tuple-element.59), channel_id=1, source_target_pairs={{0,10},{1,11},{2,12},{3,13},{4,14},{5,15},{6,0},{7,1},{8,2},{9,3},... | collective-permute-start | bytes 589832 | tf_op jit(solution)/shard_map/ppermute | solution.py:271
  10.8 2.4 %collective-permute-start.13 = (bf16[12,64,128]{2,1,0:T(8,128)(2,1)}, bf16[12,64,128]{2,1,0:T(8,128)(2,1)S(1)}, u32[]{:S(2)}, u32[]{:S(2)}) collective-permute-start(bf16[12,64,128]{2,1,0:T(8,128)(2,1)} %get-tuple-element.60), channel_id=1, source_target_pairs={{0,7},{1,6},{2,9},{3,8},{4,11},{5,10},{6,13},{7,12},{8,15},{9,14},... | collective-permute-start | bytes 589832 | tf_op jit(solution)/shard_map/ppermute | solution.py:271
  13.2 3.2 %collective-permute-start.14 = (bf16[12,64,128]{2,1,0:T(8,128)(2,1)}, bf16[12,64,128]{2,1,0:T(8,128)(2,1)S(1)}, u32[]{:S(2)}, u32[]{:S(2)}) collective-permute-start(bf16[12,64,128]{2,1,0:T(8,128)(2,1)} %get-tuple-element.61), channel_id=1, source_target_pairs={{0,11},{1,10},{2,13},{3,12},{4,15},{5,14},{6,1},{7,0},{8,3},{9,2},... | collective-permute-start | bytes 589832 | tf_op jit(solution)/shard_map/ppermute | solution.py:271
  16.4 4.3 %shard_map.108 = (bf16[12,64,128]{2,1,0:T(8,128)(2,1)}, bf16[12,64,128]{2,1,0:T(8,128)(2,1)}, bf16[12,64,128]{2,1,0:T(8,128)(2,1)}, bf16[12,64,128]{2,1,0:T(8,12...) custom-call(f32[4,128,1024]{2,1,0:T(8,128)} %gate.5, ...), custom_call_target="tpu_custom_call" | custom-call | tf_op jit(solution)/shard_map/pallas_call | solution.py:237
  20.8 1.8 %collective-permute-start.2 = (bf16[12,64,128]{2,1,0:T(8,128)(2,1)}, bf16[12,64,128]{2,1,0:T(8,128)(2,1)S(1)}, u32[]{:S(2)}, u32[]{:S(2)}) collective-permute-start(bf16[12,64,128]{2,1,0:T(8,128)(2,1)} %get-tuple-element.47), channel_id=1, source_target_pairs={{0,5},{1,4},{2,7},{3,6},{4,9},{5,8},{6,11},{7,10},{8,13},{9,12},{1... | collective-permute-start | bytes 589832 | tf_op jit(solution)/shard_map/ppermute | solution.py:271
  22.6 3.7 %collective-permute-start.6 = (bf16[12,64,128]{2,1,0:T(8,128)(2,1)}, bf16[12,64,128]{2,1,0:T(8,128)(2,1)S(1)}, u32[]{:S(2)}, u32[]{:S(2)}) collective-permute-start(bf16[12,64,128]{2,1,0:T(8,128)(2,1)} %get-tuple-element.52), channel_id=1, source_target_pairs={{0,4},{1,5},{2,6},{3,7},{4,8},{5,9},{6,10},{7,11},{8,12},{9,13},{1... | collective-permute-start | bytes 589832 | tf_op jit(solution)/shard_map/ppermute | solution.py:271
  27.0 3.2 %collective-permute-start.7 = (bf16[12,64,128]{2,1,0:T(8,128)(2,1)}, bf16[12,64,128]{2,1,0:T(8,128)(2,1)S(1)}, u32[]{:S(2)}, u32[]{:S(2)}) collective-permute-start(bf16[12,64,128]{2,1,0:T(8,128)(2,1)} %get-tuple-element.53), channel_id=1, source_target_pairs={{0,12},{1,13},{2,14},{3,15},{4,0},{5,1},{6,2},{7,3},{8,4},{9,5},{1... | collective-permute-start | bytes 589832 | tf_op jit(solution)/shard_map/ppermute | solution.py:271
  30.2 5.6 %collective-permute-done.13.rest_4_ = bf16[12,64,128]{2,1,0:T(8,128)(2,1)S(1)} collective-permute-done((bf16[12,64,128]{2,1,0:T(8,128)(2,1)}, bf16[12,64,128]{2,1,0:T(8,128)(2,1)S(1)}, u32[]{:S(2)}, u32[]{:S(2)}) %collective-permute-start.13) | collective-permute-done | bytes 196640 | tf_op jit(solution)/shard_map/ppermute | solution.py:271
  36.5 6.2 %collective-permute-start.8 = (bf16[12,64,128]{2,1,0:T(8,128)(2,1)}, bf16[12,64,128]{2,1,0:T(8,128)(2,1)S(1)}, u32[]{:S(2)}, u32[]{:S(2)}) collective-permute-start(bf16[12,64,128]{2,1,0:T(8,128)(2,1)} %get-tuple-element.54), channel_id=1, source_target_pairs={{0,8},{1,9},{2,10},{3,11},{4,12},{5,13},{6,14},{7,15},{8,0},{9,1},... | collective-permute-start | bytes 589832 | tf_op jit(solution)/shard_map/ppermute | solution.py:271
  43.4 2.0 %collective-permute-done.2.rest_0_ = bf16[12,64,128]{2,1,0:T(8,128)(2,1)S(1)} collective-permute-done((bf16[12,64,128]{2,1,0:T(8,128)(2,1)}, bf16[12,64,128]{2,1,0:T(8,128)(2,1)S(1)}, u32[]{:S(2)}, u32[]{:S(2)}) %collective-permute-start.2) | collective-permute-done | bytes 196640 | tf_op jit(solution)/shard_map/ppermute | solution.py:271
  45.4 2.0 %totals.1 = bf16[16,16,128]{2,1,0:T(8,128)(2,1)S(1)} custom-call(f32[4,128,1024]{2,1,0:T(8,128)S(1)} %copy-done, f32[4,128,1024]{2,1,0:T(8,128)S(1)} %copy-done.1, f32[4,1024,128]{2,1,0:T(8,128)S(1)} %copy-done.2, f32[4,128]{1,0:T(4,128)S(1)} %bitcast.5, f32[1,128]{1,0:T(1,128)S(1)} %bitcast.6), custom_call_target="tpu_custom_call" | custom-call | tf_op jit(solution)/shard_map/totals/pallas_call | solution.py:254
  47.4 24.8 %all_to_all.10.table = bf16[16,16,128]{2,1,0:T(8,128)(2,1)S(1)} all-to-all(bf16[16,16,128]{2,1,0:T(8,128)(2,1)S(1)} %totals.1), channel_id=1, replica_groups=mesh['owner'=16,'rows'=16] {'rows'}, dimensions={0} | all-to-all | bytes 131072 | tf_op jit(solution)/shard_map/all_to_all | solution.py:272
  72.3 1.0 %scales.1 = (f32[4,64]{1,0:T(4,128)}, f32[4,64]{1,0:T(4,128)}, f32[4,64]{1,0:T(4,128)}, f32[16,128,8]{2,1,0:T(8,128)S(1)}, bf16[16,4,2048]{2,1,0:T(4,128)(2,1)}) custom-call(bf16[16,16,128]{2,1,0:T(8,128)(2,1)S(1)} %all_to_all.10.table), custom_call_target="tpu_custom_call" | custom-call | tf_op jit(solution)/shard_map/scales/pallas_call | solution.py:274
  73.3 6.8 %all-to-all-start.1 = ((bf16[16,4,2048]{2,1,0:T(4,128)(2,1)}), bf16[16,4,2048]{2,1,0:T(4,128)(2,1)S(1)}, u32[]{:S(2)}, u32[]{:S(2)}) async-start(bf16[16,4,2048]{2,1,0:T(4,128)(2,1)} %get-tuple-element.51), calls=%async_computation.1 | async-start | bytes 524288 | tf_op jit(solution)/shard_map/all_to_all | solution.py:287
  80.1 4.8 %collective-permute-start.3 = (bf16[12,64,128]{2,1,0:T(8,128)(2,1)}, bf16[12,64,128]{2,1,0:T(8,128)(2,1)S(1)}, u32[]{:S(2)}, u32[]{:S(2)}) collective-permute-start(bf16[12,64,128]{2,1,0:T(8,128)(2,1)} %get-tuple-element.48), channel_id=1, source_target_pairs={{0,13},{1,12},{2,15},{3,14},{4,1},{5,0},{6,3},{7,2},{8,5},{9,4},{1... | collective-permute-start | bytes 589832 | tf_op jit(solution)/shard_map/ppermute | solution.py:271
  84.9 2.7 %collective-permute-start.5 = (bf16[12,64,128]{2,1,0:T(8,128)(2,1)}, bf16[12,64,128]{2,1,0:T(8,128)(2,1)S(1)}, u32[]{:S(2)}, u32[]{:S(2)}) collective-permute-start(bf16[12,64,128]{2,1,0:T(8,128)(2,1)} %get-tuple-element.50), channel_id=1, source_target_pairs={{0,14},{1,15},{2,0},{3,1},{4,2},{5,3},{6,4},{7,5},{8,6},{9,7},{10,... | collective-permute-start | bytes 589832 | tf_op jit(solution)/shard_map/ppermute | solution.py:271
  88.2 2.9 %collective-permute-start = (bf16[12,64,128]{2,1,0:T(8,128)(2,1)}, bf16[12,64,128]{2,1,0:T(8,128)(2,1)S(1)}, u32[]{:S(2)}, u32[]{:S(2)}) collective-permute-start(bf16[12,64,128]{2,1,0:T(8,128)(2,1)} %get-tuple-element.45), channel_id=1, source_target_pairs={{0,15},{1,14},{2,1},{3,0},{4,3},{5,2},{6,5},{7,4},{8,7},{9,6},{10,... | collective-permute-start | bytes 589832 | tf_op jit(solution)/shard_map/ppermute | solution.py:271
  91.2 0.9 copy-done.4
  92.1 0.9 copy-done.6
  94.9 2.9 %shard_map.110 = (bf16[4,64,2048]{2,1,0:T(8,128)(2,1)}, bf16[4,64,2048]{2,1,0:T(8,128)(2,1)}, bf16[4,64,2048]{2,1,0:T(8,128)(2,1)}) custom-call(f32[16,128,8]{2,1,0:T(8,128)S(1)} %get-tuple-element.44.factors, bf16[12,64,128]{2,1,0:T(8,128)(2,1)} %get-tuple-element.56.rest_0_, bf16[12,64,128]{2,1,0:T(8,128)(2,1)S(1)} %copy-done.10, ...), custom_call_target="tpu_custom_call" | custom-call | flops 60000000 | bytes 2400000 | tf_op jit(solution)/shard_map/pallas_call | solution.py:206
  97.8 1.5 %shard_map.111 = (bf16[4,64,2048]{2,1,0:T(8,128)(2,1)}, bf16[4,64,2048]{2,1,0:T(8,128)(2,1)}, bf16[4,64,2048]{2,1,0:T(8,128)(2,1)}) custom-call(f32[16,128,8]{2,1,0:T(8,128)S(1)} %get-tuple-element.44.factors, bf16[12,64,128]{2,1,0:T(8,128)(2,1)S(1)} %collective-permute-done.6.rest_0_, ...), custom_call_target="tpu_custom_call", output_to_operand_aliasing={{0}: (5, {}), {1}: (6, {}), {2}: (7, {})} | custom-call | flops 40000000 | bytes 1600000 | tf_op jit(solution)/shard_map/pallas_call | solution.py:206
  99.3 2.3 %shard_map.112 = (bf16[4,64,2048]{2,1,0:T(8,128)(2,1)}, bf16[4,64,2048]{2,1,0:T(8,128)(2,1)}, bf16[4,64,2048]{2,1,0:T(8,128)(2,1)}, bf16[64,2048]{1,0:T(8,128)(2,1)}) custom-call(f32[16,128,8]{2,1,0:T(8,128)S(1)} %get-tuple-element.44.factors, ...), custom_call_target="tpu_custom_call", output_to_operand_aliasing={{0}: (6, {}), {1}: (7, {}), {2}: (8, {})} | custom-call | flops 40000000 | bytes 1600000 | tf_op jit(solution)/shard_map/pallas_call | solution.py:206
  (44 shorter events, 6.4 us)
Async XLA Ops:
  3.3 19.3 %collective-permute-start.11 = (bf16[12,64,128]{2,1,0:T(8,128)(2,1)}, bf16[12,64,128]{2,1,0:T(8,128)(2,1)S(1)}, u32[]{:S(2)}, u32[]{:S(2)}) collective-permute-start(bf16[12,64,128]{2,1,0:T(8,128)(2,1)} %get-tuple-element.58), channel_id=1, source_target_pairs={{0,6},{1,7},{2,8},{3,9},{4,10},{5,11},{6,12},{7,13},{8,14},{9,15},... | collective-permute-start | bytes 589832 | tf_op jit(solution)/shard_map/ppermute | solution.py:271
  8.6 17.7 %collective-permute-start.12 = (bf16[12,64,128]{2,1,0:T(8,128)(2,1)}, bf16[12,64,128]{2,1,0:T(8,128)(2,1)S(1)}, u32[]{:S(2)}, u32[]{:S(2)}) collective-permute-start(bf16[12,64,128]{2,1,0:T(8,128)(2,1)} %get-tuple-element.59), channel_id=1, source_target_pairs={{0,10},{1,11},{2,12},{3,13},{4,14},{5,15},{6,0},{7,1},{8,2},{9,3},... | collective-permute-start | bytes 589832 | tf_op jit(solution)/shard_map/ppermute | solution.py:271
  10.8 25.0 %collective-permute-start.13 = (bf16[12,64,128]{2,1,0:T(8,128)(2,1)}, bf16[12,64,128]{2,1,0:T(8,128)(2,1)S(1)}, u32[]{:S(2)}, u32[]{:S(2)}) collective-permute-start(bf16[12,64,128]{2,1,0:T(8,128)(2,1)} %get-tuple-element.60), channel_id=1, source_target_pairs={{0,7},{1,6},{2,9},{3,8},{4,11},{5,10},{6,13},{7,12},{8,15},{9,14},... | collective-permute-start | bytes 589832 | tf_op jit(solution)/shard_map/ppermute | solution.py:271
  13.2 32.2 %copy-start = (f32[4,128,1024]{2,1,0:T(8,128)S(1)}, f32[4,128,1024]{2,1,0:T(8,128)}, u32[]{:S(2)}) copy-start(f32[4,128,1024]{2,1,0:T(8,128)} %gate.5) | copy-start | bytes 6291460
  13.2 32.2 %copy-start.1 = (f32[4,128,1024]{2,1,0:T(8,128)S(1)}, f32[4,128,1024]{2,1,0:T(8,128)}, u32[]{:S(2)}) copy-start(f32[4,128,1024]{2,1,0:T(8,128)} %up.5) | copy-start | bytes 6291460
  13.2 32.2 %copy-start.2 = (f32[4,1024,128]{2,1,0:T(8,128)S(1)}, f32[4,1024,128]{2,1,0:T(8,128)}, u32[]{:S(2)}) copy-start(f32[4,1024,128]{2,1,0:T(8,128)} %down.5) | copy-start | bytes 6291460
  13.2 32.2 %copy-start.11 = (f32[128,4]{0,1:T(4,128)S(1)}, f32[128,4]{0,1:T(4,128)}, u32[]{:S(2)}) copy-start(f32[128,4]{0,1:T(4,128)} %param.8) | copy-start | bytes 6148
  13.2 32.2 %copy-start.12 = (f32[128]{0:T(128)S(1)}, f32[128]{0:T(128)}, u32[]{:S(2)}) copy-start(f32[128]{0:T(128)} %param.9) | copy-start | bytes 1540
  13.2 29.5 %collective-permute-start.14 = (bf16[12,64,128]{2,1,0:T(8,128)(2,1)}, bf16[12,64,128]{2,1,0:T(8,128)(2,1)S(1)}, u32[]{:S(2)}, u32[]{:S(2)}) collective-permute-start(bf16[12,64,128]{2,1,0:T(8,128)(2,1)} %get-tuple-element.61), channel_id=1, source_target_pairs={{0,11},{1,10},{2,13},{3,12},{4,15},{5,14},{6,1},{7,0},{8,3},{9,2},... | collective-permute-start | bytes 589832 | tf_op jit(solution)/shard_map/ppermute | solution.py:271
  20.8 24.6 %collective-permute-start.2 = (bf16[12,64,128]{2,1,0:T(8,128)(2,1)}, bf16[12,64,128]{2,1,0:T(8,128)(2,1)S(1)}, u32[]{:S(2)}, u32[]{:S(2)}) collective-permute-start(bf16[12,64,128]{2,1,0:T(8,128)(2,1)} %get-tuple-element.47), channel_id=1, source_target_pairs={{0,5},{1,4},{2,7},{3,6},{4,9},{5,8},{6,11},{7,10},{8,13},{9,12},{1... | collective-permute-start | bytes 589832 | tf_op jit(solution)/shard_map/ppermute | solution.py:271
  22.6 57.5 %collective-permute-start.6 = (bf16[12,64,128]{2,1,0:T(8,128)(2,1)}, bf16[12,64,128]{2,1,0:T(8,128)(2,1)S(1)}, u32[]{:S(2)}, u32[]{:S(2)}) collective-permute-start(bf16[12,64,128]{2,1,0:T(8,128)(2,1)} %get-tuple-element.52), channel_id=1, source_target_pairs={{0,4},{1,5},{2,6},{3,7},{4,8},{5,9},{6,10},{7,11},{8,12},{9,13},{1... | collective-permute-start | bytes 589832 | tf_op jit(solution)/shard_map/ppermute | solution.py:271
  27.0 57.9 %collective-permute-start.7 = (bf16[12,64,128]{2,1,0:T(8,128)(2,1)}, bf16[12,64,128]{2,1,0:T(8,128)(2,1)S(1)}, u32[]{:S(2)}, u32[]{:S(2)}) collective-permute-start(bf16[12,64,128]{2,1,0:T(8,128)(2,1)} %get-tuple-element.53), channel_id=1, source_target_pairs={{0,12},{1,13},{2,14},{3,15},{4,0},{5,1},{6,2},{7,3},{8,4},{9,5},{1... | collective-permute-start | bytes 589832 | tf_op jit(solution)/shard_map/ppermute | solution.py:271
  36.5 48.4 %collective-permute-start.8 = (bf16[12,64,128]{2,1,0:T(8,128)(2,1)}, bf16[12,64,128]{2,1,0:T(8,128)(2,1)S(1)}, u32[]{:S(2)}, u32[]{:S(2)}) collective-permute-start(bf16[12,64,128]{2,1,0:T(8,128)(2,1)} %get-tuple-element.54), channel_id=1, source_target_pairs={{0,8},{1,9},{2,10},{3,11},{4,12},{5,13},{6,14},{7,15},{8,0},{9,1},... | collective-permute-start | bytes 589832 | tf_op jit(solution)/shard_map/ppermute | solution.py:271
  43.4 44.1 %collective-permute-start.9 = (bf16[12,64,128]{2,1,0:T(8,128)(2,1)}, bf16[12,64,128]{2,1,0:T(8,128)(2,1)S(1)}, u32[]{:S(2)}, u32[]{:S(2)}) collective-permute-start(bf16[12,64,128]{2,1,0:T(8,128)(2,1)} %get-tuple-element.55), channel_id=1, source_target_pairs={{0,9},{1,8},{2,11},{3,10},{4,13},{5,12},{6,15},{7,14},{8,1},{9,0},... | collective-permute-start | bytes 589832 | tf_op jit(solution)/shard_map/ppermute | solution.py:271
  45.4 42.1 %collective-permute-start.10 = (bf16[12,64,128]{2,1,0:T(8,128)(2,1)}, bf16[12,64,128]{2,1,0:T(8,128)(2,1)S(1)}, u32[]{:S(2)}, u32[]{:S(2)}) collective-permute-start(bf16[12,64,128]{2,1,0:T(8,128)(2,1)} %get-tuple-element.57), channel_id=1, source_target_pairs={{0,1},{1,0},{2,3},{3,2},{4,5},{5,4},{6,7},{7,6},{8,9},{9,8},{10,11... | collective-permute-start | bytes 589832 | tf_op jit(solution)/shard_map/ppermute | solution.py:271
  73.3 26.0 %all-to-all-start.1 = ((bf16[16,4,2048]{2,1,0:T(4,128)(2,1)}), bf16[16,4,2048]{2,1,0:T(4,128)(2,1)S(1)}, u32[]{:S(2)}, u32[]{:S(2)}) async-start(bf16[16,4,2048]{2,1,0:T(4,128)(2,1)} %get-tuple-element.51), calls=%async_computation.1 | async-start | bytes 524288 | tf_op jit(solution)/shard_map/all_to_all | solution.py:287
  80.1 19.2 %collective-permute-start.3 = (bf16[12,64,128]{2,1,0:T(8,128)(2,1)}, bf16[12,64,128]{2,1,0:T(8,128)(2,1)S(1)}, u32[]{:S(2)}, u32[]{:S(2)}) collective-permute-start(bf16[12,64,128]{2,1,0:T(8,128)(2,1)} %get-tuple-element.48), channel_id=1, source_target_pairs={{0,13},{1,12},{2,15},{3,14},{4,1},{5,0},{6,3},{7,2},{8,5},{9,4},{1... | collective-permute-start | bytes 589832 | tf_op jit(solution)/shard_map/ppermute | solution.py:271
  84.9 14.4 %collective-permute-start.4 = (bf16[12,64,128]{2,1,0:T(8,128)(2,1)}, bf16[12,64,128]{2,1,0:T(8,128)(2,1)S(1)}, u32[]{:S(2)}, u32[]{:S(2)}) collective-permute-start(bf16[12,64,128]{2,1,0:T(8,128)(2,1)} %get-tuple-element.49), channel_id=1, source_target_pairs={{0,2},{1,3},{2,4},{3,5},{4,6},{5,7},{6,8},{7,9},{8,10},{9,11},{10,... | collective-permute-start | bytes 589832 | tf_op jit(solution)/shard_map/ppermute | solution.py:271
  84.9 14.4 %collective-permute-start.5 = (bf16[12,64,128]{2,1,0:T(8,128)(2,1)}, bf16[12,64,128]{2,1,0:T(8,128)(2,1)S(1)}, u32[]{:S(2)}, u32[]{:S(2)}) collective-permute-start(bf16[12,64,128]{2,1,0:T(8,128)(2,1)} %get-tuple-element.50), channel_id=1, source_target_pairs={{0,14},{1,15},{2,0},{3,1},{4,2},{5,3},{6,4},{7,5},{8,6},{9,7},{10,... | collective-permute-start | bytes 589832 | tf_op jit(solution)/shard_map/ppermute | solution.py:271
  87.5 14.1 %collective-permute-start.1 = (bf16[12,64,128]{2,1,0:T(8,128)(2,1)}, bf16[12,64,128]{2,1,0:T(8,128)(2,1)S(1)}, u32[]{:S(2)}, u32[]{:S(2)}) collective-permute-start(bf16[12,64,128]{2,1,0:T(8,128)(2,1)} %get-tuple-element.46), channel_id=1, source_target_pairs={{0,3},{1,2},{2,5},{3,4},{4,7},{5,6},{6,9},{7,8},{8,11},{9,10},{10,... | collective-permute-start | bytes 589832 | tf_op jit(solution)/shard_map/ppermute | solution.py:271
  88.2 14.3 %collective-permute-start = (bf16[12,64,128]{2,1,0:T(8,128)(2,1)}, bf16[12,64,128]{2,1,0:T(8,128)(2,1)S(1)}, u32[]{:S(2)}, u32[]{:S(2)}) collective-permute-start(bf16[12,64,128]{2,1,0:T(8,128)(2,1)} %get-tuple-element.45), channel_id=1, source_target_pairs={{0,15},{1,14},{2,1},{3,0},{4,3},{5,2},{6,5},{7,4},{8,7},{9,6},{10,... | collective-permute-start | bytes 589832 | tf_op jit(solution)/shard_map/ppermute | solution.py:271
  91.2 0.9 copy-start.4
  92.1 0.9 copy-start.6
  93.0 0.9 copy-start.8
  (5 other events, 3.6 us)

commit v5 on v4

--- a/solution.py
+++ b/solution.py
@@ -18,10 +18,10 @@
 
 UNROLL = 2
 MiB = 1 << 20
-FIRST = (3, -3)
-REST = (1, -1, 2, -2, 4, 0)
+FIRST = (4,)
+REST = (3, -3, 2, -2, 1, -1, 0)
 ORDER = (
-    (3, 0), (-3, 0), (3, 1), (-3, 1), (2, 0), (-2, 0), (0, 1), (4, 0), (4, 1), (2, 1), (-2, 1), (1, 0), (-1, 0), (1, 1), (-1, 1),
+    (4, 0), (4, 1), (3, 0), (-3, 0), (3, 1), (-3, 1), (0, 1), (2, 0), (-2, 0), (2, 1), (-2, 1), (1, 0), (-1, 0), (1, 1), (-1, 1),
 )
 
 
@@ -221,9 +221,9 @@
 
 
 GROUPS = (
-    ((0, 0), (0, 1), (3, 0), (-3, 0), (3, 1), (-3, 1)),
-    ((2, 0), (-2, 0), (4, 0), (4, 1)),
-    ((2, 1), (-2, 1), (1, 0), (-1, 0)),
+    ((0, 0), (0, 1), (4, 0), (4, 1), (3, 0), (-3, 0),),
+    ((3, 1), (-3, 1), (2, 0), (-2, 0),),
+    ((2, 1), (-2, 1), (1, 0), (-1, 0),),
     ((1, 1),),
     ((-1, 1),),
 )

time: 104 us -> 106 us (1.019)
  blocking collectives: 24.8 us -> 13 us
  starting transfers between devices: 45.2 us -> 56.2 us
  waiting for transfers between devices: 7.6 us -> 11.3 us
  local copies, waits for them, and re-layouts: 6.42 us -> 4.83 us
    all_to_all x1, blocking collectives: 24.8 us -> 13 us  [local(): table = lax.all_to_all(table, 'rows', 0, 0, tiled=True)]
    ppermute x15, starting transfers between devices: 38.5 us -> 49.5 us  [local(): got[dz, dc] = lax.ppermute(sent[dz, dc], 'rows', pairs_of(dz, dc))]
    ppermute x15, waiting for transfers between devices: 7.6 us -> 11.3 us  [local(): got[dz, dc] = lax.ppermute(sent[dz, dc], 'rows', pairs_of(dz, dc))]
    unnamed x26 -> x22, local copies, waits for them, and re-layouts: 6.42 us -> 4.83 us
  transfers between devices with their start and end apart: 16 -> 16, of which waited for: 2 -> 3; matrix products, arithmetic and copies ran while one was open for 0% -> 0% of each run, Pallas kernels for 14% -> 15%
where the time goes in v5:
time: 106 us; the launch traced here: 105 us
  starting transfers between devices  56.2 us (53%)
  Pallas kernels  19.1 us (18%)
  blocking collectives  13 us (12%)
  waiting for transfers between devices  11.3 us (11%)
  local copies, waits for them, and re-layouts  4.83 us (5%)
    ppermute x15, starting transfers between devices, local(): got[dz, dc] = lax.ppermute(sent[dz, dc], 'rows', pairs_of(dz, dc))  49.5 us
    all_to_all x1, blocking collectives, local(): table = lax.all_to_all(table, 'rows', 0, 0, tiled=True)  13 us
    ppermute x15, waiting for transfers between devices, local(): got[dz, dc] = lax.ppermute(sent[dz, dc], 'rows', pairs_of(dz, dc))  11.3 us
    pallas_call x5, Pallas kernels, decode(): pl.pallas_call(functools.partial(decode_kernel, where, len(before), wide...  8.52 us
    pallas_call x2, Pallas kernels, coded(): pl.pallas_call(functools.partial(code_kernel, dzs), out_shape=(PIECE,) *...  7.58 us
    all_to_all x1, starting transfers between devices, local(): wide = lax.all_to_all(rows, 'owner', 0, 0, tiled=True)  6.75 us
    unnamed x22, local copies, waits for them, and re-layouts  4.83 us
  transfers between devices with their start and end apart: 16, of which 3 were waited for; matrix products, arithmetic and copies ran while one was open for 0% of the time, Pallas kernels for 15%

profile of v5, /device:TPU:1, one launch (start us, length us, event | category | flops | bytes accessed | tf_op | source)
XLA Modules:
  0.0 105.3 jit_solution(14623220614131571226)
XLA Ops:
  0.6 2.3 %shard_map.109 = (bf16[12,64,128]{2,1,0:T(8,128)(2,1)}, bf16[12,64,128]{2,1,0:T(8,128)(2,1)}) custom-call(f32[4,128,1024]{2,1,0:T(8,128)} %gate.5, f32[4,128,1024]{2,1,0:T(8,128)} %up.5, f32[4,1024,128]{2,1,0:T(8,128)} %down.5), custom_call_target="tpu_custom_call" | custom-call | tf_op jit(solution)/shard_map/pallas_call | solution.py:237
  2.9 7.8 %collective-permute-start.11 = (bf16[12,64,128]{2,1,0:T(8,128)(2,1)}, bf16[12,64,128]{2,1,0:T(8,128)(2,1)S(1)}, u32[]{:S(2)}, u32[]{:S(2)}) collective-permute-start(bf16[12,64,128]{2,1,0:T(8,128)(2,1)} %get-tuple-element.58), channel_id=1, source_target_pairs={{0,8},{1,9},{2,10},{3,11},{4,12},{5,13},{6,14},{7,15},{8,0},{9,1},... | collective-permute-start | bytes 589832 | tf_op jit(solution)/shard_map/ppermute | solution.py:271
  10.8 1.1 %collective-permute-start.12 = (bf16[12,64,128]{2,1,0:T(8,128)(2,1)}, bf16[12,64,128]{2,1,0:T(8,128)(2,1)S(1)}, u32[]{:S(2)}, u32[]{:S(2)}) collective-permute-start(bf16[12,64,128]{2,1,0:T(8,128)(2,1)} %get-tuple-element.59), channel_id=1, source_target_pairs={{0,9},{1,8},{2,11},{3,10},{4,13},{5,12},{6,15},{7,14},{8,1},{9,0},... | collective-permute-start | bytes 589832 | tf_op jit(solution)/shard_map/ppermute | solution.py:271
  11.9 5.3 %shard_map.108 = (bf16[12,64,128]{2,1,0:T(8,128)(2,1)}, bf16[12,64,128]{2,1,0:T(8,128)(2,1)}, bf16[12,64,128]{2,1,0:T(8,128)(2,1)}, bf16[12,64,128]{2,1,0:T(8,12...) custom-call(f32[4,128,1024]{2,1,0:T(8,128)} %gate.5, ...), custom_call_target="tpu_custom_call" | custom-call | tf_op jit(solution)/shard_map/pallas_call | solution.py:237
  17.9 5.0 %collective-permute-start.6 = (bf16[12,64,128]{2,1,0:T(8,128)(2,1)}, bf16[12,64,128]{2,1,0:T(8,128)(2,1)S(1)}, u32[]{:S(2)}, u32[]{:S(2)}) collective-permute-start(bf16[12,64,128]{2,1,0:T(8,128)(2,1)} %get-tuple-element.52), channel_id=1, source_target_pairs={{0,7},{1,6},{2,9},{3,8},{4,11},{5,10},{6,13},{7,12},{8,15},{9,14},... | collective-permute-start | bytes 589832 | tf_op jit(solution)/shard_map/ppermute | solution.py:271
  23.0 3.4 %collective-permute-start.8 = (bf16[12,64,128]{2,1,0:T(8,128)(2,1)}, bf16[12,64,128]{2,1,0:T(8,128)(2,1)S(1)}, u32[]{:S(2)}, u32[]{:S(2)}) collective-permute-start(bf16[12,64,128]{2,1,0:T(8,128)(2,1)} %get-tuple-element.54), channel_id=1, source_target_pairs={{0,4},{1,5},{2,6},{3,7},{4,8},{5,9},{6,10},{7,11},{8,12},{9,13},{1... | collective-permute-start | bytes 589832 | tf_op jit(solution)/shard_map/ppermute | solution.py:271
  27.1 7.7 %collective-permute-start.9 = (bf16[12,64,128]{2,1,0:T(8,128)(2,1)}, bf16[12,64,128]{2,1,0:T(8,128)(2,1)S(1)}, u32[]{:S(2)}, u32[]{:S(2)}) collective-permute-start(bf16[12,64,128]{2,1,0:T(8,128)(2,1)} %get-tuple-element.55), channel_id=1, source_target_pairs={{0,12},{1,13},{2,14},{3,15},{4,0},{5,1},{6,2},{7,3},{8,4},{9,5},{1... | collective-permute-start | bytes 589832 | tf_op jit(solution)/shard_map/ppermute | solution.py:271
  34.8 10.0 %collective-permute-start.10 = (bf16[12,64,128]{2,1,0:T(8,128)(2,1)}, bf16[12,64,128]{2,1,0:T(8,128)(2,1)S(1)}, u32[]{:S(2)}, u32[]{:S(2)}) collective-permute-start(bf16[12,64,128]{2,1,0:T(8,128)(2,1)} %get-tuple-element.57), channel_id=1, source_target_pairs={{0,1},{1,0},{2,3},{3,2},{4,5},{5,4},{6,7},{7,6},{8,9},{9,8},{10,11... | collective-permute-start | bytes 589832 | tf_op jit(solution)/shard_map/ppermute | solution.py:271
  44.8 10.0 %collective-permute-done.6.rest_0_ = bf16[12,64,128]{2,1,0:T(8,128)(2,1)S(1)} collective-permute-done((bf16[12,64,128]{2,1,0:T(8,128)(2,1)}, bf16[12,64,128]{2,1,0:T(8,128)(2,1)S(1)}, u32[]{:S(2)}, u32[]{:S(2)}) %collective-permute-start.6) | collective-permute-done | bytes 196640 | tf_op jit(solution)/shard_map/ppermute | solution.py:271
  54.8 4.5 %collective-permute-start.14 = (bf16[12,64,128]{2,1,0:T(8,128)(2,1)}, bf16[12,64,128]{2,1,0:T(8,128)(2,1)}, u32[]{:S(2)}, u32[]{:S(2)}) collective-permute-start(bf16[12,64,128]{2,1,0:T(8,128)(2,1)} %get-tuple-element.61), channel_id=1, source_target_pairs={{0,10},{1,11},{2,12},{3,13},{4,14},{5,15},{6,0},{7,1},{8,2},{9,3},... | collective-permute-start | bytes 589832 | tf_op jit(solution)/shard_map/ppermute | solution.py:271
  59.3 2.0 %totals.1 = bf16[16,16,128]{2,1,0:T(8,128)(2,1)S(1)} custom-call(f32[4,128,1024]{2,1,0:T(8,128)S(1)} %copy-done, f32[4,128,1024]{2,1,0:T(8,128)S(1)} %copy-done.1, f32[4,1024,128]{2,1,0:T(8,128)S(1)} %copy-done.2, f32[4,128]{1,0:T(4,128)S(1)} %bitcast.5, f32[1,128]{1,0:T(1,128)S(1)} %bitcast.6), custom_call_target="tpu_custom_call" | custom-call | tf_op jit(solution)/shard_map/totals/pallas_call | solution.py:254
  61.3 13.0 %all_to_all.10.table = bf16[16,16,128]{2,1,0:T(8,128)(2,1)S(1)} all-to-all(bf16[16,16,128]{2,1,0:T(8,128)(2,1)S(1)} %totals.1), channel_id=1, replica_groups=mesh['owner'=16,'rows'=16] {'rows'}, dimensions={0} | all-to-all | bytes 131072 | tf_op jit(solution)/shard_map/all_to_all | solution.py:272
  74.3 1.0 scales.1
  75.3 6.8 %all-to-all-start.1 = ((bf16[16,4,2048]{2,1,0:T(4,128)(2,1)}), bf16[16,4,2048]{2,1,0:T(4,128)(2,1)S(1)}, u32[]{:S(2)}, u32[]{:S(2)}) async-start(bf16[16,4,2048]{2,1,0:T(4,128)(2,1)} %get-tuple-element.51), calls=%async_computation.1 | async-start | bytes 524288 | tf_op jit(solution)/shard_map/all_to_all | solution.py:287
  82.1 3.5 %collective-permute-start.3 = (bf16[12,64,128]{2,1,0:T(8,128)(2,1)}, bf16[12,64,128]{2,1,0:T(8,128)(2,1)S(1)}, u32[]{:S(2)}, u32[]{:S(2)}) collective-permute-start(bf16[12,64,128]{2,1,0:T(8,128)(2,1)} %get-tuple-element.48), channel_id=1, source_target_pairs={{0,13},{1,12},{2,15},{3,14},{4,1},{5,0},{6,3},{7,2},{8,5},{9,4},{1... | collective-permute-start | bytes 589832 | tf_op jit(solution)/shard_map/ppermute | solution.py:271
  86.8 2.1 %collective-permute-start.5 = (bf16[12,64,128]{2,1,0:T(8,128)(2,1)}, bf16[12,64,128]{2,1,0:T(8,128)(2,1)S(1)}, u32[]{:S(2)}, u32[]{:S(2)}) collective-permute-start(bf16[12,64,128]{2,1,0:T(8,128)(2,1)} %get-tuple-element.50), channel_id=1, source_target_pairs={{0,14},{1,15},{2,0},{3,1},{4,2},{5,3},{6,4},{7,5},{8,6},{9,7},{10,... | collective-permute-start | bytes 589832 | tf_op jit(solution)/shard_map/ppermute | solution.py:271
  89.7 3.0 %collective-permute-start = (bf16[12,64,128]{2,1,0:T(8,128)(2,1)}, bf16[12,64,128]{2,1,0:T(8,128)(2,1)S(1)}, u32[]{:S(2)}, u32[]{:S(2)}) collective-permute-start(bf16[12,64,128]{2,1,0:T(8,128)(2,1)} %get-tuple-element.45), channel_id=1, source_target_pairs={{0,15},{1,14},{2,1},{3,0},{4,3},{5,2},{6,5},{7,4},{8,7},{9,6},{10,... | collective-permute-start | bytes 589832 | tf_op jit(solution)/shard_map/ppermute | solution.py:271
  92.6 0.9 copy-done.4
  93.5 0.9 copy-done.6
  94.5 0.9 copy-done.8
  95.4 3.0 %shard_map.110 = (bf16[4,64,2048]{2,1,0:T(8,128)(2,1)}, bf16[4,64,2048]{2,1,0:T(8,128)(2,1)}, bf16[4,64,2048]{2,1,0:T(8,128)(2,1)}) custom-call(f32[16,128,8]{2,1,0:T(8,128)S(1)} %get-tuple-element.44.factors, bf16[12,64,128]{2,1,0:T(8,128)(2,1)} %get-tuple-element.56.rest_0_, bf16[12,64,128]{2,1,0:T(8,128)(2,1)S(1)} %copy-done.6, ...), custom_call_target="tpu_custom_call" | custom-call | flops 60000000 | bytes 2400000 | tf_op jit(solution)/shard_map/pallas_call | solution.py:206
  98.4 1.5 %shard_map.111 = (bf16[4,64,2048]{2,1,0:T(8,128)(2,1)}, bf16[4,64,2048]{2,1,0:T(8,128)(2,1)}, bf16[4,64,2048]{2,1,0:T(8,128)(2,1)}) custom-call(f32[16,128,8]{2,1,0:T(8,128)S(1)} %get-tuple-element.44.factors, bf16[12,64,128]{2,1,0:T(8,128)(2,1)S(1)} %collective-permute-done.6.rest_0_, ...), custom_call_target="tpu_custom_call", output_to_operand_aliasing={{0}: (5, {}), {1}: (6, {}), {2}: (7, {})} | custom-call | flops 40000000 | bytes 1600000 | tf_op jit(solution)/shard_map/pallas_call | solution.py:206
  100.1 2.2 %shard_map.112 = (bf16[4,64,2048]{2,1,0:T(8,128)(2,1)}, bf16[4,64,2048]{2,1,0:T(8,128)(2,1)}, bf16[4,64,2048]{2,1,0:T(8,128)(2,1)}, bf16[64,2048]{1,0:T(8,128)(2,1)}) custom-call(f32[16,128,8]{2,1,0:T(8,128)S(1)} %get-tuple-element.44.factors, ...), custom_call_target="tpu_custom_call", output_to_operand_aliasing={{0}: (6, {}), {1}: (7, {}), {2}: (8, {})} | custom-call | flops 40000000 | bytes 1600000 | tf_op jit(solution)/shard_map/pallas_call | solution.py:206
  103.2 1.0 collective-permute-done.rest_0_
  (40 shorter events, 5.3 us)
Async XLA Ops:
  2.9 20.0 %collective-permute-start.11 = (bf16[12,64,128]{2,1,0:T(8,128)(2,1)}, bf16[12,64,128]{2,1,0:T(8,128)(2,1)S(1)}, u32[]{:S(2)}, u32[]{:S(2)}) collective-permute-start(bf16[12,64,128]{2,1,0:T(8,128)(2,1)} %get-tuple-element.58), channel_id=1, source_target_pairs={{0,8},{1,9},{2,10},{3,11},{4,12},{5,13},{6,14},{7,15},{8,0},{9,1},... | collective-permute-start | bytes 589832 | tf_op jit(solution)/shard_map/ppermute | solution.py:271
  10.7 48.6 %copy-start = (f32[4,128,1024]{2,1,0:T(8,128)S(1)}, f32[4,128,1024]{2,1,0:T(8,128)}, u32[]{:S(2)}) copy-start(f32[4,128,1024]{2,1,0:T(8,128)} %gate.5) | copy-start | bytes 6291460
  10.7 48.6 %copy-start.1 = (f32[4,128,1024]{2,1,0:T(8,128)S(1)}, f32[4,128,1024]{2,1,0:T(8,128)}, u32[]{:S(2)}) copy-start(f32[4,128,1024]{2,1,0:T(8,128)} %up.5) | copy-start | bytes 6291460
  10.7 48.6 %copy-start.2 = (f32[4,1024,128]{2,1,0:T(8,128)S(1)}, f32[4,1024,128]{2,1,0:T(8,128)}, u32[]{:S(2)}) copy-start(f32[4,1024,128]{2,1,0:T(8,128)} %down.5) | copy-start | bytes 6291460
  10.7 48.6 %copy-start.9 = (f32[128,4]{0,1:T(4,128)S(1)}, f32[128,4]{0,1:T(4,128)}, u32[]{:S(2)}) copy-start(f32[128,4]{0,1:T(4,128)} %param.8) | copy-start | bytes 6148
  10.7 48.6 %copy-start.10 = (f32[128]{0:T(128)S(1)}, f32[128]{0:T(128)}, u32[]{:S(2)}) copy-start(f32[128]{0:T(128)} %param.9) | copy-start | bytes 1540
  10.8 15.7 %collective-permute-start.12 = (bf16[12,64,128]{2,1,0:T(8,128)(2,1)}, bf16[12,64,128]{2,1,0:T(8,128)(2,1)S(1)}, u32[]{:S(2)}, u32[]{:S(2)}) collective-permute-start(bf16[12,64,128]{2,1,0:T(8,128)(2,1)} %get-tuple-element.59), channel_id=1, source_target_pairs={{0,9},{1,8},{2,11},{3,10},{4,13},{5,12},{6,15},{7,14},{8,1},{9,0},... | collective-permute-start | bytes 589832 | tf_op jit(solution)/shard_map/ppermute | solution.py:271
  17.2 17.6 %collective-permute-start.2 = (bf16[12,64,128]{2,1,0:T(8,128)(2,1)}, bf16[12,64,128]{2,1,0:T(8,128)(2,1)S(1)}, u32[]{:S(2)}, u32[]{:S(2)}) collective-permute-start(bf16[12,64,128]{2,1,0:T(8,128)(2,1)} %get-tuple-element.47), channel_id=1, source_target_pairs={{0,5},{1,4},{2,7},{3,6},{4,9},{5,8},{6,11},{7,10},{8,13},{9,12},{1... | collective-permute-start | bytes 589832 | tf_op jit(solution)/shard_map/ppermute | solution.py:271
  17.9 36.9 %collective-permute-start.6 = (bf16[12,64,128]{2,1,0:T(8,128)(2,1)}, bf16[12,64,128]{2,1,0:T(8,128)(2,1)S(1)}, u32[]{:S(2)}, u32[]{:S(2)}) collective-permute-start(bf16[12,64,128]{2,1,0:T(8,128)(2,1)} %get-tuple-element.52), channel_id=1, source_target_pairs={{0,7},{1,6},{2,9},{3,8},{4,11},{5,10},{6,13},{7,12},{8,15},{9,14},... | collective-permute-start | bytes 589832 | tf_op jit(solution)/shard_map/ppermute | solution.py:271
  22.9 31.9 %collective-permute-start.7 = (bf16[12,64,128]{2,1,0:T(8,128)(2,1)}, bf16[12,64,128]{2,1,0:T(8,128)(2,1)S(1)}, u32[]{:S(2)}, u32[]{:S(2)}) collective-permute-start(bf16[12,64,128]{2,1,0:T(8,128)(2,1)} %get-tuple-element.53), channel_id=1, source_target_pairs={{0,11},{1,10},{2,13},{3,12},{4,15},{5,14},{6,1},{7,0},{8,3},{9,2},... | collective-permute-start | bytes 589832 | tf_op jit(solution)/shard_map/ppermute | solution.py:271
  23.0 59.1 %collective-permute-start.8 = (bf16[12,64,128]{2,1,0:T(8,128)(2,1)}, bf16[12,64,128]{2,1,0:T(8,128)(2,1)S(1)}, u32[]{:S(2)}, u32[]{:S(2)}) collective-permute-start(bf16[12,64,128]{2,1,0:T(8,128)(2,1)} %get-tuple-element.54), channel_id=1, source_target_pairs={{0,4},{1,5},{2,6},{3,7},{4,8},{5,9},{6,10},{7,11},{8,12},{9,13},{1... | collective-permute-start | bytes 589832 | tf_op jit(solution)/shard_map/ppermute | solution.py:271
  27.1 58.5 %collective-permute-start.9 = (bf16[12,64,128]{2,1,0:T(8,128)(2,1)}, bf16[12,64,128]{2,1,0:T(8,128)(2,1)S(1)}, u32[]{:S(2)}, u32[]{:S(2)}) collective-permute-start(bf16[12,64,128]{2,1,0:T(8,128)(2,1)} %get-tuple-element.55), channel_id=1, source_target_pairs={{0,12},{1,13},{2,14},{3,15},{4,0},{5,1},{6,2},{7,3},{8,4},{9,5},{1... | collective-permute-start | bytes 589832 | tf_op jit(solution)/shard_map/ppermute | solution.py:271
  34.8 51.3 %collective-permute-start.10 = (bf16[12,64,128]{2,1,0:T(8,128)(2,1)}, bf16[12,64,128]{2,1,0:T(8,128)(2,1)S(1)}, u32[]{:S(2)}, u32[]{:S(2)}) collective-permute-start(bf16[12,64,128]{2,1,0:T(8,128)(2,1)} %get-tuple-element.57), channel_id=1, source_target_pairs={{0,1},{1,0},{2,3},{3,2},{4,5},{5,4},{6,7},{7,6},{8,9},{9,8},{10,11... | collective-permute-start | bytes 589832 | tf_op jit(solution)/shard_map/ppermute | solution.py:271
  54.8 34.1 %collective-permute-start.13 = (bf16[12,64,128]{2,1,0:T(8,128)(2,1)}, bf16[12,64,128]{2,1,0:T(8,128)(2,1)S(1)}, u32[]{:S(2)}, u32[]{:S(2)}) collective-permute-start(bf16[12,64,128]{2,1,0:T(8,128)(2,1)} %get-tuple-element.60), channel_id=1, source_target_pairs={{0,6},{1,7},{2,8},{3,9},{4,10},{5,11},{6,12},{7,13},{8,14},{9,15},... | collective-permute-start | bytes 589832 | tf_op jit(solution)/shard_map/ppermute | solution.py:271
  54.8 34.8 %collective-permute-start.14 = (bf16[12,64,128]{2,1,0:T(8,128)(2,1)}, bf16[12,64,128]{2,1,0:T(8,128)(2,1)}, u32[]{:S(2)}, u32[]{:S(2)}) collective-permute-start(bf16[12,64,128]{2,1,0:T(8,128)(2,1)} %get-tuple-element.61), channel_id=1, source_target_pairs={{0,10},{1,11},{2,12},{3,13},{4,14},{5,15},{6,0},{7,1},{8,2},{9,3},... | collective-permute-start | bytes 589832 | tf_op jit(solution)/shard_map/ppermute | solution.py:271
  75.3 24.7 %all-to-all-start.1 = ((bf16[16,4,2048]{2,1,0:T(4,128)(2,1)}), bf16[16,4,2048]{2,1,0:T(4,128)(2,1)S(1)}, u32[]{:S(2)}, u32[]{:S(2)}) async-start(bf16[16,4,2048]{2,1,0:T(4,128)(2,1)} %get-tuple-element.51), calls=%async_computation.1 | async-start | bytes 524288 | tf_op jit(solution)/shard_map/all_to_all | solution.py:287
  82.1 17.8 %collective-permute-start.3 = (bf16[12,64,128]{2,1,0:T(8,128)(2,1)}, bf16[12,64,128]{2,1,0:T(8,128)(2,1)S(1)}, u32[]{:S(2)}, u32[]{:S(2)}) collective-permute-start(bf16[12,64,128]{2,1,0:T(8,128)(2,1)} %get-tuple-element.48), channel_id=1, source_target_pairs={{0,13},{1,12},{2,15},{3,14},{4,1},{5,0},{6,3},{7,2},{8,5},{9,4},{1... | collective-permute-start | bytes 589832 | tf_op jit(solution)/shard_map/ppermute | solution.py:271
  85.6 14.3 %collective-permute-start.4 = (bf16[12,64,128]{2,1,0:T(8,128)(2,1)}, bf16[12,64,128]{2,1,0:T(8,128)(2,1)S(1)}, u32[]{:S(2)}, u32[]{:S(2)}) collective-permute-start(bf16[12,64,128]{2,1,0:T(8,128)(2,1)} %get-tuple-element.49), channel_id=1, source_target_pairs={{0,2},{1,3},{2,4},{3,5},{4,6},{5,7},{6,8},{7,9},{8,10},{9,11},{10,... | collective-permute-start | bytes 589832 | tf_op jit(solution)/shard_map/ppermute | solution.py:271
  86.8 13.2 %collective-permute-start.5 = (bf16[12,64,128]{2,1,0:T(8,128)(2,1)}, bf16[12,64,128]{2,1,0:T(8,128)(2,1)S(1)}, u32[]{:S(2)}, u32[]{:S(2)}) collective-permute-start(bf16[12,64,128]{2,1,0:T(8,128)(2,1)} %get-tuple-element.50), channel_id=1, source_target_pairs={{0,14},{1,15},{2,0},{3,1},{4,2},{5,3},{6,4},{7,5},{8,6},{9,7},{10,... | collective-permute-start | bytes 589832 | tf_op jit(solution)/shard_map/ppermute | solution.py:271
  89.6 12.7 %collective-permute-start.1 = (bf16[12,64,128]{2,1,0:T(8,128)(2,1)}, bf16[12,64,128]{2,1,0:T(8,128)(2,1)S(1)}, u32[]{:S(2)}, u32[]{:S(2)}) collective-permute-start(bf16[12,64,128]{2,1,0:T(8,128)(2,1)} %get-tuple-element.46), channel_id=1, source_target_pairs={{0,3},{1,2},{2,5},{3,4},{4,7},{5,6},{6,9},{7,8},{8,11},{9,10},{10,... | collective-permute-start | bytes 589832 | tf_op jit(solution)/shard_map/ppermute | solution.py:271
  89.7 14.6 %collective-permute-start = (bf16[12,64,128]{2,1,0:T(8,128)(2,1)}, bf16[12,64,128]{2,1,0:T(8,128)(2,1)S(1)}, u32[]{:S(2)}, u32[]{:S(2)}) collective-permute-start(bf16[12,64,128]{2,1,0:T(8,128)(2,1)} %get-tuple-element.45), channel_id=1, source_target_pairs={{0,15},{1,14},{2,1},{3,0},{4,3},{5,2},{6,5},{7,4},{8,7},{9,6},{10,... | collective-permute-start | bytes 589832 | tf_op jit(solution)/shard_map/ppermute | solution.py:271
  92.6 0.9 copy-start.4
  93.5 0.9 copy-start.6
  94.5 0.9 copy-start.8
  (3 other events, 2.0 us)

commit v6 on v5

--- a/solution.py
+++ b/solution.py
@@ -21,7 +21,7 @@
 FIRST = (4,)
 REST = (3, -3, 2, -2, 1, -1, 0)
 ORDER = (
-    (4, 0), (4, 1), (3, 0), (-3, 0), (3, 1), (-3, 1), (0, 1), (2, 0), (-2, 0), (2, 1), (-2, 1), (1, 0), (-1, 0), (1, 1), (-1, 1),
+    (4, 0), (4, 1), (2, 0), (-2, 0), (0, 1), (1, 0), (-1, 0), (3, 0), (-3, 0), (1, 1), (-1, 1), (2, 1), (-2, 1), (3, 1), (-3, 1),
 )
 
 
@@ -221,11 +221,11 @@
 
 
 GROUPS = (
-    ((0, 0), (0, 1), (4, 0), (4, 1), (3, 0), (-3, 0),),
-    ((3, 1), (-3, 1), (2, 0), (-2, 0),),
-    ((2, 1), (-2, 1), (1, 0), (-1, 0),),
-    ((1, 1),),
-    ((-1, 1),),
+    ((0, 0), (0, 1), (4, 0), (4, 1), (2, 0), (-2, 0),),
+    ((1, 0), (-1, 0), (3, 0), (-3, 0),),
+    ((1, 1), (-1, 1), (2, 1), (-2, 1),),
+    ((3, 1),),
+    ((-3, 1),),
 )
 
 

time: 106 us -> 99.7 us (0.941)
  starting transfers between devices: 56.2 us -> 45.4 us
  blocking collectives: 13 us -> 20.7 us
  waiting for transfers between devices: 11.3 us -> 8.45 us
    ppermute x15, starting transfers between devices: 49.5 us -> 38.6 us  [local(): got[dz, dc] = lax.ppermute(sent[dz, dc], 'rows', pairs_of(dz, dc))]
    all_to_all x1, blocking collectives: 13 us -> 20.7 us  [local(): table = lax.all_to_all(table, 'rows', 0, 0, tiled=True)]
    ppermute x15, waiting for transfers between devices: 11.3 us -> 8.45 us  [local(): got[dz, dc] = lax.ppermute(sent[dz, dc], 'rows', pairs_of(dz, dc))]
  transfers between devices with their start and end apart: 16 -> 16, of which waited for: 3 -> 4; matrix products, arithmetic and copies ran while one was open for 0% -> 0% of each run, Pallas kernels for 15% -> 16%
where the time goes in v6:
time: 99.7 us; the launch traced here: 99.4 us
  starting transfers between devices  45.4 us (46%)
  blocking collectives  20.7 us (21%)
  Pallas kernels  19.1 us (19%)
  waiting for transfers between devices  8.45 us (8%)
  local copies, waits for them, and re-layouts  4.82 us (5%)
    ppermute x15, starting transfers between devices, local(): got[dz, dc] = lax.ppermute(sent[dz, dc], 'rows', pairs_of(dz, dc))  38.6 us
    all_to_all x1, blocking collectives, local(): table = lax.all_to_all(table, 'rows', 0, 0, tiled=True)  20.7 us
    pallas_call x5, Pallas kernels, decode(): pl.pallas_call(functools.partial(decode_kernel, where, len(before), wide...  8.52 us
    ppermute x15, waiting for transfers between devices, local(): got[dz, dc] = lax.ppermute(sent[dz, dc], 'rows', pairs_of(dz, dc))  8.45 us
    pallas_call x2, Pallas kernels, coded(): pl.pallas_call(functools.partial(code_kernel, dzs), out_shape=(PIECE,) *...  7.57 us
    all_to_all x1, starting transfers between devices, local(): wide = lax.all_to_all(rows, 'owner', 0, 0, tiled=True)  6.75 us
    unnamed x22, local copies, waits for them, and re-layouts  4.82 us
  transfers between devices with their start and end apart: 16, of which 4 were waited for; matrix products, arithmetic and copies ran while one was open for 0% of the time, Pallas kernels for 16%

profile of v6, /device:TPU:1, one launch (start us, length us, event | category | flops | bytes accessed | tf_op | source)
XLA Modules:
  0.0 99.4 jit_solution(11438686727595266937)
XLA Ops:
  0.6 2.3 %shard_map.109 = (bf16[12,64,128]{2,1,0:T(8,128)(2,1)}, bf16[12,64,128]{2,1,0:T(8,128)(2,1)}) custom-call(f32[4,128,1024]{2,1,0:T(8,128)} %gate.5, f32[4,128,1024]{2,1,0:T(8,128)} %up.5, f32[4,1024,128]{2,1,0:T(8,128)} %down.5), custom_call_target="tpu_custom_call" | custom-call | tf_op jit(solution)/shard_map/pallas_call | solution.py:237
  2.9 7.8 %collective-permute-start.11 = (bf16[12,64,128]{2,1,0:T(8,128)(2,1)}, bf16[12,64,128]{2,1,0:T(8,128)(2,1)S(1)}, u32[]{:S(2)}, u32[]{:S(2)}) collective-permute-start(bf16[12,64,128]{2,1,0:T(8,128)(2,1)} %get-tuple-element.58), channel_id=1, source_target_pairs={{0,8},{1,9},{2,10},{3,11},{4,12},{5,13},{6,14},{7,15},{8,0},{9,1},... | collective-permute-start | bytes 589832 | tf_op jit(solution)/shard_map/ppermute | solution.py:271
  10.8 1.1 %collective-permute-start.12 = (bf16[12,64,128]{2,1,0:T(8,128)(2,1)}, bf16[12,64,128]{2,1,0:T(8,128)(2,1)S(1)}, u32[]{:S(2)}, u32[]{:S(2)}) collective-permute-start(bf16[12,64,128]{2,1,0:T(8,128)(2,1)} %get-tuple-element.59), channel_id=1, source_target_pairs={{0,9},{1,8},{2,11},{3,10},{4,13},{5,12},{6,15},{7,14},{8,1},{9,0},... | collective-permute-start | bytes 589832 | tf_op jit(solution)/shard_map/ppermute | solution.py:271
  11.9 5.3 %shard_map.108 = (bf16[12,64,128]{2,1,0:T(8,128)(2,1)}, bf16[12,64,128]{2,1,0:T(8,128)(2,1)}, bf16[12,64,128]{2,1,0:T(8,128)(2,1)}, bf16[12,64,128]{2,1,0:T(8,12...) custom-call(f32[4,128,1024]{2,1,0:T(8,128)} %gate.5, ...), custom_call_target="tpu_custom_call" | custom-call | tf_op jit(solution)/shard_map/pallas_call | solution.py:237
  18.2 2.6 %collective-permute-start.7 = (bf16[12,64,128]{2,1,0:T(8,128)(2,1)}, bf16[12,64,128]{2,1,0:T(8,128)(2,1)S(1)}, u32[]{:S(2)}, u32[]{:S(2)}) collective-permute-start(bf16[12,64,128]{2,1,0:T(8,128)(2,1)} %get-tuple-element.53), channel_id=1, source_target_pairs={{0,14},{1,15},{2,0},{3,1},{4,2},{5,3},{6,4},{7,5},{8,6},{9,7},{10,... | collective-permute-start | bytes 589832 | tf_op jit(solution)/shard_map/ppermute | solution.py:271
  20.8 2.3 %collective-permute-start.8 = (bf16[12,64,128]{2,1,0:T(8,128)(2,1)}, bf16[12,64,128]{2,1,0:T(8,128)(2,1)S(1)}, u32[]{:S(2)}, u32[]{:S(2)}) collective-permute-start(bf16[12,64,128]{2,1,0:T(8,128)(2,1)} %get-tuple-element.54), channel_id=1, source_target_pairs={{0,6},{1,7},{2,8},{3,9},{4,10},{5,11},{6,12},{7,13},{8,14},{9,15},... | collective-permute-start | bytes 589832 | tf_op jit(solution)/shard_map/ppermute | solution.py:271
  23.1 1.0 collective-permute-done.12.rest_3_
  24.7 10.8 %collective-permute-start.9 = (bf16[12,64,128]{2,1,0:T(8,128)(2,1)}, bf16[12,64,128]{2,1,0:T(8,128)(2,1)S(1)}, u32[]{:S(2)}, u32[]{:S(2)}) collective-permute-start(bf16[12,64,128]{2,1,0:T(8,128)(2,1)} %get-tuple-element.55), channel_id=1, source_target_pairs={{0,10},{1,11},{2,12},{3,13},{4,14},{5,15},{6,0},{7,1},{8,2},{9,3},... | collective-permute-start | bytes 589832 | tf_op jit(solution)/shard_map/ppermute | solution.py:271
  35.5 2.0 %collective-permute-done.6.rest_0_ = bf16[12,64,128]{2,1,0:T(8,128)(2,1)S(1)} collective-permute-done((bf16[12,64,128]{2,1,0:T(8,128)(2,1)}, bf16[12,64,128]{2,1,0:T(8,128)(2,1)S(1)}, u32[]{:S(2)}, u32[]{:S(2)}) %collective-permute-start.6) | collective-permute-done | bytes 196640 | tf_op jit(solution)/shard_map/ppermute | solution.py:271
  37.5 2.0 %collective-permute-start.13 = (bf16[12,64,128]{2,1,0:T(8,128)(2,1)}, bf16[12,64,128]{2,1,0:T(8,128)(2,1)S(1)}, u32[]{:S(2)}, u32[]{:S(2)}) collective-permute-start(bf16[12,64,128]{2,1,0:T(8,128)(2,1)} %get-tuple-element.60), channel_id=1, source_target_pairs={{0,4},{1,5},{2,6},{3,7},{4,8},{5,9},{6,10},{7,11},{8,12},{9,13},{1... | collective-permute-start | bytes 589832 | tf_op jit(solution)/shard_map/ppermute | solution.py:271
  39.4 1.6 %collective-permute-start.14 = (bf16[12,64,128]{2,1,0:T(8,128)(2,1)}, bf16[12,64,128]{2,1,0:T(8,128)(2,1)}, u32[]{:S(2)}, u32[]{:S(2)}) collective-permute-start(bf16[12,64,128]{2,1,0:T(8,128)(2,1)} %get-tuple-element.61), channel_id=1, source_target_pairs={{0,12},{1,13},{2,14},{3,15},{4,0},{5,1},{6,2},{7,3},{8,4},{9,5},{1... | collective-permute-start | bytes 589832 | tf_op jit(solution)/shard_map/ppermute | solution.py:271
  41.1 2.0 %totals.1 = bf16[16,16,128]{2,1,0:T(8,128)(2,1)S(1)} custom-call(f32[4,128,1024]{2,1,0:T(8,128)S(1)} %copy-done, f32[4,128,1024]{2,1,0:T(8,128)S(1)} %copy-done.1, f32[4,1024,128]{2,1,0:T(8,128)S(1)} %copy-done.2, f32[4,128]{1,0:T(4,128)S(1)} %bitcast.5, f32[1,128]{1,0:T(1,128)S(1)} %bitcast.6), custom_call_target="tpu_custom_call" | custom-call | tf_op jit(solution)/shard_map/totals/pallas_call | solution.py:254
  43.1 20.7 %all_to_all.10.table = bf16[16,16,128]{2,1,0:T(8,128)(2,1)S(1)} all-to-all(bf16[16,16,128]{2,1,0:T(8,128)(2,1)S(1)} %totals.1), channel_id=1, replica_groups=mesh['owner'=16,'rows'=16] {'rows'}, dimensions={0} | all-to-all | bytes 131072 | tf_op jit(solution)/shard_map/all_to_all | solution.py:272
  63.8 1.0 %scales.1 = (f32[4,64]{1,0:T(4,128)}, f32[4,64]{1,0:T(4,128)}, f32[4,64]{1,0:T(4,128)}, f32[16,128,8]{2,1,0:T(8,128)S(1)}, bf16[16,4,2048]{2,1,0:T(4,128)(2,1)}) custom-call(bf16[16,16,128]{2,1,0:T(8,128)(2,1)S(1)} %all_to_all.10.table), custom_call_target="tpu_custom_call" | custom-call | tf_op jit(solution)/shard_map/scales/pallas_call | solution.py:274
  64.8 6.8 %all-to-all-start.1 = ((bf16[16,4,2048]{2,1,0:T(4,128)(2,1)}), bf16[16,4,2048]{2,1,0:T(4,128)(2,1)S(1)}, u32[]{:S(2)}, u32[]{:S(2)}) async-start(bf16[16,4,2048]{2,1,0:T(4,128)(2,1)} %get-tuple-element.51), calls=%async_computation.1 | async-start | bytes 524288 | tf_op jit(solution)/shard_map/all_to_all | solution.py:287
  73.1 3.8 %collective-permute-start.5 = (bf16[12,64,128]{2,1,0:T(8,128)(2,1)}, bf16[12,64,128]{2,1,0:T(8,128)(2,1)S(1)}, u32[]{:S(2)}, u32[]{:S(2)}) collective-permute-start(bf16[12,64,128]{2,1,0:T(8,128)(2,1)} %get-tuple-element.50), channel_id=1, source_target_pairs={{0,13},{1,12},{2,15},{3,14},{4,1},{5,0},{6,3},{7,2},{8,5},{9,4},{1... | collective-permute-start | bytes 589832 | tf_op jit(solution)/shard_map/ppermute | solution.py:271
  77.6 4.8 %collective-permute-start = (bf16[12,64,128]{2,1,0:T(8,128)(2,1)}, bf16[12,64,128]{2,1,0:T(8,128)(2,1)S(1)}, u32[]{:S(2)}, u32[]{:S(2)}) collective-permute-start(bf16[12,64,128]{2,1,0:T(8,128)(2,1)} %get-tuple-element.45), channel_id=1, source_target_pairs={{0,11},{1,10},{2,13},{3,12},{4,15},{5,14},{6,1},{7,0},{8,3},{9,2},... | collective-permute-start | bytes 589832 | tf_op jit(solution)/shard_map/ppermute | solution.py:271
  82.4 0.9 copy-done.4
  83.3 0.9 copy-done.6
  84.2 0.9 copy-done.8
  85.2 3.0 %shard_map.110 = (bf16[4,64,2048]{2,1,0:T(8,128)(2,1)}, bf16[4,64,2048]{2,1,0:T(8,128)(2,1)}, bf16[4,64,2048]{2,1,0:T(8,128)(2,1)}) custom-call(f32[16,128,8]{2,1,0:T(8,128)S(1)} %get-tuple-element.44.factors, bf16[12,64,128]{2,1,0:T(8,128)(2,1)} %get-tuple-element.56.rest_0_, bf16[12,64,128]{2,1,0:T(8,128)(2,1)S(1)} %copy-done.6, ...), custom_call_target="tpu_custom_call" | custom-call | flops 60000000 | bytes 2400000 | tf_op jit(solution)/shard_map/pallas_call | solution.py:206
  88.1 1.5 %shard_map.111 = (bf16[4,64,2048]{2,1,0:T(8,128)(2,1)}, bf16[4,64,2048]{2,1,0:T(8,128)(2,1)}, bf16[4,64,2048]{2,1,0:T(8,128)(2,1)}) custom-call(f32[16,128,8]{2,1,0:T(8,128)S(1)} %get-tuple-element.44.factors, bf16[12,64,128]{2,1,0:T(8,128)(2,1)S(1)} %collective-permute-done.6.rest_0_, ...), custom_call_target="tpu_custom_call", output_to_operand_aliasing={{0}: (5, {}), {1}: (6, {}), {2}: (7, {})} | custom-call | flops 40000000 | bytes 1600000 | tf_op jit(solution)/shard_map/pallas_call | solution.py:206
  89.7 2.3 %shard_map.112 = (bf16[4,64,2048]{2,1,0:T(8,128)(2,1)}, bf16[4,64,2048]{2,1,0:T(8,128)(2,1)}, bf16[4,64,2048]{2,1,0:T(8,128)(2,1)}, bf16[64,2048]{1,0:T(8,128)(2,1)}) custom-call(f32[16,128,8]{2,1,0:T(8,128)S(1)} %get-tuple-element.44.factors, ...), custom_call_target="tpu_custom_call", output_to_operand_aliasing={{0}: (6, {}), {1}: (7, {}), {2}: (8, {})} | custom-call | flops 40000000 | bytes 1600000 | tf_op jit(solution)/shard_map/pallas_call | solution.py:206
  92.0 5.2 %collective-permute-done.1.rest_0_ = bf16[12,64,128]{2,1,0:T(8,128)(2,1)S(1)} collective-permute-done((bf16[12,64,128]{2,1,0:T(8,128)(2,1)}, bf16[12,64,128]{2,1,0:T(8,128)(2,1)S(1)}, u32[]{:S(2)}, u32[]{:S(2)}) %collective-permute-start.1) | collective-permute-done | bytes 196640 | tf_op jit(solution)/shard_map/ppermute | solution.py:271
  (40 shorter events, 6.1 us)
Async XLA Ops:
  2.9 17.8 %collective-permute-start.11 = (bf16[12,64,128]{2,1,0:T(8,128)(2,1)}, bf16[12,64,128]{2,1,0:T(8,128)(2,1)S(1)}, u32[]{:S(2)}, u32[]{:S(2)}) collective-permute-start(bf16[12,64,128]{2,1,0:T(8,128)(2,1)} %get-tuple-element.58), channel_id=1, source_target_pairs={{0,8},{1,9},{2,10},{3,11},{4,12},{5,13},{6,14},{7,15},{8,0},{9,1},... | collective-permute-start | bytes 589832 | tf_op jit(solution)/shard_map/ppermute | solution.py:271
  10.7 30.3 %copy-start = (f32[4,128,1024]{2,1,0:T(8,128)S(1)}, f32[4,128,1024]{2,1,0:T(8,128)}, u32[]{:S(2)}) copy-start(f32[4,128,1024]{2,1,0:T(8,128)} %gate.5) | copy-start | bytes 6291460
  10.7 30.3 %copy-start.1 = (f32[4,128,1024]{2,1,0:T(8,128)S(1)}, f32[4,128,1024]{2,1,0:T(8,128)}, u32[]{:S(2)}) copy-start(f32[4,128,1024]{2,1,0:T(8,128)} %up.5) | copy-start | bytes 6291460
  10.7 30.3 %copy-start.2 = (f32[4,1024,128]{2,1,0:T(8,128)S(1)}, f32[4,1024,128]{2,1,0:T(8,128)}, u32[]{:S(2)}) copy-start(f32[4,1024,128]{2,1,0:T(8,128)} %down.5) | copy-start | bytes 6291460
  10.7 30.3 %copy-start.9 = (f32[128,4]{0,1:T(4,128)S(1)}, f32[128,4]{0,1:T(4,128)}, u32[]{:S(2)}) copy-start(f32[128,4]{0,1:T(4,128)} %param.8) | copy-start | bytes 6148
  10.7 30.3 %copy-start.10 = (f32[128]{0:T(128)S(1)}, f32[128]{0:T(128)}, u32[]{:S(2)}) copy-start(f32[128]{0:T(128)} %param.9) | copy-start | bytes 1540
  10.8 13.3 %collective-permute-start.12 = (bf16[12,64,128]{2,1,0:T(8,128)(2,1)}, bf16[12,64,128]{2,1,0:T(8,128)(2,1)S(1)}, u32[]{:S(2)}, u32[]{:S(2)}) collective-permute-start(bf16[12,64,128]{2,1,0:T(8,128)(2,1)} %get-tuple-element.59), channel_id=1, source_target_pairs={{0,9},{1,8},{2,11},{3,10},{4,13},{5,12},{6,15},{7,14},{8,1},{9,0},... | collective-permute-start | bytes 589832 | tf_op jit(solution)/shard_map/ppermute | solution.py:271
  17.2 18.4 %collective-permute-start.2 = (bf16[12,64,128]{2,1,0:T(8,128)(2,1)}, bf16[12,64,128]{2,1,0:T(8,128)(2,1)S(1)}, u32[]{:S(2)}, u32[]{:S(2)}) collective-permute-start(bf16[12,64,128]{2,1,0:T(8,128)(2,1)} %get-tuple-element.47), channel_id=1, source_target_pairs={{0,3},{1,2},{2,5},{3,4},{4,7},{5,6},{6,9},{7,8},{8,11},{9,10},{10,... | collective-permute-start | bytes 589832 | tf_op jit(solution)/shard_map/ppermute | solution.py:271
  17.5 20.0 %collective-permute-start.6 = (bf16[12,64,128]{2,1,0:T(8,128)(2,1)}, bf16[12,64,128]{2,1,0:T(8,128)(2,1)S(1)}, u32[]{:S(2)}, u32[]{:S(2)}) collective-permute-start(bf16[12,64,128]{2,1,0:T(8,128)(2,1)} %get-tuple-element.52), channel_id=1, source_target_pairs={{0,2},{1,3},{2,4},{3,5},{4,6},{5,7},{6,8},{7,9},{8,10},{9,11},{10,... | collective-permute-start | bytes 589832 | tf_op jit(solution)/shard_map/ppermute | solution.py:271
  18.2 21.3 %collective-permute-start.7 = (bf16[12,64,128]{2,1,0:T(8,128)(2,1)}, bf16[12,64,128]{2,1,0:T(8,128)(2,1)S(1)}, u32[]{:S(2)}, u32[]{:S(2)}) collective-permute-start(bf16[12,64,128]{2,1,0:T(8,128)(2,1)} %get-tuple-element.53), channel_id=1, source_target_pairs={{0,14},{1,15},{2,0},{3,1},{4,2},{5,3},{6,4},{7,5},{8,6},{9,7},{10,... | collective-permute-start | bytes 589832 | tf_op jit(solution)/shard_map/ppermute | solution.py:271
  20.8 50.8 %collective-permute-start.8 = (bf16[12,64,128]{2,1,0:T(8,128)(2,1)}, bf16[12,64,128]{2,1,0:T(8,128)(2,1)S(1)}, u32[]{:S(2)}, u32[]{:S(2)}) collective-permute-start(bf16[12,64,128]{2,1,0:T(8,128)(2,1)} %get-tuple-element.54), channel_id=1, source_target_pairs={{0,6},{1,7},{2,8},{3,9},{4,10},{5,11},{6,12},{7,13},{8,14},{9,15},... | collective-permute-start | bytes 589832 | tf_op jit(solution)/shard_map/ppermute | solution.py:271
  24.7 47.7 %collective-permute-start.9 = (bf16[12,64,128]{2,1,0:T(8,128)(2,1)}, bf16[12,64,128]{2,1,0:T(8,128)(2,1)S(1)}, u32[]{:S(2)}, u32[]{:S(2)}) collective-permute-start(bf16[12,64,128]{2,1,0:T(8,128)(2,1)} %get-tuple-element.55), channel_id=1, source_target_pairs={{0,10},{1,11},{2,12},{3,13},{4,14},{5,15},{6,0},{7,1},{8,2},{9,3},... | collective-permute-start | bytes 589832 | tf_op jit(solution)/shard_map/ppermute | solution.py:271
  35.5 36.9 %collective-permute-start.10 = (bf16[12,64,128]{2,1,0:T(8,128)(2,1)}, bf16[12,64,128]{2,1,0:T(8,128)(2,1)S(1)}, u32[]{:S(2)}, u32[]{:S(2)}) collective-permute-start(bf16[12,64,128]{2,1,0:T(8,128)(2,1)} %get-tuple-element.57), channel_id=1, source_target_pairs={{0,1},{1,0},{2,3},{3,2},{4,5},{5,4},{6,7},{7,6},{8,9},{9,8},{10,11... | collective-permute-start | bytes 589832 | tf_op jit(solution)/shard_map/ppermute | solution.py:271
  37.5 39.5 %collective-permute-start.13 = (bf16[12,64,128]{2,1,0:T(8,128)(2,1)}, bf16[12,64,128]{2,1,0:T(8,128)(2,1)S(1)}, u32[]{:S(2)}, u32[]{:S(2)}) collective-permute-start(bf16[12,64,128]{2,1,0:T(8,128)(2,1)} %get-tuple-element.60), channel_id=1, source_target_pairs={{0,4},{1,5},{2,6},{3,7},{4,8},{5,9},{6,10},{7,11},{8,12},{9,13},{1... | collective-permute-start | bytes 589832 | tf_op jit(solution)/shard_map/ppermute | solution.py:271
  39.4 38.2 %collective-permute-start.14 = (bf16[12,64,128]{2,1,0:T(8,128)(2,1)}, bf16[12,64,128]{2,1,0:T(8,128)(2,1)}, u32[]{:S(2)}, u32[]{:S(2)}) collective-permute-start(bf16[12,64,128]{2,1,0:T(8,128)(2,1)} %get-tuple-element.61), channel_id=1, source_target_pairs={{0,12},{1,13},{2,14},{3,15},{4,0},{5,1},{6,2},{7,3},{8,4},{9,5},{1... | collective-permute-start | bytes 589832 | tf_op jit(solution)/shard_map/ppermute | solution.py:271
  64.8 24.9 %all-to-all-start.1 = ((bf16[16,4,2048]{2,1,0:T(4,128)(2,1)}), bf16[16,4,2048]{2,1,0:T(4,128)(2,1)S(1)}, u32[]{:S(2)}, u32[]{:S(2)}) async-start(bf16[16,4,2048]{2,1,0:T(4,128)(2,1)} %get-tuple-element.51), calls=%async_computation.1 | async-start | bytes 524288 | tf_op jit(solution)/shard_map/all_to_all | solution.py:287
  71.6 18.1 %collective-permute-start.3 = (bf16[12,64,128]{2,1,0:T(8,128)(2,1)}, bf16[12,64,128]{2,1,0:T(8,128)(2,1)S(1)}, u32[]{:S(2)}, u32[]{:S(2)}) collective-permute-start(bf16[12,64,128]{2,1,0:T(8,128)(2,1)} %get-tuple-element.48), channel_id=1, source_target_pairs={{0,15},{1,14},{2,1},{3,0},{4,3},{5,2},{6,5},{7,4},{8,7},{9,6},{10,... | collective-permute-start | bytes 589832 | tf_op jit(solution)/shard_map/ppermute | solution.py:271
  72.4 17.3 %collective-permute-start.4 = (bf16[12,64,128]{2,1,0:T(8,128)(2,1)}, bf16[12,64,128]{2,1,0:T(8,128)(2,1)S(1)}, u32[]{:S(2)}, u32[]{:S(2)}) collective-permute-start(bf16[12,64,128]{2,1,0:T(8,128)(2,1)} %get-tuple-element.49), channel_id=1, source_target_pairs={{0,5},{1,4},{2,7},{3,6},{4,9},{5,8},{6,11},{7,10},{8,13},{9,12},{1... | collective-permute-start | bytes 589832 | tf_op jit(solution)/shard_map/ppermute | solution.py:271
  73.1 16.6 %collective-permute-start.5 = (bf16[12,64,128]{2,1,0:T(8,128)(2,1)}, bf16[12,64,128]{2,1,0:T(8,128)(2,1)S(1)}, u32[]{:S(2)}, u32[]{:S(2)}) collective-permute-start(bf16[12,64,128]{2,1,0:T(8,128)(2,1)} %get-tuple-element.50), channel_id=1, source_target_pairs={{0,13},{1,12},{2,15},{3,14},{4,1},{5,0},{6,3},{7,2},{8,5},{9,4},{1... | collective-permute-start | bytes 589832 | tf_op jit(solution)/shard_map/ppermute | solution.py:271
  77.6 19.5 %collective-permute-start.1 = (bf16[12,64,128]{2,1,0:T(8,128)(2,1)}, bf16[12,64,128]{2,1,0:T(8,128)(2,1)S(1)}, u32[]{:S(2)}, u32[]{:S(2)}) collective-permute-start(bf16[12,64,128]{2,1,0:T(8,128)(2,1)} %get-tuple-element.46), channel_id=1, source_target_pairs={{0,7},{1,6},{2,9},{3,8},{4,11},{5,10},{6,13},{7,12},{8,15},{9,14},... | collective-permute-start | bytes 589832 | tf_op jit(solution)/shard_map/ppermute | solution.py:271
  77.6 20.7 %collective-permute-start = (bf16[12,64,128]{2,1,0:T(8,128)(2,1)}, bf16[12,64,128]{2,1,0:T(8,128)(2,1)S(1)}, u32[]{:S(2)}, u32[]{:S(2)}) collective-permute-start(bf16[12,64,128]{2,1,0:T(8,128)(2,1)} %get-tuple-element.45), channel_id=1, source_target_pairs={{0,11},{1,10},{2,13},{3,12},{4,15},{5,14},{6,1},{7,0},{8,3},{9,2},... | collective-permute-start | bytes 589832 | tf_op jit(solution)/shard_map/ppermute | solution.py:271
  82.4 0.9 copy-start.4
  83.3 0.9 copy-start.6
  84.2 0.9 copy-start.8
  (3 other events, 2.0 us)

commit v7 on v6

--- a/solution.py
+++ b/solution.py
@@ -21,7 +21,7 @@
 FIRST = (4,)
 REST = (3, -3, 2, -2, 1, -1, 0)
 ORDER = (
-    (4, 0), (4, 1), (2, 0), (-2, 0), (0, 1), (1, 0), (-1, 0), (3, 0), (-3, 0), (1, 1), (-1, 1), (2, 1), (-2, 1), (3, 1), (-3, 1),
+    (4, 0), (4, 1), (2, 0), (-2, 0), (0, 1), (1, 0), (-1, 0), (1, 1), (-1, 1), (2, 1), (-2, 1), (3, 0), (-3, 0), (3, 1), (-3, 1),
 )
 
 
@@ -222,8 +222,8 @@
 
 GROUPS = (
     ((0, 0), (0, 1), (4, 0), (4, 1), (2, 0), (-2, 0),),
-    ((1, 0), (-1, 0), (3, 0), (-3, 0),),
-    ((1, 1), (-1, 1), (2, 1), (-2, 1),),
+    ((1, 0), (-1, 0), (1, 1), (-1, 1),),
+    ((2, 1), (-2, 1), (3, 0), (-3, 0),),
     ((3, 1),),
     ((-3, 1),),
 )

time: 99.7 us -> 108 us (1.083)
  the two profiles are of different devices: /device:TPU:1 before, /device:TPU:35 now
where the time goes in v7:
time: 108 us
  starting transfers between devices  39.7 us (37%)
  waiting for transfers between devices  28.5 us (26%)
  Pallas kernels  19 us (18%)
  blocking collectives  15.1 us (14%)
  local copies, waits for them, and re-layouts  4.83 us (4%)
    ppermute x15, starting transfers between devices, local(): got[dz, dc] = lax.ppermute(sent[dz, dc], 'rows', pairs_of(dz, dc))  32.8 us
    ppermute x15, waiting for transfers between devices, local(): got[dz, dc] = lax.ppermute(sent[dz, dc], 'rows', pairs_of(dz, dc))  28.5 us
    all_to_all x1, blocking collectives, local(): table = lax.all_to_all(table, 'rows', 0, 0, tiled=True)  15.1 us
    pallas_call x5, Pallas kernels, decode(): pl.pallas_call(functools.partial(decode_kernel, where, len(before), wide...  8.52 us
    pallas_call x2, Pallas kernels, coded(): pl.pallas_call(functools.partial(code_kernel, dzs), out_shape=(PIECE,) *...  7.41 us
    all_to_all x1, starting transfers between devices, local(): wide = lax.all_to_all(rows, 'owner', 0, 0, tiled=True)  6.92 us
    unnamed x22, local copies, waits for them, and re-layouts  4.83 us
  transfers between devices with their start and end apart: 16, of which 5 were waited for; matrix products, arithmetic and copies ran while one was open for 0% of the time, Pallas kernels for 15%

profile of v7, /device:TPU:35, one launch (start us, length us, event | category | flops | bytes accessed | tf_op | source)
XLA Modules:
  0.0 108.0 jit_solution(10469532527951460367)
XLA Ops:
  0.6 2.3 %shard_map.109 = (bf16[12,64,128]{2,1,0:T(8,128)(2,1)}, bf16[12,64,128]{2,1,0:T(8,128)(2,1)}) custom-call(f32[4,128,1024]{2,1,0:T(8,128)} %gate.5, f32[4,128,1024]{2,1,0:T(8,128)} %up.5, f32[4,1024,128]{2,1,0:T(8,128)} %down.5), custom_call_target="tpu_custom_call" | custom-call | tf_op jit(solution)/shard_map/pallas_call | solution.py:237
  2.9 6.1 %collective-permute-start.11 = (bf16[12,64,128]{2,1,0:T(8,128)(2,1)}, bf16[12,64,128]{2,1,0:T(8,128)(2,1)S(1)}, u32[]{:S(2)}, u32[]{:S(2)}) collective-permute-start(bf16[12,64,128]{2,1,0:T(8,128)(2,1)} %get-tuple-element.58), channel_id=1, source_target_pairs={{0,8},{1,9},{2,10},{3,11},{4,12},{5,13},{6,14},{7,15},{8,0},{9,1},... | collective-permute-start | bytes 589832 | tf_op jit(solution)/shard_map/ppermute | solution.py:271
  9.7 5.1 %shard_map.108 = (bf16[12,64,128]{2,1,0:T(8,128)(2,1)}, bf16[12,64,128]{2,1,0:T(8,128)(2,1)}, bf16[12,64,128]{2,1,0:T(8,128)(2,1)}, bf16[12,64,128]{2,1,0:T(8,12...) custom-call(f32[4,128,1024]{2,1,0:T(8,128)} %gate.5, ...), custom_call_target="tpu_custom_call" | custom-call | tf_op jit(solution)/shard_map/pallas_call | solution.py:237
  14.9 2.1 %collective-permute-start.2 = (bf16[12,64,128]{2,1,0:T(8,128)(2,1)}, bf16[12,64,128]{2,1,0:T(8,128)(2,1)S(1)}, u32[]{:S(2)}, u32[]{:S(2)}) collective-permute-start(bf16[12,64,128]{2,1,0:T(8,128)(2,1)} %get-tuple-element.47), channel_id=1, source_target_pairs={{0,5},{1,4},{2,7},{3,6},{4,9},{5,8},{6,11},{7,10},{8,13},{9,12},{1... | collective-permute-start | bytes 589832 | tf_op jit(solution)/shard_map/ppermute | solution.py:271
  17.0 2.5 %collective-permute-start.6 = (bf16[12,64,128]{2,1,0:T(8,128)(2,1)}, bf16[12,64,128]{2,1,0:T(8,128)(2,1)S(1)}, u32[]{:S(2)}, u32[]{:S(2)}) collective-permute-start(bf16[12,64,128]{2,1,0:T(8,128)(2,1)} %get-tuple-element.52), channel_id=1, source_target_pairs={{0,2},{1,3},{2,4},{3,5},{4,6},{5,7},{6,8},{7,9},{8,10},{9,11},{10,... | collective-permute-start | bytes 589832 | tf_op jit(solution)/shard_map/ppermute | solution.py:271
  19.5 5.9 %collective-permute-start.8 = (bf16[12,64,128]{2,1,0:T(8,128)(2,1)}, bf16[12,64,128]{2,1,0:T(8,128)(2,1)S(1)}, u32[]{:S(2)}, u32[]{:S(2)}) collective-permute-start(bf16[12,64,128]{2,1,0:T(8,128)(2,1)} %get-tuple-element.54), channel_id=1, source_target_pairs={{0,3},{1,2},{2,5},{3,4},{4,7},{5,6},{6,9},{7,8},{8,11},{9,10},{10,... | collective-permute-start | bytes 589832 | tf_op jit(solution)/shard_map/ppermute | solution.py:271
  25.4 2.5 %collective-permute-done.12.rest_3_ = bf16[12,64,128]{2,1,0:T(8,128)(2,1)S(1)} collective-permute-done((bf16[12,64,128]{2,1,0:T(8,128)(2,1)}, bf16[12,64,128]{2,1,0:T(8,128)(2,1)S(1)}, u32[]{:S(2)}, u32[]{:S(2)}) %collective-permute-start.12) | collective-permute-done | bytes 196640 | tf_op jit(solution)/shard_map/ppermute | solution.py:271
  28.9 6.6 %collective-permute-done.2.rest_0_ = bf16[12,64,128]{2,1,0:T(8,128)(2,1)S(1)} collective-permute-done((bf16[12,64,128]{2,1,0:T(8,128)(2,1)}, bf16[12,64,128]{2,1,0:T(8,128)(2,1)S(1)}, u32[]{:S(2)}, u32[]{:S(2)}) %collective-permute-start.2) | collective-permute-done | bytes 196640 | tf_op jit(solution)/shard_map/ppermute | solution.py:271
  36.0 3.0 %collective-permute-done.6.rest_0_ = bf16[12,64,128]{2,1,0:T(8,128)(2,1)S(1)} collective-permute-done((bf16[12,64,128]{2,1,0:T(8,128)(2,1)}, bf16[12,64,128]{2,1,0:T(8,128)(2,1)S(1)}, u32[]{:S(2)}, u32[]{:S(2)}) %collective-permute-start.6) | collective-permute-done | bytes 196640 | tf_op jit(solution)/shard_map/ppermute | solution.py:271
  39.1 1.9 %collective-permute-start.13 = (bf16[12,64,128]{2,1,0:T(8,128)(2,1)}, bf16[12,64,128]{2,1,0:T(8,128)(2,1)S(1)}, u32[]{:S(2)}, u32[]{:S(2)}) collective-permute-start(bf16[12,64,128]{2,1,0:T(8,128)(2,1)} %get-tuple-element.60), channel_id=1, source_target_pairs={{0,4},{1,5},{2,6},{3,7},{4,8},{5,9},{6,10},{7,11},{8,12},{9,13},{1... | collective-permute-start | bytes 589832 | tf_op jit(solution)/shard_map/ppermute | solution.py:271
  40.9 1.7 %collective-permute-start.14 = (bf16[12,64,128]{2,1,0:T(8,128)(2,1)}, bf16[12,64,128]{2,1,0:T(8,128)(2,1)}, u32[]{:S(2)}, u32[]{:S(2)}) collective-permute-start(bf16[12,64,128]{2,1,0:T(8,128)(2,1)} %get-tuple-element.61), channel_id=1, source_target_pairs={{0,12},{1,13},{2,14},{3,15},{4,0},{5,1},{6,2},{7,3},{8,4},{9,5},{1... | collective-permute-start | bytes 589832 | tf_op jit(solution)/shard_map/ppermute | solution.py:271
  42.7 2.0 %totals.1 = bf16[16,16,128]{2,1,0:T(8,128)(2,1)S(1)} custom-call(f32[4,128,1024]{2,1,0:T(8,128)S(1)} %copy-done, f32[4,128,1024]{2,1,0:T(8,128)S(1)} %copy-done.1, f32[4,1024,128]{2,1,0:T(8,128)S(1)} %copy-done.2, f32[4,128]{1,0:T(4,128)S(1)} %bitcast.5, f32[1,128]{1,0:T(1,128)S(1)} %bitcast.6), custom_call_target="tpu_custom_call" | custom-call | tf_op jit(solution)/shard_map/totals/pallas_call | solution.py:254
  44.6 15.1 %all_to_all.10.table = bf16[16,16,128]{2,1,0:T(8,128)(2,1)S(1)} all-to-all(bf16[16,16,128]{2,1,0:T(8,128)(2,1)S(1)} %totals.1), channel_id=1, replica_groups=mesh['owner'=16,'rows'=16] {'rows'}, dimensions={0} | all-to-all | bytes 131072 | tf_op jit(solution)/shard_map/all_to_all | solution.py:272
  60.8 6.9 %all-to-all-start.1 = ((bf16[16,4,2048]{2,1,0:T(4,128)(2,1)}), bf16[16,4,2048]{2,1,0:T(4,128)(2,1)S(1)}, u32[]{:S(2)}, u32[]{:S(2)}) async-start(bf16[16,4,2048]{2,1,0:T(4,128)(2,1)} %get-tuple-element.51), calls=%async_computation.1 | async-start | bytes 524288 | tf_op jit(solution)/shard_map/all_to_all | solution.py:287
  67.7 1.9 %collective-permute-start.3 = (bf16[12,64,128]{2,1,0:T(8,128)(2,1)}, bf16[12,64,128]{2,1,0:T(8,128)(2,1)S(1)}, u32[]{:S(2)}, u32[]{:S(2)}) collective-permute-start(bf16[12,64,128]{2,1,0:T(8,128)(2,1)} %get-tuple-element.48), channel_id=1, source_target_pairs={{0,13},{1,12},{2,15},{3,14},{4,1},{5,0},{6,3},{7,2},{8,5},{9,4},{1... | collective-permute-start | bytes 589832 | tf_op jit(solution)/shard_map/ppermute | solution.py:271
  69.6 2.7 %collective-permute-start.4 = (bf16[12,64,128]{2,1,0:T(8,128)(2,1)}, bf16[12,64,128]{2,1,0:T(8,128)(2,1)S(1)}, u32[]{:S(2)}, u32[]{:S(2)}) collective-permute-start(bf16[12,64,128]{2,1,0:T(8,128)(2,1)} %get-tuple-element.49), channel_id=1, source_target_pairs={{0,6},{1,7},{2,8},{3,9},{4,10},{5,11},{6,12},{7,13},{8,14},{9,15},... | collective-permute-start | bytes 589832 | tf_op jit(solution)/shard_map/ppermute | solution.py:271
  72.9 1.8 %collective-permute-start.5 = (bf16[12,64,128]{2,1,0:T(8,128)(2,1)}, bf16[12,64,128]{2,1,0:T(8,128)(2,1)S(1)}, u32[]{:S(2)}, u32[]{:S(2)}) collective-permute-start(bf16[12,64,128]{2,1,0:T(8,128)(2,1)} %get-tuple-element.50), channel_id=1, source_target_pairs={{0,10},{1,11},{2,12},{3,13},{4,14},{5,15},{6,0},{7,1},{8,2},{9,3},... | collective-permute-start | bytes 589832 | tf_op jit(solution)/shard_map/ppermute | solution.py:271
  75.4 2.7 %collective-permute-start.1 = (bf16[12,64,128]{2,1,0:T(8,128)(2,1)}, bf16[12,64,128]{2,1,0:T(8,128)(2,1)S(1)}, u32[]{:S(2)}, u32[]{:S(2)}) collective-permute-start(bf16[12,64,128]{2,1,0:T(8,128)(2,1)} %get-tuple-element.46), channel_id=1, source_target_pairs={{0,7},{1,6},{2,9},{3,8},{4,11},{5,10},{6,13},{7,12},{8,15},{9,14},... | collective-permute-start | bytes 589832 | tf_op jit(solution)/shard_map/ppermute | solution.py:271
  78.1 2.1 %collective-permute-start = (bf16[12,64,128]{2,1,0:T(8,128)(2,1)}, bf16[12,64,128]{2,1,0:T(8,128)(2,1)S(1)}, u32[]{:S(2)}, u32[]{:S(2)}) collective-permute-start(bf16[12,64,128]{2,1,0:T(8,128)(2,1)} %get-tuple-element.45), channel_id=1, source_target_pairs={{0,11},{1,10},{2,13},{3,12},{4,15},{5,14},{6,1},{7,0},{8,3},{9,2},... | collective-permute-start | bytes 589832 | tf_op jit(solution)/shard_map/ppermute | solution.py:271
  83.0 3.0 %shard_map.110 = (bf16[4,64,2048]{2,1,0:T(8,128)(2,1)}, bf16[4,64,2048]{2,1,0:T(8,128)(2,1)}, bf16[4,64,2048]{2,1,0:T(8,128)(2,1)}) custom-call(f32[16,128,8]{2,1,0:T(8,128)S(1)} %get-tuple-element.44.factors, bf16[12,64,128]{2,1,0:T(8,128)(2,1)} %get-tuple-element.56.rest_0_, bf16[12,64,128]{2,1,0:T(8,128)(2,1)S(1)} %copy-done.6, ...), custom_call_target="tpu_custom_call" | custom-call | flops 60000000 | bytes 2400000 | tf_op jit(solution)/shard_map/pallas_call | solution.py:206
  85.9 1.5 %shard_map.111 = (bf16[4,64,2048]{2,1,0:T(8,128)(2,1)}, bf16[4,64,2048]{2,1,0:T(8,128)(2,1)}, bf16[4,64,2048]{2,1,0:T(8,128)(2,1)}) custom-call(f32[16,128,8]{2,1,0:T(8,128)S(1)} %get-tuple-element.44.factors, bf16[12,64,128]{2,1,0:T(8,128)(2,1)S(1)} %collective-permute-done.6.rest_0_, ...), custom_call_target="tpu_custom_call", output_to_operand_aliasing={{0}: (5, {}), {1}: (6, {}), {2}: (7, {})} | custom-call | flops 40000000 | bytes 1600000 | tf_op jit(solution)/shard_map/pallas_call | solution.py:206
  87.5 6.9 %collective-permute-done.5.rest_3_ = bf16[12,64,128]{2,1,0:T(8,128)(2,1)S(1)} collective-permute-done((bf16[12,64,128]{2,1,0:T(8,128)(2,1)}, bf16[12,64,128]{2,1,0:T(8,128)(2,1)S(1)}, u32[]{:S(2)}, u32[]{:S(2)}) %collective-permute-start.5) | collective-permute-done | bytes 196640 | tf_op jit(solution)/shard_map/ppermute | solution.py:271
  94.4 2.2 %shard_map.112 = (bf16[4,64,2048]{2,1,0:T(8,128)(2,1)}, bf16[4,64,2048]{2,1,0:T(8,128)(2,1)}, bf16[4,64,2048]{2,1,0:T(8,128)(2,1)}, bf16[64,2048]{1,0:T(8,128)(2,1)}) custom-call(f32[16,128,8]{2,1,0:T(8,128)S(1)} %get-tuple-element.44.factors, ...), custom_call_target="tpu_custom_call", output_to_operand_aliasing={{0}: (6, {}), {1}: (7, {}), {2}: (8, {})} | custom-call | flops 40000000 | bytes 1600000 | tf_op jit(solution)/shard_map/pallas_call | solution.py:206
  97.6 9.4 %collective-permute-done.rest_0_ = bf16[12,64,128]{2,1,0:T(8,128)(2,1)S(1)} collective-permute-done((bf16[12,64,128]{2,1,0:T(8,128)(2,1)}, bf16[12,64,128]{2,1,0:T(8,128)(2,1)S(1)}, u32[]{:S(2)}, u32[]{:S(2)}) %collective-permute-start) | collective-permute-done | bytes 196640 | tf_op jit(solution)/shard_map/ppermute | solution.py:271
  (40 shorter events, 9.2 us)
Async XLA Ops:
  2.9 16.6 %collective-permute-start.11 = (bf16[12,64,128]{2,1,0:T(8,128)(2,1)}, bf16[12,64,128]{2,1,0:T(8,128)(2,1)S(1)}, u32[]{:S(2)}, u32[]{:S(2)}) collective-permute-start(bf16[12,64,128]{2,1,0:T(8,128)(2,1)} %get-tuple-element.58), channel_id=1, source_target_pairs={{0,8},{1,9},{2,10},{3,11},{4,12},{5,13},{6,14},{7,15},{8,0},{9,1},... | collective-permute-start | bytes 589832 | tf_op jit(solution)/shard_map/ppermute | solution.py:271
  9.0 33.6 %copy-start = (f32[4,128,1024]{2,1,0:T(8,128)S(1)}, f32[4,128,1024]{2,1,0:T(8,128)}, u32[]{:S(2)}) copy-start(f32[4,128,1024]{2,1,0:T(8,128)} %gate.5) | copy-start | bytes 6291460
  9.0 33.6 %copy-start.1 = (f32[4,128,1024]{2,1,0:T(8,128)S(1)}, f32[4,128,1024]{2,1,0:T(8,128)}, u32[]{:S(2)}) copy-start(f32[4,128,1024]{2,1,0:T(8,128)} %up.5) | copy-start | bytes 6291460
  9.0 33.6 %copy-start.2 = (f32[4,1024,128]{2,1,0:T(8,128)S(1)}, f32[4,1024,128]{2,1,0:T(8,128)}, u32[]{:S(2)}) copy-start(f32[4,1024,128]{2,1,0:T(8,128)} %down.5) | copy-start | bytes 6291460
  9.0 33.6 %copy-start.9 = (f32[128,4]{0,1:T(4,128)S(1)}, f32[128,4]{0,1:T(4,128)}, u32[]{:S(2)}) copy-start(f32[128,4]{0,1:T(4,128)} %param.8) | copy-start | bytes 6148
  9.0 33.6 %copy-start.10 = (f32[128]{0:T(128)S(1)}, f32[128]{0:T(128)}, u32[]{:S(2)}) copy-start(f32[128]{0:T(128)} %param.9) | copy-start | bytes 1540
  9.0 18.8 %collective-permute-start.12 = (bf16[12,64,128]{2,1,0:T(8,128)(2,1)}, bf16[12,64,128]{2,1,0:T(8,128)(2,1)S(1)}, u32[]{:S(2)}, u32[]{:S(2)}) collective-permute-start(bf16[12,64,128]{2,1,0:T(8,128)(2,1)} %get-tuple-element.59), channel_id=1, source_target_pairs={{0,9},{1,8},{2,11},{3,10},{4,13},{5,12},{6,15},{7,14},{8,1},{9,0},... | collective-permute-start | bytes 589832 | tf_op jit(solution)/shard_map/ppermute | solution.py:271
  14.9 20.7 %collective-permute-start.2 = (bf16[12,64,128]{2,1,0:T(8,128)(2,1)}, bf16[12,64,128]{2,1,0:T(8,128)(2,1)S(1)}, u32[]{:S(2)}, u32[]{:S(2)}) collective-permute-start(bf16[12,64,128]{2,1,0:T(8,128)(2,1)} %get-tuple-element.47), channel_id=1, source_target_pairs={{0,5},{1,4},{2,7},{3,6},{4,9},{5,8},{6,11},{7,10},{8,13},{9,12},{1... | collective-permute-start | bytes 589832 | tf_op jit(solution)/shard_map/ppermute | solution.py:271
  17.0 22.1 %collective-permute-start.6 = (bf16[12,64,128]{2,1,0:T(8,128)(2,1)}, bf16[12,64,128]{2,1,0:T(8,128)(2,1)S(1)}, u32[]{:S(2)}, u32[]{:S(2)}) collective-permute-start(bf16[12,64,128]{2,1,0:T(8,128)(2,1)} %get-tuple-element.52), channel_id=1, source_target_pairs={{0,2},{1,3},{2,4},{3,5},{4,6},{5,7},{6,8},{7,9},{8,10},{9,11},{10,... | collective-permute-start | bytes 589832 | tf_op jit(solution)/shard_map/ppermute | solution.py:271
  19.5 21.5 %collective-permute-start.7 = (bf16[12,64,128]{2,1,0:T(8,128)(2,1)}, bf16[12,64,128]{2,1,0:T(8,128)(2,1)S(1)}, u32[]{:S(2)}, u32[]{:S(2)}) collective-permute-start(bf16[12,64,128]{2,1,0:T(8,128)(2,1)} %get-tuple-element.53), channel_id=1, source_target_pairs={{0,14},{1,15},{2,0},{3,1},{4,2},{5,3},{6,4},{7,5},{8,6},{9,7},{10,... | collective-permute-start | bytes 589832 | tf_op jit(solution)/shard_map/ppermute | solution.py:271
  19.5 48.3 %collective-permute-start.8 = (bf16[12,64,128]{2,1,0:T(8,128)(2,1)}, bf16[12,64,128]{2,1,0:T(8,128)(2,1)S(1)}, u32[]{:S(2)}, u32[]{:S(2)}) collective-permute-start(bf16[12,64,128]{2,1,0:T(8,128)(2,1)} %get-tuple-element.54), channel_id=1, source_target_pairs={{0,3},{1,2},{2,5},{3,4},{4,7},{5,6},{6,9},{7,8},{8,11},{9,10},{10,... | collective-permute-start | bytes 589832 | tf_op jit(solution)/shard_map/ppermute | solution.py:271
  28.6 41.0 %collective-permute-start.9 = (bf16[12,64,128]{2,1,0:T(8,128)(2,1)}, bf16[12,64,128]{2,1,0:T(8,128)(2,1)S(1)}, u32[]{:S(2)}, u32[]{:S(2)}) collective-permute-start(bf16[12,64,128]{2,1,0:T(8,128)(2,1)} %get-tuple-element.55), channel_id=1, source_target_pairs={{0,15},{1,14},{2,1},{3,0},{4,3},{5,2},{6,5},{7,4},{8,7},{9,6},{10,... | collective-permute-start | bytes 589832 | tf_op jit(solution)/shard_map/ppermute | solution.py:271
  35.6 36.7 %collective-permute-start.10 = (bf16[12,64,128]{2,1,0:T(8,128)(2,1)}, bf16[12,64,128]{2,1,0:T(8,128)(2,1)S(1)}, u32[]{:S(2)}, u32[]{:S(2)}) collective-permute-start(bf16[12,64,128]{2,1,0:T(8,128)(2,1)} %get-tuple-element.57), channel_id=1, source_target_pairs={{0,1},{1,0},{2,3},{3,2},{4,5},{5,4},{6,7},{7,6},{8,9},{9,8},{10,11... | collective-permute-start | bytes 589832 | tf_op jit(solution)/shard_map/ppermute | solution.py:271
  39.1 35.7 %collective-permute-start.13 = (bf16[12,64,128]{2,1,0:T(8,128)(2,1)}, bf16[12,64,128]{2,1,0:T(8,128)(2,1)S(1)}, u32[]{:S(2)}, u32[]{:S(2)}) collective-permute-start(bf16[12,64,128]{2,1,0:T(8,128)(2,1)} %get-tuple-element.60), channel_id=1, source_target_pairs={{0,4},{1,5},{2,6},{3,7},{4,8},{5,9},{6,10},{7,11},{8,12},{9,13},{1... | collective-permute-start | bytes 589832 | tf_op jit(solution)/shard_map/ppermute | solution.py:271
  40.9 37.2 %collective-permute-start.14 = (bf16[12,64,128]{2,1,0:T(8,128)(2,1)}, bf16[12,64,128]{2,1,0:T(8,128)(2,1)}, u32[]{:S(2)}, u32[]{:S(2)}) collective-permute-start(bf16[12,64,128]{2,1,0:T(8,128)(2,1)} %get-tuple-element.61), channel_id=1, source_target_pairs={{0,12},{1,13},{2,14},{3,15},{4,0},{5,1},{6,2},{7,3},{8,4},{9,5},{1... | collective-permute-start | bytes 589832 | tf_op jit(solution)/shard_map/ppermute | solution.py:271
  60.8 33.6 %all-to-all-start.1 = ((bf16[16,4,2048]{2,1,0:T(4,128)(2,1)}), bf16[16,4,2048]{2,1,0:T(4,128)(2,1)S(1)}, u32[]{:S(2)}, u32[]{:S(2)}) async-start(bf16[16,4,2048]{2,1,0:T(4,128)(2,1)} %get-tuple-element.51), calls=%async_computation.1 | async-start | bytes 524288 | tf_op jit(solution)/shard_map/all_to_all | solution.py:287
  67.7 19.7 %collective-permute-start.3 = (bf16[12,64,128]{2,1,0:T(8,128)(2,1)}, bf16[12,64,128]{2,1,0:T(8,128)(2,1)S(1)}, u32[]{:S(2)}, u32[]{:S(2)}) collective-permute-start(bf16[12,64,128]{2,1,0:T(8,128)(2,1)} %get-tuple-element.48), channel_id=1, source_target_pairs={{0,13},{1,12},{2,15},{3,14},{4,1},{5,0},{6,3},{7,2},{8,5},{9,4},{1... | collective-permute-start | bytes 589832 | tf_op jit(solution)/shard_map/ppermute | solution.py:271
  69.6 17.9 %collective-permute-start.4 = (bf16[12,64,128]{2,1,0:T(8,128)(2,1)}, bf16[12,64,128]{2,1,0:T(8,128)(2,1)S(1)}, u32[]{:S(2)}, u32[]{:S(2)}) collective-permute-start(bf16[12,64,128]{2,1,0:T(8,128)(2,1)} %get-tuple-element.49), channel_id=1, source_target_pairs={{0,6},{1,7},{2,8},{3,9},{4,10},{5,11},{6,12},{7,13},{8,14},{9,15},... | collective-permute-start | bytes 589832 | tf_op jit(solution)/shard_map/ppermute | solution.py:271
  72.9 21.5 %collective-permute-start.5 = (bf16[12,64,128]{2,1,0:T(8,128)(2,1)}, bf16[12,64,128]{2,1,0:T(8,128)(2,1)S(1)}, u32[]{:S(2)}, u32[]{:S(2)}) collective-permute-start(bf16[12,64,128]{2,1,0:T(8,128)(2,1)} %get-tuple-element.50), channel_id=1, source_target_pairs={{0,10},{1,11},{2,12},{3,13},{4,14},{5,15},{6,0},{7,1},{8,2},{9,3},... | collective-permute-start | bytes 589832 | tf_op jit(solution)/shard_map/ppermute | solution.py:271
  75.4 21.2 %collective-permute-start.1 = (bf16[12,64,128]{2,1,0:T(8,128)(2,1)}, bf16[12,64,128]{2,1,0:T(8,128)(2,1)S(1)}, u32[]{:S(2)}, u32[]{:S(2)}) collective-permute-start(bf16[12,64,128]{2,1,0:T(8,128)(2,1)} %get-tuple-element.46), channel_id=1, source_target_pairs={{0,7},{1,6},{2,9},{3,8},{4,11},{5,10},{6,13},{7,12},{8,15},{9,14},... | collective-permute-start | bytes 589832 | tf_op jit(solution)/shard_map/ppermute | solution.py:271
  78.1 28.9 %collective-permute-start = (bf16[12,64,128]{2,1,0:T(8,128)(2,1)}, bf16[12,64,128]{2,1,0:T(8,128)(2,1)S(1)}, u32[]{:S(2)}, u32[]{:S(2)}) collective-permute-start(bf16[12,64,128]{2,1,0:T(8,128)(2,1)} %get-tuple-element.45), channel_id=1, source_target_pairs={{0,11},{1,10},{2,13},{3,12},{4,15},{5,14},{6,1},{7,0},{8,3},{9,2},... | collective-permute-start | bytes 589832 | tf_op jit(solution)/shard_map/ppermute | solution.py:271
  80.2 0.9 copy-start.4
  81.1 0.9 copy-start.6
  82.0 0.9 copy-start.8
  (3 other events, 2.0 us)
